TPU v7x, 32 devices: a whole 2x2x4 slice. The times are simulated.
32 devices in a mesh: dp: 2 (over x), tp: 4 (over z), sp: 4 (over y, core).
Axes of the slice: x: 2, y: 2, z: 4, core: 2. Of those that a mesh axis runs over, the one named last changes fastest.
Arguments:
- k_cache: bfloat16 [4, 8, 8, 8192, 64], P(None, 'dp', 'tp', 'sp'), parts along dimension 1
- v_cache: bfloat16 [4, 8, 8, 8192, 64], P(None, 'dp', 'tp', 'sp'), parts along dimension 1
- lengths: int32 [8], P('dp'), parts along dimension 0
- hidden: bfloat16 [8, 2048], P(('dp', 'sp')), parts along dimension 0
- ln_gain: bfloat16 [4, 2048], replicated
- w_query: bfloat16 [4, 2048, 2048], P(None, None, 'tp')
- w_key: bfloat16 [4, 2048, 512], P(None, None, 'tp')
- w_value: bfloat16 [4, 2048, 512], P(None, None, 'tp')
- w_out: bfloat16 [4, 2048, 2048], P(None, 'tp')
- w_gate: bfloat16 [4, 2048, 8192], P(None, None, 'tp')
- w_up: bfloat16 [4, 2048, 8192], P(None, None, 'tp')
- w_down: bfloat16 [4, 8192, 2048], P(None, 'tp')
Outputs:
- output 1: bfloat16 [8, 2048], P(('dp', 'sp')), parts along dimension 0
- output 2: bfloat16 [3, 8, 8, 4096, 64], P(None, ('dp', 'sp'), 'tp'), parts along dimension 1
- output 3: bfloat16 [3, 8, 8, 4096, 64], P(None, ('dp', 'sp'), 'tp'), parts along dimension 1
- output 4: bfloat16 [8, 8, 8192, 64], P(('dp', 'sp'), 'tp'), parts along dimension 0
- output 5: bfloat16 [8, 8, 8192, 64], P(('dp', 'sp'), 'tp'), parts along dimension 0
There are 2 independent parts. A program takes and returns all parts, laid end to end along the dimension named above; an argument that names none is the same for every part.
All inputs are finite; a program needn't handle non-finite values.
Results may differ from a plain program's by a relative error of at most 0.02.
Values are sent between devices in bfloat16 or wider.
A program may use at most 1 GiB of HBM per device.

v0:
```python
import functools

import jax
import jax.numpy as jnp
from jax import lax
from jax.experimental import pallas as pl
from jax.experimental.pallas import tpu as pltpu
from jax.sharding import PartitionSpec as P


WINDOW = 4096
ROPE_BASE = 50000
NORM_EPS = 1e-5
UNIT = 128
SIZES = (18, 23, 28, 32)
FFN_STEPS = 4
CHUNK = 16
HBM = pl.BlockSpec(memory_space=pltpu.HBM)
VMEM = pl.BlockSpec(memory_space=pltpu.VMEM)
SMEM = pl.BlockSpec(memory_space=pltpu.SMEM)
F32 = jnp.float32
BF16 = jnp.bfloat16


def cost(n_bytes):
    return pl.CostEstimate(flops=n_bytes, bytes_accessed=n_bytes, transcendentals=0)


def lanes(block, count=1):
    return pl.ds(pl.multiple_of(block * UNIT, UNIT), count * UNIT)


def crossing(beta, on_second_chip, n_units):
    above = (beta + 1) // UNIT
    below = (beta + UNIT - 1) // UNIT
    return jnp.where(on_second_chip, above, 0), jnp.where(on_second_chip, n_units - above, below)


def move(pairs):
    for src, dst, sem in pairs:
        pltpu.make_async_copy(src, dst, sem).start()


def pack_body(layer, size, half, ids, k_own, v_own, k_near, v_near, *refs):
    outs, (buf, sem, out_sem) = refs[:-3], refs[-3:]
    me = ids[0]
    core = lax.rem(me, 2)
    base = (1 - me // 2) * 2
    second = base == 2
    row, other = base + core, base + 1 - core
    first, count = crossing(ids[1 + row] - WINDOW, second, 2 * half)
    other_first, other_count = crossing(ids[1 + other] - WINDOW, second, 2 * half)
    over = jnp.maximum(other_count - size, 0)

    def issue(i, carry):
        mine = i < count
        dest = jnp.where(mine, row, other)
        unit = jnp.where(mine, first + i, other_first + size + i - (size - over))
        unit = jnp.clip(unit, 0, 2 * half - 1)
        at = lanes(lax.rem(unit, half))
        local = unit // half == core

        @pl.when(local)
        def _():
            move([(k_own.at[layer, dest, :, :, at], buf.at[0, :, :, lanes(i)], sem), (v_own.at[layer, dest, :, :, at], buf.at[1, :, :, lanes(i)], sem)])

        @pl.when(jnp.logical_not(local))
        def _():
            move([(near.at[layer, dest, :, :, at], buf.at[p, :, :, lanes(i)], sem) for p, near in enumerate((k_near, v_near))])

        return carry

    lax.fori_loop(0, size, issue, 0)
    pltpu.make_async_copy(buf, buf, sem).wait()
    cut = size - half
    copies = [pltpu.make_async_copy(buf.at[:, :, :, cut * UNIT:], outs[0], out_sem)]
    if cut:
        copies.append(pltpu.make_async_copy(buf.at[:, :, :, :cut * UNIT], outs[1], out_sem))
    for copy in copies:
        copy.start()
    for copy in copies:
        copy.wait()


def pack(layer, size, ids, k_t, v_t, nears):
    heads, dim, shard = k_t.shape[2:]
    half = shard // UNIT
    widths = [half] + ([size - half] if size > half else [])
    return pl.pallas_call(
        functools.partial(pack_body, layer, size, half),
        in_specs=[SMEM] + [HBM] * 4,
        out_specs=[HBM] * len(widths),
        out_shape=[jax.ShapeDtypeStruct((2, heads, dim, w * UNIT), BF16) for w in widths],
        scratch_shapes=[pltpu.VMEM((2, heads, dim, size * UNIT), BF16), pltpu.SemaphoreType.DMA, pltpu.SemaphoreType.DMA],
        cost_estimate=cost(8 * heads * dim * size * UNIT),
        name="pack",
    )(ids, k_t, v_t, *nears)


def after(value, *others):
    return lax.optimization_barrier((value, others))[0]


def settle(kv, new_rows, beta, rest_of, units):
    fresh = new_rows[:, :, None]
    lane = lax.broadcasted_iota(jnp.int32, (1, 1, UNIT), 2)

    def fix(w, carry):
        pos = lane + w * UNIT
        old = kv[:, :, lanes(w)].astype(F32)
        put = jnp.where(pos < beta, old, jnp.where(pos == beta, fresh, rest_of(old)))
        kv[:, :, lanes(w)] = put.astype(BF16)
        return carry

    lax.fori_loop(*units, fix, 0)


def stacked(q_ref):
    return jnp.concatenate([q_ref[j] for j in range(q_ref.shape[0])], axis=0).astype(BF16)


def softmax_weights(q, keys, scores, beta):
    upper = lax.broadcasted_iota(jnp.int32, (q.shape[0], 1), 0) < q.shape[0] // 2

    def chunk(i, carry):
        at = lanes(i * CHUNK, CHUNK)
        s0 = jnp.dot(q, keys[0, :, at], preferred_element_type=F32)
        s1 = jnp.dot(q, keys[1, :, at], preferred_element_type=F32)
        part = jnp.where(upper, s0, s1) * (q.shape[1] ** -0.5)
        if beta is not None:
            part = jnp.where(lax.broadcasted_iota(jnp.int32, (1, part.shape[1]), 1) + i * CHUNK * UNIT <= beta, part, -1e30)
        scores[:, at] = part
        return carry

    lax.fori_loop(0, keys.shape[-1] // (CHUNK * UNIT), chunk, 0)
    top = scores[...].max(axis=-1, keepdims=True)
    expd = jnp.exp(scores[...] - top)
    return (expd / expd.sum(axis=-1, keepdims=True)).astype(BF16)


def mix_and_project(weights, values, copy, wo, mlp, out):
    rows = weights.shape[0]
    dim = values.shape[1]
    upper = lax.broadcasted_iota(jnp.int32, (rows, 1), 0) < rows // 2
    dims = (((1,), (1,)), ((), ()))

    def chunk(i, carry):
        at = lanes(i * CHUNK, CHUNK)
        return tuple(carry[h] + lax.dot_general(weights[:, at], values[h, :, at], dims, preferred_element_type=F32) for h in range(2))

    m0, m1 = lax.fori_loop(0, values.shape[-1] // (CHUNK * UNIT), chunk, (jnp.zeros((rows, dim), F32),) * 2)
    copy.start()
    mixed = jnp.where(upper, m0, m1).astype(BF16).astype(F32)
    flat = jnp.concatenate([mixed[j:j + 1] for j in range(rows)], axis=1)
    flat = jnp.broadcast_to(flat, (8, flat.shape[1])).astype(BF16)

    def project(i, carry):
        at = lanes(i * 4, 4)
        out[:, at] = jnp.dot(flat, wo[:, at], preferred_element_type=F32)[0:1] + mlp[:, at]
        return carry

    lax.fori_loop(0, out.shape[1] // (4 * UNIT), project, 0)


def window_body(layer, size, half, n_pipe, ids, q_ref, new_ref, mlp_ref, wo_hbm, k_own, v_own, k_near, v_near, *refs):
    pipe = refs[:n_pipe]
    k_out, v_out = refs[n_pipe + 3:n_pipe + 5]
    part_ref = refs[n_pipe + 2]
    kv, edge, wo, scores, weights, sems, out_sems, wo_sem = refs[n_pipe + 5:]
    me = ids[0]
    core = lax.rem(me, 2)
    second = me // 2 == 1
    beta = ids[1 + me] - WINDOW
    last = beta // UNIT
    first, count = crossing(beta, second, 2 * half)
    direct = size is None
    over = 0 if direct else jnp.maximum(count - size, 0)
    cut = 0 if direct else size - half

    def fetch(w, low, part, dst, sem):
        high = jnp.logical_and(w <= last, jnp.logical_not(low))
        crosses = jnp.logical_xor(high, second)
        at = lanes(lax.rem(w, half))
        local = w // half == core
        idx = jnp.clip(w - first, 0, 2 * half - 1)
        stay = jnp.logical_not(crosses)

        @pl.when(jnp.logical_and(stay, local))
        def _():
            move([((k_own, v_own)[part].at[layer, me, :, :, at], dst, sem)])

        @pl.when(jnp.logical_and(stay, jnp.logical_not(local)))
        def _():
            move([((k_near, v_near)[part].at[layer, me, :, :, at], dst, sem)])

        if direct:
            for here, ref in ((local, pipe[2 * part]), (jnp.logical_not(local), pipe[2 * part + 1])):
                @pl.when(jnp.logical_and(crosses, here))
                def _(ref=ref):
                    move([(ref.at[:, :, at], dst, sem)])
            return

        @pl.when(jnp.logical_and(crosses, jnp.logical_and(idx >= cut, idx < size)))
        def _():
            move([(pipe[0].at[part, :, :, lanes(idx - cut)], dst, sem)])

        if cut:
            @pl.when(jnp.logical_and(crosses, idx < cut))
            def _():
                move([(pipe[1].at[part, :, :, lanes(idx)], dst, sem)])

        if size < 2 * half:
            @pl.when(jnp.logical_and(crosses, idx >= size))
            def _():
                move([(pipe[-1].at[part, :, :, lanes(jnp.clip(half - over + idx - size, 0, half - 1))], dst, sem)])

    wo_copy = pltpu.make_async_copy(wo_hbm.at[layer], wo, wo_sem)
    for part in range(2):
        def issue(w, carry, part=part):
            fetch(w, False, part, kv.at[part, :, :, lanes(w)], sems.at[part])
            return carry

        lax.fori_loop(0, 2 * half, issue, 0)
        fetch(last, True, part, edge.at[part], sems.at[part])
    wo_copy.start()

    def ready(part):
        pltpu.make_async_copy(kv.at[part], kv.at[part], sems.at[part]).wait()
        pltpu.make_async_copy(edge.at[part], edge.at[part], sems.at[part]).wait()
        settle(kv.at[part], new_ref[part], beta, lambda old: edge[part].astype(F32), (last, last + 1))

    ready(0)
    weights[...] = softmax_weights(stacked(q_ref), kv.at[0], scores, None)
    k_copy = pltpu.make_async_copy(kv.at[0], k_out.at[layer], out_sems.at[0])
    k_copy.start()
    ready(1)
    wo_copy.wait()
    v_copy = pltpu.make_async_copy(kv.at[1], v_out.at[layer], out_sems.at[1])
    mix_and_project(weights, kv.at[1], v_copy, wo, mlp_ref, part_ref)
    k_copy.wait()
    v_copy.wait()


def attend_window(layer, size, ids, q, new_kv, mlp, w_out, k_t, v_t, nears, pipe, k_buf, v_buf):
    heads, dim, shard = k_t.shape[2:]
    half = shard // UNIT
    n_pipe = len(pipe)
    return pl.pallas_call(
        functools.partial(window_body, layer, size, half, n_pipe),
        in_specs=[SMEM, VMEM, VMEM, VMEM] + [HBM] * (5 + n_pipe + 2),
        out_specs=[VMEM, HBM, HBM],
        out_shape=[jax.ShapeDtypeStruct(mlp.shape, F32), jax.ShapeDtypeStruct(k_buf.shape, BF16), jax.ShapeDtypeStruct(v_buf.shape, BF16)],
        scratch_shapes=[
            pltpu.VMEM((2, heads, dim, 2 * shard), BF16),
            pltpu.VMEM((2, heads, dim, UNIT), BF16),
            pltpu.VMEM(w_out.shape[1:], BF16),
            pltpu.VMEM((q.shape[0] * q.shape[1], 2 * shard), F32),
            pltpu.VMEM((q.shape[0] * q.shape[1], 2 * shard), BF16),
            pltpu.SemaphoreType.DMA((2,)),
            pltpu.SemaphoreType.DMA((2,)),
            pltpu.SemaphoreType.DMA,
        ],
        input_output_aliases={9 + n_pipe: 1, 10 + n_pipe: 2},
        cost_estimate=cost(16 * heads * dim * shard),
        name="attend_window",
    )(ids, q, new_kv, mlp, w_out, k_t, v_t, *nears, *pipe, k_buf, v_buf)


def fetch_row(layer, me, own, blocks, kv, sem):
    shard = own.shape[-1]
    for relation in range(4):
        at = pl.ds(pl.multiple_of(jnp.bitwise_xor(me, relation) * shard, UNIT), shard)
        src = (own, blocks[0])[relation].at[layer, me] if relation < 2 else blocks[relation - 1]
        move([(src, kv.at[:, :, at], sem)])


def scores_body(layer, ids, q_ref, new_ref, own, b1, b2, b3, w_ref, k_out, kv, sem, out_sem, scores):
    me = ids[0]
    length = ids[1 + me]
    fetch_row(layer, me, own, (b1, b2, b3), kv, sem)
    pltpu.make_async_copy(kv, kv, sem).wait()
    settle(kv, new_ref[0], length, jnp.zeros_like, (length // UNIT, kv.shape[-1] // UNIT))
    w_ref[...] = softmax_weights(stacked(q_ref), kv, scores, length)
    copy = pltpu.make_async_copy(kv, k_out, out_sem)
    copy.start()
    copy.wait()


def values_body(layer, ids, w_ref, new_ref, mlp_ref, wo_hbm, own, b1, b2, b3, part_ref, v_out, kv, wo, sem, out_sem, wo_sem):
    me = ids[0]
    length = ids[1 + me]
    fetch_row(layer, me, own, (b1, b2, b3), kv, sem)
    wo_copy = pltpu.make_async_copy(wo_hbm.at[layer], wo, wo_sem)
    wo_copy.start()
    pltpu.make_async_copy(kv, kv, sem).wait()
    settle(kv, new_ref[1], length, jnp.zeros_like, (length // UNIT, kv.shape[-1] // UNIT))
    wo_copy.wait()
    copy = pltpu.make_async_copy(kv, v_out, out_sem)
    mix_and_project(w_ref, kv, copy, wo, mlp_ref, part_ref)
    copy.wait()


def attend_global(layer, ids, q, new_kv, mlp, w_out, k_t, v_t, k_blocks, v_blocks):
    heads, dim, shard = k_t.shape[2:]
    row = jax.ShapeDtypeStruct((heads, dim, 4 * shard), BF16)
    scratch = [pltpu.VMEM(row.shape, BF16), pltpu.SemaphoreType.DMA, pltpu.SemaphoreType.DMA]
    n_q = q.shape[0] * q.shape[1]
    weights, k_glob = pl.pallas_call(
        functools.partial(scores_body, layer),
        in_specs=[SMEM, VMEM, VMEM] + [HBM] * 4,
        out_specs=[VMEM, HBM],
        out_shape=[jax.ShapeDtypeStruct((n_q, 4 * shard), BF16), row],
        scratch_shapes=scratch + [pltpu.VMEM((n_q, 4 * shard), F32)],
        cost_estimate=cost(16 * heads * dim * shard),
        name="scores",
    )(ids, q, new_kv, k_t, *k_blocks)
    part, v_glob = pl.pallas_call(
        functools.partial(values_body, layer),
        in_specs=[SMEM, VMEM, VMEM, VMEM] + [HBM] * 5,
        out_specs=[VMEM, HBM],
        out_shape=[jax.ShapeDtypeStruct(mlp.shape, F32), row],
        scratch_shapes=scratch[:1] + [pltpu.VMEM(w_out.shape[1:], BF16)] + [pltpu.SemaphoreType.DMA] * 3,
        cost_estimate=cost(16 * heads * dim * shard),
        name="values",
    )(ids, weights, new_kv, mlp, w_out, v_t, *v_blocks)
    return part, k_glob, v_glob


def summed(tp, residual, parts):
    total = residual.astype(F32)
    for t in range(4):
        at = jnp.bitwise_xor(tp, t)
        pick = parts[3][...]
        for r in range(3):
            pick = jnp.where(at == r, parts[r][...], pick)
        total = pick if t == 0 else total + pick
    return (residual.astype(F32) + total).astype(BF16)


def front_body(layer, dim, n_parts, tp_ref, h_ref, *refs):
    parts, (gain, cosine, sine, wq, wk, wv, wg, wu, wd, h_out, q_out, new_out, mlp_out, u, acc) = refs[:n_parts], refs[n_parts:]
    step = pl.program_id(0)

    def turn(proj):
        if cosine is None:
            return proj
        width = proj.shape[1]
        lane = lax.broadcasted_iota(jnp.int32, proj.shape, 1)
        ahead = pltpu.roll(proj, width - dim // 2, 1)
        behind = pltpu.roll(proj, dim // 2, 1)
        swapped = jnp.where(lax.rem(lane, dim) < dim // 2, -ahead, behind)
        return proj * cosine[...] + swapped * sine[...]

    def over_rows(mats):
        depth = 8 * UNIT

        def block(i, sums):
            rows = lanes(i * 8, 8)
            return tuple(t + jnp.dot(u[:, rows], m[0, rows, :], preferred_element_type=F32) for t, m in zip(sums, mats))

        return lax.fori_loop(0, u.shape[1] // depth, block, tuple(jnp.zeros((u.shape[0], m.shape[2]), F32) for m in mats))

    def rounded(proj):
        return proj.astype(BF16).astype(F32)

    @pl.when(step == 0)
    def _():
        h = summed(tp_ref[0], h_ref[...], parts) if n_parts else h_ref[...]
        h_out[...] = h
        rows32 = h.astype(F32)
        centered = rows32 - rows32.mean(axis=-1, keepdims=True)
        variance = (centered * centered).mean(axis=-1, keepdims=True)
        scaled = centered * lax.rsqrt(variance + NORM_EPS) * gain[...].astype(F32)[layer:layer + 1]
        u[...] = jnp.broadcast_to(scaled, u.shape).astype(BF16)
        acc[...] = jnp.zeros_like(acc)
        both = over_rows((wk, wv))
        key_new, value_new = rounded(turn(both[0])), rounded(both[1])
        for part, new in ((0, key_new), (1, value_new)):
            for head in range(new_out.shape[1]):
                new_out[part, head:head + 1, :] = new[0:1, head * dim:(head + 1) * dim]

    query, gate, up = over_rows((wq, wg, wu))
    query = rounded(turn(query))
    for head in range(q_out.shape[1]):
        q_out[0, head:head + 1, :] = query[0:1, head * dim:(head + 1) * dim]
    active = (jax.nn.silu(gate) * up).astype(BF16)

    def down(i, carry):
        at = lanes(i * 8, 8)
        acc[:, at] += jnp.dot(active, wd[0, :, at], preferred_element_type=F32)
        return carry

    lax.fori_loop(0, acc.shape[1] // (8 * UNIT), down, 0)

    @pl.when(step == FFN_STEPS - 1)
    def _():
        mlp_out[...] = acc[0:1, :]


def plain_front_body(layer, dim, n_parts, tp_ref, h_ref, *refs):
    front_body(layer, dim, n_parts, tp_ref, h_ref, *refs[:n_parts + 1], None, None, *refs[n_parts + 1:])


def front(layer, dim, tp, residual, parts, ln_gain, turns, w_query, w_key, w_value, w_gate, w_up, w_down):
    width = residual.shape[1]
    q_width, kv_width, ffn = w_query.shape[2], w_key.shape[2], w_gate.shape[2]
    q_step, ffn_step = q_width // FFN_STEPS, ffn // FFN_STEPS
    whole = lambda *shape: pl.BlockSpec(shape, lambda j: (0,) * len(shape))
    col = lambda rows, cols: pl.BlockSpec((1, rows, cols), lambda j: (layer, 0, j))
    fixed = lambda rows, cols: pl.BlockSpec((1, rows, cols), lambda j: (layer, 0, 0))
    n_parts = len(parts)
    body = front_body if turns else plain_front_body
    return pl.pallas_call(
        functools.partial(body, layer, dim, n_parts),
        grid=(FFN_STEPS,),
        in_specs=[SMEM, whole(1, width)] + [whole(1, width)] * n_parts + [whole(*ln_gain.shape)] + [whole(1, kv_width)] * len(turns)
        + [col(width, q_step), fixed(width, kv_width), fixed(width, kv_width), col(width, ffn_step), col(width, ffn_step), pl.BlockSpec((1, ffn_step, width), lambda j: (layer, j, 0))],
        out_specs=[whole(1, width), pl.BlockSpec((1, q_step // dim, dim), lambda j: (j, 0, 0)), whole(2, kv_width // dim, dim), whole(1, width)],
        out_shape=[
            jax.ShapeDtypeStruct((1, width), BF16),
            jax.ShapeDtypeStruct((FFN_STEPS, q_step // dim, dim), F32),
            jax.ShapeDtypeStruct((2, kv_width // dim, dim), F32),
            jax.ShapeDtypeStruct((1, width), F32),
        ],
        scratch_shapes=[pltpu.VMEM((8, width), BF16), pltpu.VMEM((8, width), F32)],
        compiler_params=pltpu.CompilerParams(dimension_semantics=("arbitrary",)),
        cost_estimate=cost(2 * width * (q_width + 2 * kv_width + 3 * ffn)),
        name="front",
    )(tp, residual, *parts, ln_gain, *turns, w_query, w_key, w_value, w_gate, w_up, w_down)


def close_body(tp_ref, h_ref, p0, p1, p2, p3, out_ref):
    out_ref[...] = summed(tp_ref[0], h_ref[...], (p0, p1, p2, p3))


def close(tp, residual, parts):
    return pl.pallas_call(
        close_body,
        in_specs=[SMEM] + [VMEM] * 5,
        out_specs=VMEM,
        out_shape=jax.ShapeDtypeStruct(residual.shape, BF16),
        name="close",
    )(tp, residual, *parts)


def fresh_body(*refs):
    pass


def fresh_buffers(shapes):
    return pl.pallas_call(fresh_body, out_specs=[HBM] * len(shapes), out_shape=[jax.ShapeDtypeStruct(s, BF16) for s in shapes], name="fresh")()


def solution(mesh):
    cache_spec = P(None, "dp", "tp", "sp", None)
    row_spec = P(("dp", "sp"), None)
    col_spec = P(None, None, "tp")
    inner_spec = P(None, "tp", None)
    window_spec = P(None, ("dp", "sp"), "tp", None, None)
    global_spec = P(("dp", "sp"), "tp", None, None)
    in_specs = (cache_spec, cache_spec, P("dp"), row_spec, P(None, None), col_spec, col_spec, col_spec, inner_spec, col_spec, col_spec, inner_spec)
    out_specs = (row_spec, window_spec, window_spec, global_spec, global_spec)
    n_sp, n_tp = mesh.shape["sp"], mesh.shape["tp"]

    def swap(t, axis, relation):
        return lax.ppermute(t, axis, [(i, i ^ relation) for i in range(n_sp if axis == "sp" else n_tp)])

    def device_step(k_cache, v_cache, lengths, hidden, ln_gain, w_query, w_key, w_value, w_out, w_gate, w_up, w_down):
        n_layers = w_query.shape[0]
        heads, shard, dim = k_cache.shape[2:]
        half = shard // UNIT
        final = n_layers - 1
        me = lax.axis_index("sp").astype(jnp.int32)
        tp = lax.axis_index("tp").astype(jnp.int32)[None]
        ids = jnp.concatenate([me[None], lengths])
        k_t = jnp.swapaxes(k_cache, 3, 4)
        v_t = jnp.swapaxes(v_cache, 3, 4)

        inv_freq = 1.0 / (ROPE_BASE ** (jnp.arange(dim // 2, dtype=F32) * 2.0 / dim))
        angles = lax.dynamic_slice_in_dim(lengths, me, 1).astype(F32)[:, None] * inv_freq[None, :]
        repeat = 2 * w_key.shape[2] // dim
        turns = (jnp.tile(jnp.cos(angles), (1, repeat)), jnp.tile(jnp.sin(angles), (1, repeat)))

        _, counts = crossing(lengths - WINDOW, jnp.arange(n_sp) >= n_sp // 2, 2 * half)
        need = lax.pmax(jnp.max((counts.reshape(2, -1).sum(axis=1) + 1) // 2), "dp")
        choice = sum((need > size).astype(jnp.int32) for size in SIZES[:-1])

        def block(t, layer, relation):
            return lax.dynamic_slice(t, (layer, jnp.bitwise_xor(me, relation), 0, 0, 0), (1, 1, heads, dim, shard))[0, 0]

        weights = (w_query, w_key, w_value, w_gate, w_up, w_down)
        k_first = [swap(block(k_t, 0, r), "sp", r) for r in (2, 3)]
        nears = [swap(k_t, "sp", 1), swap(v_t, "sp", 1)]
        begun = front(0, dim, tp, hidden, (), ln_gain, turns, *weights)

        def run(size):
            return run_scoped(size)

        def run_scoped(size):
            k_win, v_win = fresh_buffers([(final, heads, dim, WINDOW)] * 2)
            pipes = [k_first + [swap(block(v_t, 0, r), "sp", r) for r in (2, 3)]]
            for layer in range(1, final):
                packed = pack(layer, size, ids, k_t, v_t, nears)
                pipes.append([swap(p, "sp", 2) for p in packed])
            residual, q, new_kv, mlp = begun
            for layer in range(n_layers):
                sliding = layer < final
                if layer:
                    residual, q, new_kv, mlp = front(layer, dim, tp, residual, parts, ln_gain, turns if sliding else (), *weights)
                if layer == 1:
                    cuts = after([block(t, final, r) for t in (k_t, v_t) for r in (2, 3)], q)
                    late = [swap(c, "sp", 2 + i % 2) for i, c in enumerate(cuts)]
                if sliding:
                    if layer and size < 2 * half:
                        pipes[layer].append(swap(after(pipes[layer][0], q), "sp", 1))
                    part, k_win, v_win = attend_window(layer, size if layer else None, ids, q, new_kv, mlp, w_out, k_t, v_t, nears, pipes[layer], k_win, v_win)
                else:
                    part, k_glob, v_glob = attend_global(layer, ids, q, new_kv, mlp, w_out, k_t, v_t, [nears[0]] + late[:2], [nears[1]] + late[2:])
                parts = (part,) + tuple(swap(part, "tp", r) for r in (1, 2, 3))
            return close(tp, residual, parts), k_win, v_win, k_glob, v_glob

        if len(SIZES) == 1:
            out, k_win, v_win, k_glob, v_glob = run(SIZES[0])
        else:
            out, k_win, v_win, k_glob, v_glob = lax.switch(choice, [functools.partial(run, size) for size in SIZES])
        back = lambda t: jnp.swapaxes(t, -1, -2)
        return out, back(k_win)[:, None], back(v_win)[:, None], back(k_glob)[None], back(v_glob)[None]


    return jax.shard_map(device_step, mesh=mesh, in_specs=in_specs, out_specs=out_specs, check_vma=False)
```

profile of v0, /device:TPU:0, one launch (start us, length us, event | category | flops | bytes accessed | tf_op | source)
XLA Modules:
  0.0 234.9 jit_solution(1875252015879711804)
XLA Ops:
  1.3 1.3 dynamic-slice_bitcast_fusion.24
  2.5 2.7 %collective-permute-start.97 = (bf16[2,64,2048]{2,1,0:T(8,128)(2,1)S(1)}, bf16[2,64,2048]{2,1,0:T(8,128)(2,1)}, u32[]{:S(2)}, u32[]{:S(2)}) collective-permute-start(bf16[2,64,2048]{2,1,0:T(8,128)(2,1)S(1)} %get-tuple-element.469), channel_id=1, source_target_pairs={{0,3},{1,2},{2,1},{3,0},{4,7},{5,6},{6,5},{7,4},{8,11},{9,10},{10,... | collective-permute-start | bytes 1572872 | tf_op jit(solution)/shard_map/ppermute | solution.py:466
  5.6 0.7 compare_select_fusion
  7.1 4.9 %pmax.7 = s32[]{:T(128)} all-reduce(s32[]{:T(128)} %fusion), channel_id=1, replica_groups=mesh['dp'=2,'tp'=4,'sp'=4] {'dp'}, use_global_device_ids=true, to_apply=%region_2.3 | all-reduce | flops 1 | bytes 8 | tf_op jit(solution)/shard_map/pmax | solution.py:485
  12.0 1.2 dynamic_slice.81
  16.1 13.6 %front.25 = (bf16[1,2048]{1,0:T(2,128)(2,1)S(1)}, f32[4,2,64]{2,1,0:T(2,128)S(1)}, f32[2,2,64]{2,1,0:T(2,128)S(1)}, f32[1,2048]{1,0:T(1,128)S(1)}) custom-call(s32[1]{0:T(128)} %bitcast.26.tp_ref, bf16[1,2048]{1,0:T(2,128)(2,1)} %h_ref.1, bf16[4,2048]{1,0:T(4,128)(2,1)} %refs_0_.1, f32[1,128]{1,0:T(1,128)S(1)} %tile.9.refs_1_, f32[1,128]{1,0:T(1,128)S(1)} %tile.21.refs_2_, ...), custom_call_target="tpu_custom_call" | custom-call | flops 28311552 | bytes 28311552 | tf_op jit(solution)/shard_map/front/pallas_call | solution.py:413
  29.9 203.7 %conditional.1 = (bf16[1,2048]{1,0:T(2,128)(2,1)S(1)}, bf16[3,2,64,4096]{3,2,1,0:T(8,128)(2,1)}, bf16[3,2,64,4096]{3,2,1,0:T(8,128)(2,1)}, bf16[2,64,8192]{2,1,0:T(8,128)(2,1)S(1)}, bf16[2,64,8192]{2,1,0:T(8,128)(2,1)}) conditional(s32[]{:T(128)} %clamp.3, (s32[]{:T(128)}, bf16[4,4,2,64,2048]{4,3,2,1,0:T(8,128)(2,1)}, ...), branch_computations={%region_3.4_spmd, %region_4.5_spmd, %region_5.6_spmd, %region_6.7_... | conditional | flops 114294792 | bytes 175900096 | solution.py:525
  29.9 2.9 %pack.8 = (bf16[2,2,64,2048]{3,2,1,0:T(8,128)(2,1)}, bf16[2,2,64,256]{3,2,1,0:T(8,128)(2,1)}) custom-call(s32[5]{0:T(128)S(1)} %get-tuple-element.186.ids, bf16[4,4,2,64,2048]{4,3,2,1,0:T(8,128)(2,1)} %get-tuple-element.191.k_own.own, bf16[4,4,2,64,2048]{4,3,2,1,0:T(8,128)(2,1)} %get-tuple-element.192.v_own.own, ...), custom_call_target="tpu_custom_call" | custom-call | flops 2359296 | bytes 2359296 | tf_op jit(solution)/shard_map/cond/branch_0_fun/pack/pallas_call | solution.py:89
  32.8 1.7 collective-permute-start.5
  34.5 2.9 %dynamic-slice_bitcast_fusion = (bf16[2,64,2048]{2,1,0:T(8,128)(2,1)}, bf16[2,64,2048]{2,1,0:T(8,128)(2,1)}, bf16[2,64,2048]{2,1,0:T(8,128)(2,1)}, bf16[2,64,2048]{2,1,0:T(8,128)(2,1)}) fusion(bf16[4,4,2,64,2048]{4,3,2,1,0:T(8,128)(2,1)} %get-tuple-element.192.v_own.own, s32[]{:T(128)S(6)} %select_n.36, s32[]{:T(128)S(6)} %select_n.35), kind=kLoop, calls=%fused_computation | loop fusion | bytes 4194312 | tf_op jit(solution)/shard_map/cond/branch_0_fun/squeeze | solution.py:489
  37.4 0.8 collective-permute-start
  38.2 31.4 %collective-permute-done.1.refs_3_ = bf16[2,64,2048]{2,1,0:T(8,128)(2,1)} collective-permute-done((bf16[2,64,2048]{2,1,0:T(8,128)(2,1)}, bf16[2,64,2048]{2,1,0:T(8,128)(2,1)}, u32[]{:S(2)}, u32[]{:S(2)}) %collective-permute-start.1) | collective-permute-done | bytes 524320 | tf_op jit(solution)/shard_map/cond/branch_0_fun/ppermute | solution.py:466
  69.6 10.5 %collective-permute-done.refs_2_ = bf16[2,64,2048]{2,1,0:T(8,128)(2,1)} collective-permute-done((bf16[2,64,2048]{2,1,0:T(8,128)(2,1)}, bf16[2,64,2048]{2,1,0:T(8,128)(2,1)}, u32[]{:S(2)}, u32[]{:S(2)}) %collective-permute-start) | collective-permute-done | bytes 524320 | tf_op jit(solution)/shard_map/cond/branch_0_fun/ppermute | solution.py:466
  80.1 5.6 %attend_window.12 = (f32[1,2048]{1,0:T(1,128)}, bf16[3,2,64,4096]{3,2,1,0:T(8,128)(2,1)S(1)}, bf16[3,2,64,4096]{3,2,1,0:T(8,128)(2,1)}) custom-call(s32[5]{0:T(128)S(1)} %get-tuple-element.186.ids, f32[4,2,64]{2,1,0:T(2,128)S(1)} %get-tuple-element.187.q_ref, ...), custom_call_target="tpu_custom_call", output_to_operand_aliasing={{1}: (13, {}), {2}: (14, {})} | custom-call | flops 4194304 | bytes 4194304 | tf_op jit(solution)/shard_map/cond/branch_0_fun/attend_window/pallas_call | solution.py:248
  85.7 3.9 %collective-permute-start.4 = (f32[1,2048]{1,0:T(1,128)}, f32[1,2048]{1,0:T(1,128)S(1)}, u32[]{:S(2)}, u32[]{:S(2)}) collective-permute-start(f32[1,2048]{1,0:T(1,128)} %get-tuple-element.200.refs_0_), channel_id=1, source_target_pairs={{0,12},{4,8},{8,4},{12,0},{1,13},{5,9},{9,5},{13,1},{2,14},{6,10},... | collective-permute-start | bytes 24584 | tf_op jit(solution)/shard_map/cond/branch_0_fun/ppermute | solution.py:466
  90.2 1.2 collective-permute-done.4.refs_3_
  91.4 2.9 %collective-permute-done.3.refs_2_ = f32[1,2048]{1,0:T(1,128)S(1)} collective-permute-done((f32[1,2048]{1,0:T(1,128)}, f32[1,2048]{1,0:T(1,128)S(1)}, u32[]{:S(2)}, u32[]{:S(2)}) %collective-permute-start.3) | collective-permute-done | bytes 8224 | tf_op jit(solution)/shard_map/cond/branch_0_fun/ppermute | solution.py:466
  94.9 13.4 %front.13 = (bf16[1,2048]{1,0:T(2,128)(2,1)}, f32[4,2,64]{2,1,0:T(2,128)}, f32[2,2,64]{2,1,0:T(2,128)}, f32[1,2048]{1,0:T(1,128)}) custom-call(s32[1]{0:T(128)} %get-tuple-element.184.tp_ref, bf16[1,2048]{1,0:T(2,128)(2,1)S(1)} %get-tuple-element.185.h_ref, f32[1,2048]{1,0:T(1,128)} %get-tuple-element.200.refs_0_, f32[1,2048]{1,0:T(1,128)} %copy-done.41, ...), custom_call_target="tpu_custom_call" | custom-call | flops 28311552 | bytes 28311552 | tf_op jit(solution)/shard_map/cond/branch_0_fun/front/pallas_call | solution.py:413
  108.5 2.9 %pack.9 = (bf16[2,2,64,2048]{3,2,1,0:T(8,128)(2,1)}, bf16[2,2,64,256]{3,2,1,0:T(8,128)(2,1)}) custom-call(s32[5]{0:T(128)S(1)} %get-tuple-element.186.ids, bf16[4,4,2,64,2048]{4,3,2,1,0:T(8,128)(2,1)} %get-tuple-element.191.k_own.own, bf16[4,4,2,64,2048]{4,3,2,1,0:T(8,128)(2,1)} %get-tuple-element.192.v_own.own, ...), custom_call_target="tpu_custom_call" | custom-call | flops 2359296 | bytes 2359296 | tf_op jit(solution)/shard_map/cond/branch_0_fun/pack/pallas_call | solution.py:89
  111.4 1.6 collective-permute-start.11
  113.5 26.5 %collective-permute-done.6.refs_1_ = bf16[2,2,64,256]{3,2,1,0:T(8,128)(2,1)S(1)} collective-permute-done((bf16[2,2,64,256]{3,2,1,0:T(8,128)(2,1)S(1)}, bf16[2,2,64,256]{3,2,1,0:T(8,128)(2,1)S(1)}, u32[]{:S(2)}, u32[]{:S(2)}) %collective-permute-start.6) | collective-permute-done | bytes 131104 | tf_op jit(solution)/shard_map/cond/branch_0_fun/ppermute | solution.py:466
  140.0 0.7 copy-done.13
  140.7 6.2 %attend_window.13 = (f32[1,2048]{1,0:T(1,128)}, bf16[3,2,64,4096]{3,2,1,0:T(8,128)(2,1)S(1)}, bf16[3,2,64,4096]{3,2,1,0:T(8,128)(2,1)}) custom-call(s32[5]{0:T(128)S(1)} %get-tuple-element.186.ids, f32[4,2,64]{2,1,0:T(2,128)} %get-tuple-element.211.q_ref, f32[2,2,64]{2,1,0:T(2,128)} %get-tuple-element.212.new_ref, ...), custom_call_target="tpu_custom_call", output_to_operand_aliasing={{1}: (12, {}), {2}: (13, {})} | custom-call | flops 4194304 | bytes 4194304 | tf_op jit(solution)/shard_map/cond/branch_0_fun/attend_window/pallas_call | solution.py:248
  146.9 1.5 collective-permute-start.10
  149.1 2.3 collective-permute-start.8
  151.4 1.3 collective-permute-done.10.refs_3_
  153.9 13.4 %front.14 = (bf16[1,2048]{1,0:T(2,128)(2,1)}, f32[4,2,64]{2,1,0:T(2,128)}, f32[2,2,64]{2,1,0:T(2,128)}, f32[1,2048]{1,0:T(1,128)}) custom-call(s32[1]{0:T(128)} %get-tuple-element.184.tp_ref, bf16[1,2048]{1,0:T(2,128)(2,1)} %get-tuple-element.210.h_ref, f32[1,2048]{1,0:T(1,128)} %get-tuple-element.219.refs_0_, f32[1,2048]{1,0:T(1,128)} %copy-done.34, ...), custom_call_target="tpu_custom_call" | custom-call | flops 28311552 | bytes 28311552 | tf_op jit(solution)/shard_map/cond/branch_0_fun/front/pallas_call | solution.py:413
  167.5 1.6 collective-permute-start.12
  169.1 2.3 dynamic-slice_bitcast_fusion.2
  171.9 1.0 collective-permute-start.18
  173.4 1.5 collective-permute-start.20
  174.9 1.0 copy-done.5
  175.9 6.2 %attend_window.14 = (f32[1,2048]{1,0:T(1,128)}, bf16[3,2,64,4096]{3,2,1,0:T(8,128)(2,1)S(1)}, bf16[3,2,64,4096]{3,2,1,0:T(8,128)(2,1)}) custom-call(s32[5]{0:T(128)S(1)} %get-tuple-element.186.ids, f32[4,2,64]{2,1,0:T(2,128)} %get-tuple-element.221.q_ref, f32[2,2,64]{2,1,0:T(2,128)} %get-tuple-element.222.new_ref, ...), custom_call_target="tpu_custom_call", output_to_operand_aliasing={{1}: (12, {}), {2}: (13, {})} | custom-call | flops 4194304 | bytes 4194304 | tf_op jit(solution)/shard_map/cond/branch_0_fun/attend_window/pallas_call | solution.py:248
  182.1 2.5 %collective-permute-start.16 = (f32[1,2048]{1,0:T(1,128)}, f32[1,2048]{1,0:T(1,128)S(1)}, u32[]{:S(2)}, u32[]{:S(2)}) collective-permute-start(f32[1,2048]{1,0:T(1,128)} %get-tuple-element.229.refs_0_), channel_id=1, source_target_pairs={{0,12},{4,8},{8,4},{12,0},{1,13},{5,9},{9,5},{13,1},{2,14},{6,10},... | collective-permute-start | bytes 24584 | tf_op jit(solution)/shard_map/cond/branch_0_fun/ppermute | solution.py:466
  184.7 3.2 %collective-permute-done.16.refs_3_ = f32[1,2048]{1,0:T(1,128)S(1)} collective-permute-done((f32[1,2048]{1,0:T(1,128)}, f32[1,2048]{1,0:T(1,128)S(1)}, u32[]{:S(2)}, u32[]{:S(2)}) %collective-permute-start.16) | collective-permute-done | bytes 8224 | tf_op jit(solution)/shard_map/cond/branch_0_fun/ppermute | solution.py:466
  188.0 4.6 %collective-permute-done.15.refs_2_ = f32[1,2048]{1,0:T(1,128)S(1)} collective-permute-done((f32[1,2048]{1,0:T(1,128)}, f32[1,2048]{1,0:T(1,128)S(1)}, u32[]{:S(2)}, u32[]{:S(2)}) %collective-permute-start.15) | collective-permute-done | bytes 8224 | tf_op jit(solution)/shard_map/cond/branch_0_fun/ppermute | solution.py:466
  192.7 3.7 %collective-permute-done.14.refs_1_ = f32[1,2048]{1,0:T(1,128)S(1)} collective-permute-done((f32[1,2048]{1,0:T(1,128)}, f32[1,2048]{1,0:T(1,128)S(1)}, u32[]{:S(2)}, u32[]{:S(2)}) %collective-permute-start.14) | collective-permute-done | bytes 8224 | tf_op jit(solution)/shard_map/cond/branch_0_fun/ppermute | solution.py:466
  197.1 13.2 %front.15 = (bf16[1,2048]{1,0:T(2,128)(2,1)}, f32[4,2,64]{2,1,0:T(2,128)}, f32[2,2,64]{2,1,0:T(2,128)}, f32[1,2048]{1,0:T(1,128)}) custom-call(s32[1]{0:T(128)} %get-tuple-element.184.tp_ref, bf16[1,2048]{1,0:T(2,128)(2,1)} %get-tuple-element.220.h_ref, f32[1,2048]{1,0:T(1,128)} %get-tuple-element.229.refs_0_, f32[1,2048]{1,0:T(1,128)} %copy-done.45, ...), custom_call_target="tpu_custom_call" | custom-call | flops 28311552 | bytes 28311552 | tf_op jit(solution)/shard_map/cond/branch_0_fun/front/pallas_call | solution.py:413
  210.4 4.3 %scores.4 = (bf16[8,8192]{1,0:T(8,128)(2,1)}, bf16[2,64,8192]{2,1,0:T(8,128)(2,1)S(1)}) custom-call(s32[5]{0:T(128)S(1)} %get-tuple-element.186.ids, f32[4,2,64]{2,1,0:T(2,128)} %get-tuple-element.231.q_ref, f32[2,2,64]{2,1,0:T(2,128)} %get-tuple-element.232.new_ref, bf16[4,4,2,64,2048]{4,3,2,1,0:T(8,128)(2,1)} %get-tuple-element.191.k_own.own, ...), custom_call_target="tpu_custom_call" | custom-call | flops 4194304 | bytes 4194304 | tf_op jit(solution)/shard_map/cond/branch_0_fun/scores/pallas_call | solution.py:308
  214.7 3.9 %collective-permute-done.20.b3 = bf16[2,64,2048]{2,1,0:T(8,128)(2,1)} collective-permute-done((bf16[2,64,2048]{2,1,0:T(8,128)(2,1)}, bf16[2,64,2048]{2,1,0:T(8,128)(2,1)}, u32[]{:S(2)}, u32[]{:S(2)}) %collective-permute-start.20) | collective-permute-done | bytes 524320 | tf_op jit(solution)/shard_map/cond/branch_0_fun/ppermute | solution.py:466
  218.6 6.0 %values.4 = (f32[1,2048]{1,0:T(1,128)}, bf16[2,64,8192]{2,1,0:T(8,128)(2,1)}) custom-call(s32[5]{0:T(128)S(1)} %get-tuple-element.186.ids, bf16[8,8192]{1,0:T(8,128)(2,1)} %get-tuple-element.235.w_ref, f32[2,2,64]{2,1,0:T(2,128)} %get-tuple-element.232.new_ref, f32[1,2048]{1,0:T(1,128)} %get-tuple-element.236.mlp_ref, ...), custom_call_target="tpu_custom_call" | custom-call | flops 4194304 | bytes 4194304 | tf_op jit(solution)/shard_map/cond/branch_0_fun/values/pallas_call | solution.py:317
  224.6 2.5 %collective-permute-start.23 = (f32[1,2048]{1,0:T(1,128)}, f32[1,2048]{1,0:T(1,128)S(1)}, u32[]{:S(2)}, u32[]{:S(2)}) collective-permute-start(f32[1,2048]{1,0:T(1,128)} %get-tuple-element.239.p0), channel_id=1, source_target_pairs={{0,12},{4,8},{8,4},{12,0},{1,13},{5,9},{9,5},{13,1},{2,14},{6,10},... | collective-permute-start | bytes 24584 | tf_op jit(solution)/shard_map/cond/branch_0_fun/ppermute | solution.py:466
  227.1 0.9 collective-permute-start.22
  228.0 1.0 collective-permute-start.21
  229.1 1.3 collective-permute-done.23.p3
  230.4 1.5 collective-permute-done.22.p2
  232.6 0.8 close.4
  234.2 0.7 copy-done.63
  (81 shorter events, 9.2 us)
Async XLA Ops:
  0.6 29.2 %collective-permute-start.95 = (bf16[4,4,2,64,2048]{4,3,2,1,0:T(8,128)(2,1)}, bf16[4,4,2,64,2048]{4,3,2,1,0:T(8,128)(2,1)}, u32[]{:S(2)}, u32[]{:S(2)}) collective-permute-start(bf16[4,4,2,64,2048]{4,3,2,1,0:T(8,128)(2,1)} %bitcast.73), channel_id=1, source_target_pairs={{0,1},{1,0},{2,3},{3,2},{4,5},{5,4},{6,7},{7,6},{8,9},{9,8},{10,11... | collective-permute-start | bytes 25165832 | tf_op jit(solution)/shard_map/ppermute | solution.py:466
  1.2 28.6 %collective-permute-start.94 = (bf16[4,4,2,64,2048]{4,3,2,1,0:T(8,128)(2,1)}, bf16[4,4,2,64,2048]{4,3,2,1,0:T(8,128)(2,1)}, u32[]{:S(2)}, u32[]{:S(2)}) collective-permute-start(bf16[4,4,2,64,2048]{4,3,2,1,0:T(8,128)(2,1)} %bitcast.78), channel_id=1, source_target_pairs={{0,1},{1,0},{2,3},{3,2},{4,5},{5,4},{6,7},{7,6},{8,9},{9,8},{10,11... | collective-permute-start | bytes 25165832 | tf_op jit(solution)/shard_map/ppermute | solution.py:466
  2.5 27.3 %collective-permute-start.97 = (bf16[2,64,2048]{2,1,0:T(8,128)(2,1)S(1)}, bf16[2,64,2048]{2,1,0:T(8,128)(2,1)}, u32[]{:S(2)}, u32[]{:S(2)}) collective-permute-start(bf16[2,64,2048]{2,1,0:T(8,128)(2,1)S(1)} %get-tuple-element.469), channel_id=1, source_target_pairs={{0,3},{1,2},{2,1},{3,0},{4,7},{5,6},{6,5},{7,4},{8,11},{9,10},{10,... | collective-permute-start | bytes 1572872 | tf_op jit(solution)/shard_map/ppermute | solution.py:466
  5.2 24.6 %collective-permute-start.96 = (bf16[2,64,2048]{2,1,0:T(8,128)(2,1)S(1)}, bf16[2,64,2048]{2,1,0:T(8,128)(2,1)}, u32[]{:S(2)}, u32[]{:S(2)}) collective-permute-start(bf16[2,64,2048]{2,1,0:T(8,128)(2,1)S(1)} %get-tuple-element.470), channel_id=1, source_target_pairs={{0,2},{1,3},{2,0},{3,1},{4,6},{5,7},{6,4},{7,5},{8,10},{9,11},{10,... | collective-permute-start | bytes 1572872 | tf_op jit(solution)/shard_map/ppermute | solution.py:466
  16.1 13.6 %copy-start.66 = (s32[4]{0:T(128)S(1)}, s32[4]{0:T(128)}, u32[]{:S(2)}) copy-start(s32[4]{0:T(128)} %param.18) | copy-start | bytes 52
  16.1 13.8 %copy-start.4 = (bf16[4,2048]{1,0:T(4,128)(2,1)S(1)}, bf16[4,2048]{1,0:T(4,128)(2,1)}, u32[]{:S(2)}) copy-start(bf16[4,2048]{1,0:T(4,128)(2,1)} %refs_0_.1) | copy-start | bytes 49156
  32.8 75.6 %collective-permute-start.5 = (bf16[2,2,64,2048]{3,2,1,0:T(8,128)(2,1)}, bf16[2,2,64,2048]{3,2,1,0:T(8,128)(2,1)}, u32[]{:S(2)}, u32[]{:S(2)}) collective-permute-start(bf16[2,2,64,2048]{3,2,1,0:T(8,128)(2,1)} %get-tuple-element.214), channel_id=1, source_target_pairs={{0,2},{1,3},{2,0},{3,1},{4,6},{5,7},{6,4},{7,5},{8,10},{9,11},{10,... | collective-permute-start | bytes 3145736 | tf_op jit(solution)/shard_map/cond/branch_0_fun/ppermute | solution.py:466
  37.4 32.2 %collective-permute-start.1 = (bf16[2,64,2048]{2,1,0:T(8,128)(2,1)}, bf16[2,64,2048]{2,1,0:T(8,128)(2,1)}, u32[]{:S(2)}, u32[]{:S(2)}) collective-permute-start(bf16[2,64,2048]{2,1,0:T(8,128)(2,1)} %get-tuple-element.447), channel_id=1, source_target_pairs={{0,3},{1,2},{2,1},{3,0},{4,7},{5,6},{6,5},{7,4},{8,11},{9,10},{10,... | collective-permute-start | bytes 1572872 | tf_op jit(solution)/shard_map/cond/branch_0_fun/ppermute | solution.py:466
  37.4 42.7 %collective-permute-start = (bf16[2,64,2048]{2,1,0:T(8,128)(2,1)}, bf16[2,64,2048]{2,1,0:T(8,128)(2,1)}, u32[]{:S(2)}, u32[]{:S(2)}) collective-permute-start(bf16[2,64,2048]{2,1,0:T(8,128)(2,1)} %get-tuple-element.448), channel_id=1, source_target_pairs={{0,2},{1,3},{2,0},{3,1},{4,6},{5,7},{6,4},{7,5},{8,10},{9,11},{10,... | collective-permute-start | bytes 1572872 | tf_op jit(solution)/shard_map/cond/branch_0_fun/ppermute | solution.py:466
  85.7 5.7 %collective-permute-start.4 = (f32[1,2048]{1,0:T(1,128)}, f32[1,2048]{1,0:T(1,128)S(1)}, u32[]{:S(2)}, u32[]{:S(2)}) collective-permute-start(f32[1,2048]{1,0:T(1,128)} %get-tuple-element.200.refs_0_), channel_id=1, source_target_pairs={{0,12},{4,8},{8,4},{12,0},{1,13},{5,9},{9,5},{13,1},{2,14},{6,10},... | collective-permute-start | bytes 24584 | tf_op jit(solution)/shard_map/cond/branch_0_fun/ppermute | solution.py:466
  89.6 4.8 %collective-permute-start.3 = (f32[1,2048]{1,0:T(1,128)}, f32[1,2048]{1,0:T(1,128)S(1)}, u32[]{:S(2)}, u32[]{:S(2)}) collective-permute-start(f32[1,2048]{1,0:T(1,128)} %get-tuple-element.200.refs_0_), channel_id=1, source_target_pairs={{0,8},{4,12},{8,0},{12,4},{1,9},{5,13},{9,1},{13,5},{2,10},{6,14},... | collective-permute-start | bytes 24584 | tf_op jit(solution)/shard_map/cond/branch_0_fun/ppermute | solution.py:466
  89.6 4.8 %collective-permute-start.2 = (f32[1,2048]{1,0:T(1,128)}, f32[1,2048]{1,0:T(1,128)S(1)}, u32[]{:S(2)}, u32[]{:S(2)}) collective-permute-start(f32[1,2048]{1,0:T(1,128)} %get-tuple-element.200.refs_0_), channel_id=1, source_target_pairs={{0,4},{4,0},{8,12},{12,8},{1,5},{5,1},{9,13},{13,9},{2,6},{6,2},{1... | collective-permute-start | bytes 24584 | tf_op jit(solution)/shard_map/cond/branch_0_fun/ppermute | solution.py:466
  91.4 2.9 %copy-start.24 = (f32[1,2048]{1,0:T(1,128)}, f32[1,2048]{1,0:T(1,128)S(1)}, u32[]{:S(2)}) copy-start(f32[1,2048]{1,0:T(1,128)S(1)} %collective-permute-done.4.refs_3_) | copy-start | bytes 24580 | tf_op jit(solution)/shard_map/cond
  94.3 0.6 copy-start.31
  94.3 0.6 copy-start.41
  108.4 4.6 %copy-start.64 = (bf16[2,2,64,256]{3,2,1,0:T(8,128)(2,1)S(1)}, bf16[2,2,64,256]{3,2,1,0:T(8,128)(2,1)}, u32[]{:S(2)}) copy-start(bf16[2,2,64,256]{3,2,1,0:T(8,128)(2,1)} %get-tuple-element.215) | copy-start | bytes 393220 | tf_op jit(solution)/shard_map/cond
  108.4 31.6 %collective-permute-start.7 = (bf16[2,2,64,2048]{3,2,1,0:T(8,128)(2,1)}, bf16[2,2,64,2048]{3,2,1,0:T(8,128)(2,1)}, u32[]{:S(2)}, u32[]{:S(2)}) collective-permute-start(bf16[2,2,64,2048]{3,2,1,0:T(8,128)(2,1)} %collective-permute-done.5.refs_0_), channel_id=1, source_target_pairs={{0,1},{1,0},{2,3},{3,2},{4,5},{5,4},{6,7},{7,6},{8,9},{9,8},{10,11... | collective-permute-start | bytes 3145736 | tf_op jit(solution)/shard_map/cond/branch_0_fun/ppermute | solution.py:466
  111.4 56.0 %collective-permute-start.11 = (bf16[2,2,64,2048]{3,2,1,0:T(8,128)(2,1)}, bf16[2,2,64,2048]{3,2,1,0:T(8,128)(2,1)}, u32[]{:S(2)}, u32[]{:S(2)}) collective-permute-start(bf16[2,2,64,2048]{3,2,1,0:T(8,128)(2,1)} %get-tuple-element.224), channel_id=1, source_target_pairs={{0,2},{1,3},{2,0},{3,1},{4,6},{5,7},{6,4},{7,5},{8,10},{9,11},{10,... | collective-permute-start | bytes 3145736 | tf_op jit(solution)/shard_map/cond/branch_0_fun/ppermute | solution.py:466
  113.0 27.1 %collective-permute-start.6 = (bf16[2,2,64,256]{3,2,1,0:T(8,128)(2,1)S(1)}, bf16[2,2,64,256]{3,2,1,0:T(8,128)(2,1)S(1)}, u32[]{:S(2)}, u32[]{:S(2)}) collective-permute-start(bf16[2,2,64,256]{3,2,1,0:T(8,128)(2,1)S(1)} %copy-done.64), channel_id=1, source_target_pairs={{0,2},{1,3},{2,0},{3,1},{4,6},{5,7},{6,4},{7,5},{8,10},{9,11},{10,... | collective-permute-start | bytes 393224 | tf_op jit(solution)/shard_map/cond/branch_0_fun/ppermute | solution.py:466
  140.0 0.7 copy-start.13
  146.9 5.7 %collective-permute-start.10 = (f32[1,2048]{1,0:T(1,128)}, f32[1,2048]{1,0:T(1,128)S(1)}, u32[]{:S(2)}, u32[]{:S(2)}) collective-permute-start(f32[1,2048]{1,0:T(1,128)} %get-tuple-element.219.refs_0_), channel_id=1, source_target_pairs={{0,12},{4,8},{8,4},{12,0},{1,13},{5,9},{9,5},{13,1},{2,14},{6,10},... | collective-permute-start | bytes 24584 | tf_op jit(solution)/shard_map/cond/branch_0_fun/ppermute | solution.py:466
  148.5 4.8 %collective-permute-start.9 = (f32[1,2048]{1,0:T(1,128)}, f32[1,2048]{1,0:T(1,128)S(1)}, u32[]{:S(2)}, u32[]{:S(2)}) collective-permute-start(f32[1,2048]{1,0:T(1,128)} %get-tuple-element.219.refs_0_), channel_id=1, source_target_pairs={{0,8},{4,12},{8,0},{12,4},{1,9},{5,13},{9,1},{13,5},{2,10},{6,14},... | collective-permute-start | bytes 24584 | tf_op jit(solution)/shard_map/cond/branch_0_fun/ppermute | solution.py:466
  149.1 4.2 %collective-permute-start.8 = (f32[1,2048]{1,0:T(1,128)}, f32[1,2048]{1,0:T(1,128)S(1)}, u32[]{:S(2)}, u32[]{:S(2)}) collective-permute-start(f32[1,2048]{1,0:T(1,128)} %get-tuple-element.219.refs_0_), channel_id=1, source_target_pairs={{0,4},{4,0},{8,12},{12,8},{1,5},{5,1},{9,13},{13,9},{2,6},{6,2},{1... | collective-permute-start | bytes 24584 | tf_op jit(solution)/shard_map/cond/branch_0_fun/ppermute | solution.py:466
  152.6 0.7 copy-start.17
  153.3 0.6 copy-start.34
  153.9 13.5 %copy-start.65 = (bf16[2,2,64,256]{3,2,1,0:T(8,128)(2,1)S(1)}, bf16[2,2,64,256]{3,2,1,0:T(8,128)(2,1)}, u32[]{:S(2)}) copy-start(bf16[2,2,64,256]{3,2,1,0:T(8,128)(2,1)} %get-tuple-element.225) | copy-start | bytes 393220 | tf_op jit(solution)/shard_map/cond
  167.4 7.5 %collective-permute-start.13 = (bf16[2,2,64,2048]{3,2,1,0:T(8,128)(2,1)}, bf16[2,2,64,2048]{3,2,1,0:T(8,128)(2,1)S(1)}, u32[]{:S(2)}, u32[]{:S(2)}) collective-permute-start(bf16[2,2,64,2048]{3,2,1,0:T(8,128)(2,1)} %collective-permute-done.11.refs_0_), channel_id=1, source_target_pairs={{0,1},{1,0},{2,3},{3,2},{4,5},{5,4},{6,7},{7,6},{8,9},{9,8},{10,11... | collective-permute-start | bytes 3145736 | tf_op jit(solution)/shard_map/cond/branch_0_fun/ppermute | solution.py:466
  167.5 6.0 %collective-permute-start.12 = (bf16[2,2,64,256]{3,2,1,0:T(8,128)(2,1)S(1)}, bf16[2,2,64,256]{3,2,1,0:T(8,128)(2,1)S(1)}, u32[]{:S(2)}, u32[]{:S(2)}) collective-permute-start(bf16[2,2,64,256]{3,2,1,0:T(8,128)(2,1)S(1)} %copy-done.65), channel_id=1, source_target_pairs={{0,2},{1,3},{2,0},{3,1},{4,6},{5,7},{6,4},{7,5},{8,10},{9,11},{10,... | collective-permute-start | bytes 393224 | tf_op jit(solution)/shard_map/cond/branch_0_fun/ppermute | solution.py:466
  171.4 38.9 %collective-permute-start.17 = (bf16[2,64,2048]{2,1,0:T(8,128)(2,1)}, bf16[2,64,2048]{2,1,0:T(8,128)(2,1)}, u32[]{:S(2)}, u32[]{:S(2)}) collective-permute-start(bf16[2,64,2048]{2,1,0:T(8,128)(2,1)} %get-tuple-element.233), channel_id=1, source_target_pairs={{0,2},{1,3},{2,0},{3,1},{4,6},{5,7},{6,4},{7,5},{8,10},{9,11},{10,... | collective-permute-start | bytes 1572872 | tf_op jit(solution)/shard_map/cond/branch_0_fun/ppermute | solution.py:466
  171.9 38.5 %collective-permute-start.18 = (bf16[2,64,2048]{2,1,0:T(8,128)(2,1)}, bf16[2,64,2048]{2,1,0:T(8,128)(2,1)}, u32[]{:S(2)}, u32[]{:S(2)}) collective-permute-start(bf16[2,64,2048]{2,1,0:T(8,128)(2,1)} %get-tuple-element.234), channel_id=1, source_target_pairs={{0,3},{1,2},{2,1},{3,0},{4,7},{5,6},{6,5},{7,4},{8,11},{9,10},{10,... | collective-permute-start | bytes 1572872 | tf_op jit(solution)/shard_map/cond/branch_0_fun/ppermute | solution.py:466
  172.9 41.8 %collective-permute-start.19 = (bf16[2,64,2048]{2,1,0:T(8,128)(2,1)}, bf16[2,64,2048]{2,1,0:T(8,128)(2,1)}, u32[]{:S(2)}, u32[]{:S(2)}) collective-permute-start(bf16[2,64,2048]{2,1,0:T(8,128)(2,1)} %get-tuple-element.237), channel_id=1, source_target_pairs={{0,2},{1,3},{2,0},{3,1},{4,6},{5,7},{6,4},{7,5},{8,10},{9,11},{10,... | collective-permute-start | bytes 1572872 | tf_op jit(solution)/shard_map/cond/branch_0_fun/ppermute | solution.py:466
  173.4 2.4 %copy-start.12 = (bf16[2,2,64,256]{3,2,1,0:T(8,128)(2,1)}, bf16[2,2,64,256]{3,2,1,0:T(8,128)(2,1)S(1)}, u32[]{:S(2)}) copy-start(bf16[2,2,64,256]{3,2,1,0:T(8,128)(2,1)S(1)} %collective-permute-done.12.refs_1_) | copy-start | bytes 393220 | tf_op jit(solution)/shard_map/cond
  173.4 45.1 %collective-permute-start.20 = (bf16[2,64,2048]{2,1,0:T(8,128)(2,1)}, bf16[2,64,2048]{2,1,0:T(8,128)(2,1)}, u32[]{:S(2)}, u32[]{:S(2)}) collective-permute-start(bf16[2,64,2048]{2,1,0:T(8,128)(2,1)} %get-tuple-element.238), channel_id=1, source_target_pairs={{0,3},{1,2},{2,1},{3,0},{4,7},{5,6},{6,5},{7,4},{8,11},{9,10},{10,... | collective-permute-start | bytes 1572872 | tf_op jit(solution)/shard_map/cond/branch_0_fun/ppermute | solution.py:466
  174.9 1.0 copy-start.5
  182.1 28.2 %copy-start = (bf16[3,2,64,4096]{3,2,1,0:T(8,128)(2,1)}, bf16[3,2,64,4096]{3,2,1,0:T(8,128)(2,1)S(1)}, u32[]{:S(2)}) copy-start(bf16[3,2,64,4096]{3,2,1,0:T(8,128)(2,1)S(1)} %get-tuple-element.474) | copy-start | bytes 9437188 | tf_op jit(solution)/shard_map/cond
  182.1 5.7 %collective-permute-start.16 = (f32[1,2048]{1,0:T(1,128)}, f32[1,2048]{1,0:T(1,128)S(1)}, u32[]{:S(2)}, u32[]{:S(2)}) collective-permute-start(f32[1,2048]{1,0:T(1,128)} %get-tuple-element.229.refs_0_), channel_id=1, source_target_pairs={{0,12},{4,8},{8,4},{12,0},{1,13},{5,9},{9,5},{13,1},{2,14},{6,10},... | collective-permute-start | bytes 24584 | tf_op jit(solution)/shard_map/cond/branch_0_fun/ppermute | solution.py:466
  187.9 8.6 %copy-start.18 = (f32[1,2048]{1,0:T(1,128)}, f32[1,2048]{1,0:T(1,128)S(1)}, u32[]{:S(2)}) copy-start(f32[1,2048]{1,0:T(1,128)S(1)} %collective-permute-done.16.refs_3_) | copy-start | bytes 24580 | tf_op jit(solution)/shard_map/cond
  187.9 4.8 %collective-permute-start.15 = (f32[1,2048]{1,0:T(1,128)}, f32[1,2048]{1,0:T(1,128)S(1)}, u32[]{:S(2)}, u32[]{:S(2)}) collective-permute-start(f32[1,2048]{1,0:T(1,128)} %get-tuple-element.229.refs_0_), channel_id=1, source_target_pairs={{0,8},{4,12},{8,0},{12,4},{1,9},{5,13},{9,1},{13,5},{2,10},{6,14},... | collective-permute-start | bytes 24584 | tf_op jit(solution)/shard_map/cond/branch_0_fun/ppermute | solution.py:466
  192.6 3.9 %copy-start.35 = (f32[1,2048]{1,0:T(1,128)}, f32[1,2048]{1,0:T(1,128)S(1)}, u32[]{:S(2)}) copy-start(f32[1,2048]{1,0:T(1,128)S(1)} %collective-permute-done.15.refs_2_) | copy-start | bytes 24580 | tf_op jit(solution)/shard_map/cond
  192.6 3.9 %collective-permute-start.14 = (f32[1,2048]{1,0:T(1,128)}, f32[1,2048]{1,0:T(1,128)S(1)}, u32[]{:S(2)}, u32[]{:S(2)}) collective-permute-start(f32[1,2048]{1,0:T(1,128)} %get-tuple-element.229.refs_0_), channel_id=1, source_target_pairs={{0,4},{4,0},{8,12},{12,8},{1,5},{5,1},{9,13},{13,9},{2,6},{6,2},{1... | collective-permute-start | bytes 24584 | tf_op jit(solution)/shard_map/cond/branch_0_fun/ppermute | solution.py:466
  196.5 0.6 copy-start.45
  224.6 5.8 %collective-permute-start.23 = (f32[1,2048]{1,0:T(1,128)}, f32[1,2048]{1,0:T(1,128)S(1)}, u32[]{:S(2)}, u32[]{:S(2)}) collective-permute-start(f32[1,2048]{1,0:T(1,128)} %get-tuple-element.239.p0), channel_id=1, source_target_pairs={{0,12},{4,8},{8,4},{12,0},{1,13},{5,9},{9,5},{13,1},{2,14},{6,10},... | collective-permute-start | bytes 24584 | tf_op jit(solution)/shard_map/cond/branch_0_fun/ppermute | solution.py:466
  227.1 4.8 %collective-permute-start.22 = (f32[1,2048]{1,0:T(1,128)}, f32[1,2048]{1,0:T(1,128)S(1)}, u32[]{:S(2)}, u32[]{:S(2)}) collective-permute-start(f32[1,2048]{1,0:T(1,128)} %get-tuple-element.239.p0), channel_id=1, source_target_pairs={{0,8},{4,12},{8,0},{12,4},{1,9},{5,13},{9,1},{13,5},{2,10},{6,14},... | collective-permute-start | bytes 24584 | tf_op jit(solution)/shard_map/cond/branch_0_fun/ppermute | solution.py:466
  228.0 3.9 %collective-permute-start.21 = (f32[1,2048]{1,0:T(1,128)}, f32[1,2048]{1,0:T(1,128)S(1)}, u32[]{:S(2)}, u32[]{:S(2)}) collective-permute-start(f32[1,2048]{1,0:T(1,128)} %get-tuple-element.239.p0), channel_id=1, source_target_pairs={{0,4},{4,0},{8,12},{12,8},{1,5},{5,1},{9,13},{13,9},{2,6},{6,2},{1... | collective-permute-start | bytes 24584 | tf_op jit(solution)/shard_map/cond/branch_0_fun/ppermute | solution.py:466
  230.4 1.6 copy-start.50
  232.0 0.6 copy-start.58
  233.6 0.6 copy-start.62
  233.6 1.3 copy-start.63
  (2 other events, 1.2 us)
where the time goes:
time: 236 us; the launch traced here: 235 us
  waiting for transfers between devices  92.8 us (39%)
  Pallas kernels  88.8 us (38%)
  starting transfers between devices  29.8 us (13%)
  local copies, waits for them, and re-layouts  13.3 us (6%)
  blocking collectives  4.89 us (2%)
  between operations  3.31 us (1%)
    ppermute x28, waiting for transfers between devices, swap(): lax.ppermute(t, axis, [(i, i ^ relation) for i in range(n_sp if axis == '...  92.8 us
    pallas_call x4, Pallas kernels, front(): pl.pallas_call(functools.partial(body, layer, dim, n_parts), grid=(FFN_ST...  53.7 us
    ppermute x28, starting transfers between devices, swap(): lax.ppermute(t, axis, [(i, i ^ relation) for i in range(n_sp if axis == '...  29.8 us
    pallas_call x3, Pallas kernels, attend_window(): pl.pallas_call(functools.partial(window_body, layer, size, half, n_pipe),...  18.1 us
    squeeze x3, local copies, waits for them, and re-layouts, block(): lax.dynamic_slice(t, (layer, jnp.bitwise_xor(me, relation), 0, 0, 0), (1,...  6.49 us
    pallas_call x1, Pallas kernels, attend_global(): pl.pallas_call(functools.partial(values_body, layer), in_specs=[SMEM, VME...  6.02 us
    pallas_call x2, Pallas kernels, pack(): pl.pallas_call(functools.partial(pack_body, layer, size, half), in_specs=...  5.82 us
    pmax x1, blocking collectives, device_step(): need = lax.pmax(jnp.max((counts.reshape(2, -1).sum(axis=1) + 1) // 2), 'dp')  4.89 us
  transfers between devices with their start and end apart: 28, of which 15 were waited for; matrix products, arithmetic and copies ran while one was open for 4% of the time, Pallas kernels for 34%

commit v1 on v0

--- a/solution.py
+++ b/solution.py
@@ -326,19 +326,45 @@
     return part, k_glob, v_glob
 
 
-def summed(tp, residual, parts):
-    total = residual.astype(F32)
+def tp_sum_body(part_ref, h_ref, out_ref, slots, send_sems, recv_sems):
+    tp = lax.axis_index("tp")
+    barrier = pltpu.get_barrier_semaphore()
+    peers = [{"tp": jnp.bitwise_xor(tp, r)} for r in (1, 2, 3)]
+    for peer in peers:
+        pl.semaphore_signal(barrier, inc=1, device_id=peer, device_id_type=pl.DeviceIdType.MESH)
+    pl.semaphore_wait(barrier, 3)
+    copies = [
+        pltpu.make_async_remote_copy(part_ref, slots.at[i], send_sems.at[i], recv_sems.at[i], device_id=peer, device_id_type=pl.DeviceIdType.MESH)
+        for i, peer in enumerate(peers)
+    ]
+    for copy in copies:
+        copy.start()
+    for copy in copies:
+        copy.wait()
+    parts = [part_ref[...]] + [slots[i] for i in range(3)]
     for t in range(4):
         at = jnp.bitwise_xor(tp, t)
-        pick = parts[3][...]
+        pick = parts[3]
         for r in range(3):
-            pick = jnp.where(at == r, parts[r][...], pick)
+            pick = jnp.where(at == r, parts[r], pick)
         total = pick if t == 0 else total + pick
-    return (residual.astype(F32) + total).astype(BF16)
-
-
-def front_body(layer, dim, n_parts, tp_ref, h_ref, *refs):
-    parts, (gain, cosine, sine, wq, wk, wv, wg, wu, wd, h_out, q_out, new_out, mlp_out, u, acc) = refs[:n_parts], refs[n_parts:]
+    out_ref[...] = (h_ref[...].astype(F32) + total).astype(BF16)
+
+
+def tp_sum(layer, part, residual):
+    return pl.pallas_call(
+        tp_sum_body,
+        in_specs=[VMEM, VMEM],
+        out_specs=VMEM,
+        out_shape=jax.ShapeDtypeStruct(residual.shape, BF16),
+        scratch_shapes=[pltpu.VMEM((3,) + part.shape, F32), pltpu.SemaphoreType.DMA((3,)), pltpu.SemaphoreType.DMA((3,))],
+        compiler_params=pltpu.CompilerParams(collective_id=layer, has_side_effects=True),
+        cost_estimate=cost(12 * part.size),
+        name="tp_sum",
+    )(part, residual)
+
+
+def front_body(layer, dim, h_ref, gain, cosine, sine, wq, wk, wv, wg, wu, wd, q_out, new_out, mlp_out, u, acc):
     step = pl.program_id(0)
 
     def turn(proj):
@@ -365,9 +391,7 @@
 
     @pl.when(step == 0)
     def _():
-        h = summed(tp_ref[0], h_ref[...], parts) if n_parts else h_ref[...]
-        h_out[...] = h
-        rows32 = h.astype(F32)
+        rows32 = h_ref[...].astype(F32)
         centered = rows32 - rows32.mean(axis=-1, keepdims=True)
         variance = (centered * centered).mean(axis=-1, keepdims=True)
         scaled = centered * lax.rsqrt(variance + NORM_EPS) * gain[...].astype(F32)[layer:layer + 1]
@@ -397,27 +421,25 @@
         mlp_out[...] = acc[0:1, :]
 
 
-def plain_front_body(layer, dim, n_parts, tp_ref, h_ref, *refs):
-    front_body(layer, dim, n_parts, tp_ref, h_ref, *refs[:n_parts + 1], None, None, *refs[n_parts + 1:])
-
-
-def front(layer, dim, tp, residual, parts, ln_gain, turns, w_query, w_key, w_value, w_gate, w_up, w_down):
+def plain_front_body(layer, dim, h_ref, gain, *refs):
+    front_body(layer, dim, h_ref, gain, None, None, *refs)
+
+
+def front(layer, dim, residual, ln_gain, turns, w_query, w_key, w_value, w_gate, w_up, w_down):
     width = residual.shape[1]
     q_width, kv_width, ffn = w_query.shape[2], w_key.shape[2], w_gate.shape[2]
     q_step, ffn_step = q_width // FFN_STEPS, ffn // FFN_STEPS
     whole = lambda *shape: pl.BlockSpec(shape, lambda j: (0,) * len(shape))
     col = lambda rows, cols: pl.BlockSpec((1, rows, cols), lambda j: (layer, 0, j))
     fixed = lambda rows, cols: pl.BlockSpec((1, rows, cols), lambda j: (layer, 0, 0))
-    n_parts = len(parts)
     body = front_body if turns else plain_front_body
     return pl.pallas_call(
-        functools.partial(body, layer, dim, n_parts),
+        functools.partial(body, layer, dim),
         grid=(FFN_STEPS,),
-        in_specs=[SMEM, whole(1, width)] + [whole(1, width)] * n_parts + [whole(*ln_gain.shape)] + [whole(1, kv_width)] * len(turns)
+        in_specs=[whole(1, width), whole(*ln_gain.shape)] + [whole(1, kv_width)] * len(turns)
         + [col(width, q_step), fixed(width, kv_width), fixed(width, kv_width), col(width, ffn_step), col(width, ffn_step), pl.BlockSpec((1, ffn_step, width), lambda j: (layer, j, 0))],
-        out_specs=[whole(1, width), pl.BlockSpec((1, q_step // dim, dim), lambda j: (j, 0, 0)), whole(2, kv_width // dim, dim), whole(1, width)],
+        out_specs=[pl.BlockSpec((1, q_step // dim, dim), lambda j: (j, 0, 0)), whole(2, kv_width // dim, dim), whole(1, width)],
         out_shape=[
-            jax.ShapeDtypeStruct((1, width), BF16),
             jax.ShapeDtypeStruct((FFN_STEPS, q_step // dim, dim), F32),
             jax.ShapeDtypeStruct((2, kv_width // dim, dim), F32),
             jax.ShapeDtypeStruct((1, width), F32),
@@ -426,21 +448,7 @@
         compiler_params=pltpu.CompilerParams(dimension_semantics=("arbitrary",)),
         cost_estimate=cost(2 * width * (q_width + 2 * kv_width + 3 * ffn)),
         name="front",
-    )(tp, residual, *parts, ln_gain, *turns, w_query, w_key, w_value, w_gate, w_up, w_down)
-
-
-def close_body(tp_ref, h_ref, p0, p1, p2, p3, out_ref):
-    out_ref[...] = summed(tp_ref[0], h_ref[...], (p0, p1, p2, p3))
-
-
-def close(tp, residual, parts):
-    return pl.pallas_call(
-        close_body,
-        in_specs=[SMEM] + [VMEM] * 5,
-        out_specs=VMEM,
-        out_shape=jax.ShapeDtypeStruct(residual.shape, BF16),
-        name="close",
-    )(tp, residual, *parts)
+    )(residual, ln_gain, *turns, w_query, w_key, w_value, w_gate, w_up, w_down)
 
 
 def fresh_body(*refs):
@@ -460,10 +468,10 @@
     global_spec = P(("dp", "sp"), "tp", None, None)
     in_specs = (cache_spec, cache_spec, P("dp"), row_spec, P(None, None), col_spec, col_spec, col_spec, inner_spec, col_spec, col_spec, inner_spec)
     out_specs = (row_spec, window_spec, window_spec, global_spec, global_spec)
-    n_sp, n_tp = mesh.shape["sp"], mesh.shape["tp"]
+    n_sp = mesh.shape["sp"]
 
     def swap(t, axis, relation):
-        return lax.ppermute(t, axis, [(i, i ^ relation) for i in range(n_sp if axis == "sp" else n_tp)])
+        return lax.ppermute(t, axis, [(i, i ^ relation) for i in range(n_sp)])
 
     def device_step(k_cache, v_cache, lengths, hidden, ln_gain, w_query, w_key, w_value, w_out, w_gate, w_up, w_down):
         n_layers = w_query.shape[0]
@@ -471,7 +479,6 @@
         half = shard // UNIT
         final = n_layers - 1
         me = lax.axis_index("sp").astype(jnp.int32)
-        tp = lax.axis_index("tp").astype(jnp.int32)[None]
         ids = jnp.concatenate([me[None], lengths])
         k_t = jnp.swapaxes(k_cache, 3, 4)
         v_t = jnp.swapaxes(v_cache, 3, 4)
@@ -490,23 +497,24 @@
 
         weights = (w_query, w_key, w_value, w_gate, w_up, w_down)
         k_first = [swap(block(k_t, 0, r), "sp", r) for r in (2, 3)]
+        v_far = swap(block(v_t, 0, 2), "sp", 2)
         nears = [swap(k_t, "sp", 1), swap(v_t, "sp", 1)]
-        begun = front(0, dim, tp, hidden, (), ln_gain, turns, *weights)
+        begun = front(0, dim, hidden, ln_gain, turns, *weights)
 
         def run(size):
             return run_scoped(size)
 
         def run_scoped(size):
             k_win, v_win = fresh_buffers([(final, heads, dim, WINDOW)] * 2)
-            pipes = [k_first + [swap(block(v_t, 0, r), "sp", r) for r in (2, 3)]]
+            pipes = [k_first + [v_far, swap(block(v_t, 0, 3), "sp", 3)]]
             for layer in range(1, final):
                 packed = pack(layer, size, ids, k_t, v_t, nears)
                 pipes.append([swap(p, "sp", 2) for p in packed])
-            residual, q, new_kv, mlp = begun
+            residual, (q, new_kv, mlp) = hidden, begun
             for layer in range(n_layers):
                 sliding = layer < final
                 if layer:
-                    residual, q, new_kv, mlp = front(layer, dim, tp, residual, parts, ln_gain, turns if sliding else (), *weights)
+                    q, new_kv, mlp = front(layer, dim, residual, ln_gain, turns if sliding else (), *weights)
                 if layer == 1:
                     cuts = after([block(t, final, r) for t in (k_t, v_t) for r in (2, 3)], q)
                     late = [swap(c, "sp", 2 + i % 2) for i, c in enumerate(cuts)]
@@ -516,8 +524,8 @@
                     part, k_win, v_win = attend_window(layer, size if layer else None, ids, q, new_kv, mlp, w_out, k_t, v_t, nears, pipes[layer], k_win, v_win)
                 else:
                     part, k_glob, v_glob = attend_global(layer, ids, q, new_kv, mlp, w_out, k_t, v_t, [nears[0]] + late[:2], [nears[1]] + late[2:])
-                parts = (part,) + tuple(swap(part, "tp", r) for r in (1, 2, 3))
-            return close(tp, residual, parts), k_win, v_win, k_glob, v_glob
+                residual = tp_sum(layer, part, residual)
+            return residual, k_win, v_win, k_glob, v_glob
 
         if len(SIZES) == 1:
             out, k_win, v_win, k_glob, v_glob = run(SIZES[0])

time: 236 us -> 229 us (0.970)
  Pallas kernels: 88.8 us -> 116 us
  starting transfers between devices: 29.8 us -> 13.4 us
  waiting for transfers between devices: 92.8 us -> 78.3 us
  local copies, waits for them, and re-layouts: 13.3 us -> 10.2 us
    pallas_call x5 -> x8, Pallas kernels: 54.5 us -> 81.2 us  [the longest x4 52.8 us: front(): pl.pallas_call(functools.partial(body, layer, dim), grid=(FFN_STEPS,), in...]
    ppermute x28 -> x16, starting transfers between devices: 29.8 us -> 13.4 us  [swap(): return lax.ppermute(t, axis, [(i, i ^ relation) for i in range(n_sp)])]
    ppermute x28 -> x16, waiting for transfers between devices: 92.8 us -> 78.3 us  [swap(): return lax.ppermute(t, axis, [(i, i ^ relation) for i in range(n_sp)])]
    cond x36 -> x12, local copies, waits for them, and re-layouts: 4.04 us -> 1.64 us
    squeeze x3 -> x4, local copies, waits for them, and re-layouts: 6.49 us -> 7.16 us  [block(): lax.dynamic_slice(t, (layer, jnp.bitwise_xor(me, relation), 0, 0, 0), (1,...]
  transfers between devices with their start and end apart: 28 -> 16, of which waited for: 15 -> 5; matrix products, arithmetic and copies ran while one was open for 4% -> 4% of each run, Pallas kernels for 34% -> 44%
where the time goes in v1:
time: 229 us; the launch traced here: 228 us
  Pallas kernels  116 us (51%)
  waiting for transfers between devices  78.3 us (34%)
  starting transfers between devices  13.4 us (6%)
  local copies, waits for them, and re-layouts  10.2 us (4%)
  blocking collectives  4.89 us (2%)
  between operations  3.31 us (1%)
    ppermute x16, waiting for transfers between devices, swap(): return lax.ppermute(t, axis, [(i, i ^ relation) for i in range(n_sp)])  78.3 us
    pallas_call x4, Pallas kernels, front(): pl.pallas_call(functools.partial(body, layer, dim), grid=(FFN_STEPS,), in...  52.8 us
    pallas_call x4, Pallas kernels, tp_sum(): pl.pallas_call(tp_sum_body, in_specs=[VMEM, VMEM], out_specs=VMEM, out_sh...  28.4 us
    pallas_call x3, Pallas kernels, attend_window(): pl.pallas_call(functools.partial(window_body, layer, size, half, n_pipe),...  18.1 us
    ppermute x16, starting transfers between devices, swap(): return lax.ppermute(t, axis, [(i, i ^ relation) for i in range(n_sp)])  13.4 us
    squeeze x4, local copies, waits for them, and re-layouts, block(): lax.dynamic_slice(t, (layer, jnp.bitwise_xor(me, relation), 0, 0, 0), (1,...  7.16 us
    pallas_call x1, Pallas kernels, attend_global(): pl.pallas_call(functools.partial(values_body, layer), in_specs=[SMEM, VME...  6.01 us
    pallas_call x2, Pallas kernels, pack(): pl.pallas_call(functools.partial(pack_body, layer, size, half), in_specs=...  5.8 us
  transfers between devices with their start and end apart: 16, of which 5 were waited for; matrix products, arithmetic and copies ran while one was open for 4% of the time, Pallas kernels for 44%

profile of v1, /device:TPU:0, one launch (start us, length us, event | category | flops | bytes accessed | tf_op | source)
XLA Modules:
  0.0 227.6 jit_solution(14671897222894636617)
XLA Ops:
  0.7 0.6 collective-permute-start.42
  1.2 0.1 collective-permute-start.43
  1.3 1.1 dynamic-slice_bitcast_fusion.20
  2.4 3.0 %collective-permute-start.46 = (bf16[2,64,2048]{2,1,0:T(8,128)(2,1)S(1)}, bf16[2,64,2048]{2,1,0:T(8,128)(2,1)}, u32[]{:S(2)}, u32[]{:S(2)}) collective-permute-start(bf16[2,64,2048]{2,1,0:T(8,128)(2,1)S(1)} %dynamic-slice_bitcast_fusion.20), channel_id=1, source_target_pairs={{0,2},{1,3},{2,0},{3,1},{4,6},{5,7},{6,4},{7,5},{8,10},{9,11},{10,... | collective-permute-start | bytes 1572872 | tf_op jit(solution)/shard_map/ppermute | solution.py:474
  5.4 1.3 dynamic-slice_bitcast_fusion.21
  6.7 1.4 collective-permute-start.44
  8.2 0.1 reshape.42
  8.2 0.1 reduce_sum.9
  8.4 0.6 fusion
  9.0 4.9 %pmax.7 = s32[]{:T(128)} all-reduce(s32[]{:T(128)} %fusion), channel_id=1, replica_groups=mesh['dp'=2,'tp'=4,'sp'=4] {'dp'}, use_global_device_ids=true, to_apply=%region_2.3 | all-reduce | flops 1 | bytes 8 | tf_op jit(solution)/shard_map/pmax | solution.py:492
  13.9 0.6 dynamic_slice.72
  17.1 0.1 tile.21.sine
  17.2 0.1 tile.9.cosine
  17.3 12.7 %front.25 = (f32[4,2,64]{2,1,0:T(2,128)S(1)}, f32[2,2,64]{2,1,0:T(2,128)S(1)}, f32[1,2048]{1,0:T(1,128)S(1)}) custom-call(bf16[1,2048]{1,0:T(2,128)(2,1)S(1)} %copy-done.11, bf16[4,2048]{1,0:T(4,128)(2,1)S(1)} %copy-done.4, f32[1,128]{1,0:T(1,128)S(1)} %tile.9.cosine, f32[1,128]{1,0:T(1,128)S(1)} %tile.21.sine, bf16[4,2048,512]{2,1,0:T(8,128)(2,1)} %wq.1, ...), custom_call_target="tpu_custom_call" | custom-call | flops 28311552 | bytes 28311552 | tf_op jit(solution)/shard_map/front/pallas_call | solution.py:436
  30.1 0.1 pad_add_fusion
  30.2 10.0 %collective-permute-done.44 = bf16[2,64,2048]{2,1,0:T(8,128)(2,1)} collective-permute-done((bf16[2,64,2048]{2,1,0:T(8,128)(2,1)S(1)}, bf16[2,64,2048]{2,1,0:T(8,128)(2,1)}, u32[]{:S(2)}, u32[]{:S(2)}) %collective-permute-start.44) | collective-permute-done | bytes 524320 | tf_op jit(solution)/shard_map/ppermute | solution.py:474
  40.1 186.8 %conditional.1 = (bf16[1,2048]{1,0:T(2,128)(2,1)S(1)}, bf16[3,2,64,4096]{3,2,1,0:T(8,128)(2,1)}, bf16[3,2,64,4096]{3,2,1,0:T(8,128)(2,1)}, bf16[2,64,8192]{2,1,0:T(8,128)(2,1)}, bf16[2,64,8192]{2,1,0:T(8,128)(2,1)}) conditional(s32[]{:T(128)} %clamp.3, (s32[]{:T(128)}, bf16[4,4,2,64,2048]{4,3,2,1,0:T(8,128)(2,1)}, ...), branch_computations={%region_3.4_spmd, %region_4.5_spmd, %region_5.6_spmd, %region_6.7_... | conditional | flops 114393096 | bytes 172065408 | solution.py:533
  40.1 2.9 %pack.8 = (bf16[2,2,64,2048]{3,2,1,0:T(8,128)(2,1)}, bf16[2,2,64,256]{3,2,1,0:T(8,128)(2,1)}) custom-call(s32[5]{0:T(128)S(1)} %get-tuple-element.184.ids, bf16[4,4,2,64,2048]{4,3,2,1,0:T(8,128)(2,1)} %get-tuple-element.189.k_own.own, bf16[4,4,2,64,2048]{4,3,2,1,0:T(8,128)(2,1)} %get-tuple-element.190.v_own.own, ...), custom_call_target="tpu_custom_call" | custom-call | flops 2359296 | bytes 2359296 | tf_op jit(solution)/shard_map/cond/branch_0_fun/pack/pallas_call | solution.py:89
  43.0 1.8 collective-permute-start.1
  44.8 2.5 %dynamic-slice_bitcast_fusion = (bf16[2,64,2048]{2,1,0:T(8,128)(2,1)}, bf16[2,64,2048]{2,1,0:T(8,128)(2,1)}, bf16[2,64,2048]{2,1,0:T(8,128)(2,1)}) fusion(bf16[4,4,2,64,2048]{4,3,2,1,0:T(8,128)(2,1)} %get-tuple-element.190.v_own.own, s32[]{:T(128)S(6)} %select_n.38, s32[]{:T(128)S(6)} %select_n.39), kind=kLoop, calls=%fused_computation | loop fusion | bytes 3145736 | tf_op jit(solution)/shard_map/cond/branch_0_fun/squeeze | solution.py:496
  47.4 30.8 %collective-permute-done.refs_3_ = bf16[2,64,2048]{2,1,0:T(8,128)(2,1)} collective-permute-done((bf16[2,64,2048]{2,1,0:T(8,128)(2,1)}, bf16[2,64,2048]{2,1,0:T(8,128)(2,1)}, u32[]{:S(2)}, u32[]{:S(2)}) %collective-permute-start) | collective-permute-done | bytes 524320 | tf_op jit(solution)/shard_map/cond/branch_0_fun/ppermute | solution.py:474
  78.2 5.6 %attend_window.12 = (f32[1,2048]{1,0:T(1,128)}, bf16[3,2,64,4096]{3,2,1,0:T(8,128)(2,1)S(1)}, bf16[3,2,64,4096]{3,2,1,0:T(8,128)(2,1)}) custom-call(s32[5]{0:T(128)S(1)} %get-tuple-element.184.ids, f32[4,2,64]{2,1,0:T(2,128)S(1)} %get-tuple-element.185.q_ref, ...), custom_call_target="tpu_custom_call", output_to_operand_aliasing={{1}: (13, {}), {2}: (14, {})} | custom-call | flops 4194304 | bytes 4194304 | tf_op jit(solution)/shard_map/cond/branch_0_fun/attend_window/pallas_call | solution.py:248
  83.8 7.5 %tp_sum.16.h_ref = bf16[1,2048]{1,0:T(2,128)(2,1)} custom-call(f32[1,2048]{1,0:T(1,128)} %get-tuple-element.199.part_ref, bf16[1,2048]{1,0:T(2,128)(2,1)S(1)} %get-tuple-element.200.h_ref), custom_call_target="tpu_custom_call" | custom-call | flops 24576 | bytes 24576 | tf_op jit(solution)/shard_map/cond/branch_0_fun/tp_sum/pallas_call | solution.py:355
  91.3 13.4 %front.13 = (f32[4,2,64]{2,1,0:T(2,128)}, f32[2,2,64]{2,1,0:T(2,128)}, f32[1,2048]{1,0:T(1,128)}) custom-call(bf16[1,2048]{1,0:T(2,128)(2,1)} %tp_sum.16.h_ref, bf16[4,2048]{1,0:T(4,128)(2,1)S(1)} %get-tuple-element.201.gain, f32[1,128]{1,0:T(1,128)S(1)} %get-tuple-element.202.cosine, f32[1,128]{1,0:T(1,128)S(1)} %get-tuple-element.203.sine, ...), custom_call_target="tpu_custom_call" | custom-call | flops 28311552 | bytes 28311552 | tf_op jit(solution)/shard_map/cond/branch_0_fun/front/pallas_call | solution.py:436
  104.8 2.9 %pack.9 = (bf16[2,2,64,2048]{3,2,1,0:T(8,128)(2,1)}, bf16[2,2,64,256]{3,2,1,0:T(8,128)(2,1)}) custom-call(s32[5]{0:T(128)S(1)} %get-tuple-element.184.ids, bf16[4,4,2,64,2048]{4,3,2,1,0:T(8,128)(2,1)} %get-tuple-element.189.k_own.own, bf16[4,4,2,64,2048]{4,3,2,1,0:T(8,128)(2,1)} %get-tuple-element.190.v_own.own, ...), custom_call_target="tpu_custom_call" | custom-call | flops 2359296 | bytes 2359296 | tf_op jit(solution)/shard_map/cond/branch_0_fun/pack/pallas_call | solution.py:89
  107.7 1.1 collective-permute-start.4
  108.8 1.0 collective-permute-start.2
  109.8 26.5 %collective-permute-done.2.refs_1_ = bf16[2,2,64,256]{3,2,1,0:T(8,128)(2,1)S(1)} collective-permute-done((bf16[2,2,64,256]{3,2,1,0:T(8,128)(2,1)S(1)}, bf16[2,2,64,256]{3,2,1,0:T(8,128)(2,1)S(1)}, u32[]{:S(2)}, u32[]{:S(2)}) %collective-permute-start.2) | collective-permute-done | bytes 131104 | tf_op jit(solution)/shard_map/cond/branch_0_fun/ppermute | solution.py:474
  136.3 0.7 copy-done.13
  137.0 6.2 %attend_window.13 = (f32[1,2048]{1,0:T(1,128)}, bf16[3,2,64,4096]{3,2,1,0:T(8,128)(2,1)S(1)}, bf16[3,2,64,4096]{3,2,1,0:T(8,128)(2,1)}) custom-call(s32[5]{0:T(128)S(1)} %get-tuple-element.184.ids, f32[4,2,64]{2,1,0:T(2,128)} %get-tuple-element.210.q_ref, f32[2,2,64]{2,1,0:T(2,128)} %get-tuple-element.211.new_ref, ...), custom_call_target="tpu_custom_call", output_to_operand_aliasing={{1}: (12, {}), {2}: (13, {})} | custom-call | flops 4194304 | bytes 4194304 | tf_op jit(solution)/shard_map/cond/branch_0_fun/attend_window/pallas_call | solution.py:248
  143.2 7.1 %tp_sum.17.h_ref = bf16[1,2048]{1,0:T(2,128)(2,1)} custom-call(f32[1,2048]{1,0:T(1,128)} %get-tuple-element.218.part_ref, bf16[1,2048]{1,0:T(2,128)(2,1)} %tp_sum.16.h_ref), custom_call_target="tpu_custom_call" | custom-call | flops 24576 | bytes 24576 | tf_op jit(solution)/shard_map/cond/branch_0_fun/tp_sum/pallas_call | solution.py:355
  150.3 13.4 %front.14 = (f32[4,2,64]{2,1,0:T(2,128)}, f32[2,2,64]{2,1,0:T(2,128)}, f32[1,2048]{1,0:T(1,128)}) custom-call(bf16[1,2048]{1,0:T(2,128)(2,1)} %tp_sum.17.h_ref, bf16[4,2048]{1,0:T(4,128)(2,1)S(1)} %get-tuple-element.201.gain, f32[1,128]{1,0:T(1,128)S(1)} %get-tuple-element.202.cosine, f32[1,128]{1,0:T(1,128)S(1)} %get-tuple-element.203.sine, ...), custom_call_target="tpu_custom_call" | custom-call | flops 28311552 | bytes 28311552 | tf_op jit(solution)/shard_map/cond/branch_0_fun/front/pallas_call | solution.py:436
  163.8 0.7 collective-permute-start.5
  164.6 2.3 dynamic-slice_bitcast_fusion.2
  166.9 1.4 collective-permute-start.7
  168.2 0.1 collective-permute-start.8
  168.3 1.4 collective-permute-start.9
  169.7 0.6 collective-permute-start.10
  170.4 1.0 copy-done.5
  171.3 6.2 %attend_window.14 = (f32[1,2048]{1,0:T(1,128)}, bf16[3,2,64,4096]{3,2,1,0:T(8,128)(2,1)S(1)}, bf16[3,2,64,4096]{3,2,1,0:T(8,128)(2,1)}) custom-call(s32[5]{0:T(128)S(1)} %get-tuple-element.184.ids, f32[4,2,64]{2,1,0:T(2,128)} %get-tuple-element.219.q_ref, f32[2,2,64]{2,1,0:T(2,128)} %get-tuple-element.220.new_ref, ...), custom_call_target="tpu_custom_call", output_to_operand_aliasing={{1}: (12, {}), {2}: (13, {})} | custom-call | flops 4194304 | bytes 4194304 | tf_op jit(solution)/shard_map/cond/branch_0_fun/attend_window/pallas_call | solution.py:248
  177.6 7.1 %tp_sum.18.h_ref = bf16[1,2048]{1,0:T(2,128)(2,1)} custom-call(f32[1,2048]{1,0:T(1,128)} %get-tuple-element.227.part_ref, bf16[1,2048]{1,0:T(2,128)(2,1)} %tp_sum.17.h_ref), custom_call_target="tpu_custom_call" | custom-call | flops 24576 | bytes 24576 | tf_op jit(solution)/shard_map/cond/branch_0_fun/tp_sum/pallas_call | solution.py:355
  184.7 13.2 %front.15 = (f32[4,2,64]{2,1,0:T(2,128)}, f32[2,2,64]{2,1,0:T(2,128)}, f32[1,2048]{1,0:T(1,128)}) custom-call(bf16[1,2048]{1,0:T(2,128)(2,1)} %tp_sum.18.h_ref, bf16[4,2048]{1,0:T(4,128)(2,1)S(1)} %get-tuple-element.201.gain, bf16[4,2048,512]{2,1,0:T(8,128)(2,1)} %get-tuple-element.204.wq.refs_0_, bf16[4,2048,128]{2,1,0:T(8,128)(2,1)} %get-tuple-element.205.wk.refs_1_, ...), custom_call_target="tpu_custom_call" | custom-call | flops 28311552 | bytes 28311552 | tf_op jit(solution)/shard_map/cond/branch_0_fun/front/pallas_call | solution.py:436
  198.0 5.1 %scores.4 = (bf16[8,8192]{1,0:T(8,128)(2,1)}, bf16[2,64,8192]{2,1,0:T(8,128)(2,1)}) custom-call(s32[5]{0:T(128)S(1)} %get-tuple-element.184.ids, f32[4,2,64]{2,1,0:T(2,128)} %get-tuple-element.228.q_ref, f32[2,2,64]{2,1,0:T(2,128)} %get-tuple-element.229.new_ref, bf16[4,4,2,64,2048]{4,3,2,1,0:T(8,128)(2,1)} %get-tuple-element.189.k_own.own, ...), custom_call_target="tpu_custom_call" | custom-call | flops 4194304 | bytes 4194304 | tf_op jit(solution)/shard_map/cond/branch_0_fun/scores/pallas_call | solution.py:308
  203.1 1.4 collective-permute-done.9.b2
  204.4 9.6 %collective-permute-done.10.b3 = bf16[2,64,2048]{2,1,0:T(8,128)(2,1)} collective-permute-done((bf16[2,64,2048]{2,1,0:T(8,128)(2,1)}, bf16[2,64,2048]{2,1,0:T(8,128)(2,1)}, u32[]{:S(2)}, u32[]{:S(2)}) %collective-permute-start.10) | collective-permute-done | bytes 524320 | tf_op jit(solution)/shard_map/cond/branch_0_fun/ppermute | solution.py:474
  214.0 6.0 %values.4 = (f32[1,2048]{1,0:T(1,128)}, bf16[2,64,8192]{2,1,0:T(8,128)(2,1)}) custom-call(s32[5]{0:T(128)S(1)} %get-tuple-element.184.ids, bf16[8,8192]{1,0:T(8,128)(2,1)} %get-tuple-element.232.w_ref, f32[2,2,64]{2,1,0:T(2,128)} %get-tuple-element.229.new_ref, f32[1,2048]{1,0:T(1,128)} %get-tuple-element.233.mlp_ref, ...), custom_call_target="tpu_custom_call" | custom-call | flops 4194304 | bytes 4194304 | tf_op jit(solution)/shard_map/cond/branch_0_fun/values/pallas_call | solution.py:317
  220.0 6.7 %tp_sum.19 = bf16[1,2048]{1,0:T(2,128)(2,1)S(1)} custom-call(f32[1,2048]{1,0:T(1,128)} %get-tuple-element.236.part_ref, bf16[1,2048]{1,0:T(2,128)(2,1)} %tp_sum.18.h_ref), custom_call_target="tpu_custom_call" | custom-call | flops 24576 | bytes 24576 | tf_op jit(solution)/shard_map/cond/branch_0_fun/tp_sum/pallas_call | solution.py:355
  227.0 0.6 copy.86
  (36 shorter events, 0.4 us)
Async XLA Ops:
  0.6 7.5 %copy-start.16 = (s32[4]{0:T(128)S(1)}, s32[4]{0:T(128)}, u32[]{:S(2)}) copy-start(s32[4]{0:T(128)} %param.18) | copy-start | bytes 52
  0.6 16.7 %copy-start.4 = (bf16[4,2048]{1,0:T(4,128)(2,1)S(1)}, bf16[4,2048]{1,0:T(4,128)(2,1)}, u32[]{:S(2)}) copy-start(bf16[4,2048]{1,0:T(4,128)(2,1)} %gain.1) | copy-start | bytes 49156
  0.7 16.7 %copy-start.11 = (bf16[1,2048]{1,0:T(2,128)(2,1)S(1)}, bf16[1,2048]{1,0:T(2,128)(2,1)}, u32[]{:S(2)}) copy-start(bf16[1,2048]{1,0:T(2,128)(2,1)} %h_ref.1) | copy-start | bytes 12292
  0.7 39.5 %collective-permute-start.42 = (bf16[4,4,2,64,2048]{4,3,2,1,0:T(8,128)(2,1)}, bf16[4,4,2,64,2048]{4,3,2,1,0:T(8,128)(2,1)}, u32[]{:S(2)}, u32[]{:S(2)}) collective-permute-start(bf16[4,4,2,64,2048]{4,3,2,1,0:T(8,128)(2,1)} %bitcast.73), channel_id=1, source_target_pairs={{0,1},{1,0},{2,3},{3,2},{4,5},{5,4},{6,7},{7,6},{8,9},{9,8},{10,11... | collective-permute-start | bytes 25165832 | tf_op jit(solution)/shard_map/ppermute | solution.py:474
  1.2 38.9 %collective-permute-start.43 = (bf16[4,4,2,64,2048]{4,3,2,1,0:T(8,128)(2,1)}, bf16[4,4,2,64,2048]{4,3,2,1,0:T(8,128)(2,1)}, u32[]{:S(2)}, u32[]{:S(2)}) collective-permute-start(bf16[4,4,2,64,2048]{4,3,2,1,0:T(8,128)(2,1)} %bitcast.68), channel_id=1, source_target_pairs={{0,1},{1,0},{2,3},{3,2},{4,5},{5,4},{6,7},{7,6},{8,9},{9,8},{10,11... | collective-permute-start | bytes 25165832 | tf_op jit(solution)/shard_map/ppermute | solution.py:474
  2.4 27.8 %collective-permute-start.46 = (bf16[2,64,2048]{2,1,0:T(8,128)(2,1)S(1)}, bf16[2,64,2048]{2,1,0:T(8,128)(2,1)}, u32[]{:S(2)}, u32[]{:S(2)}) collective-permute-start(bf16[2,64,2048]{2,1,0:T(8,128)(2,1)S(1)} %dynamic-slice_bitcast_fusion.20), channel_id=1, source_target_pairs={{0,2},{1,3},{2,0},{3,1},{4,6},{5,7},{6,4},{7,5},{8,10},{9,11},{10,... | collective-permute-start | bytes 1572872 | tf_op jit(solution)/shard_map/ppermute | solution.py:474
  6.6 23.5 %collective-permute-start.45 = (bf16[2,64,2048]{2,1,0:T(8,128)(2,1)S(1)}, bf16[2,64,2048]{2,1,0:T(8,128)(2,1)}, u32[]{:S(2)}, u32[]{:S(2)}) collective-permute-start(bf16[2,64,2048]{2,1,0:T(8,128)(2,1)S(1)} %get-tuple-element.451), channel_id=1, source_target_pairs={{0,3},{1,2},{2,1},{3,0},{4,7},{5,6},{6,5},{7,4},{8,11},{9,10},{10,... | collective-permute-start | bytes 1572872 | tf_op jit(solution)/shard_map/ppermute | solution.py:474
  6.7 33.4 %collective-permute-start.44 = (bf16[2,64,2048]{2,1,0:T(8,128)(2,1)S(1)}, bf16[2,64,2048]{2,1,0:T(8,128)(2,1)}, u32[]{:S(2)}, u32[]{:S(2)}) collective-permute-start(bf16[2,64,2048]{2,1,0:T(8,128)(2,1)S(1)} %get-tuple-element.452), channel_id=1, source_target_pairs={{0,2},{1,3},{2,0},{3,1},{4,6},{5,7},{6,4},{7,5},{8,10},{9,11},{10,... | collective-permute-start | bytes 1572872 | tf_op jit(solution)/shard_map/ppermute | solution.py:474
  43.0 61.6 %collective-permute-start.1 = (bf16[2,2,64,2048]{3,2,1,0:T(8,128)(2,1)}, bf16[2,2,64,2048]{3,2,1,0:T(8,128)(2,1)}, u32[]{:S(2)}, u32[]{:S(2)}) collective-permute-start(bf16[2,2,64,2048]{3,2,1,0:T(8,128)(2,1)} %get-tuple-element.213), channel_id=1, source_target_pairs={{0,2},{1,3},{2,0},{3,1},{4,6},{5,7},{6,4},{7,5},{8,10},{9,11},{10,... | collective-permute-start | bytes 3145736 | tf_op jit(solution)/shard_map/cond/branch_0_fun/ppermute | solution.py:474
  47.4 30.8 %collective-permute-start = (bf16[2,64,2048]{2,1,0:T(8,128)(2,1)}, bf16[2,64,2048]{2,1,0:T(8,128)(2,1)}, u32[]{:S(2)}, u32[]{:S(2)}) collective-permute-start(bf16[2,64,2048]{2,1,0:T(8,128)(2,1)} %get-tuple-element.433), channel_id=1, source_target_pairs={{0,3},{1,2},{2,1},{3,0},{4,7},{5,6},{6,5},{7,4},{8,11},{9,10},{10,... | collective-permute-start | bytes 1572872 | tf_op jit(solution)/shard_map/cond/branch_0_fun/ppermute | solution.py:474
  104.7 4.1 %copy-start.14 = (bf16[2,2,64,256]{3,2,1,0:T(8,128)(2,1)S(1)}, bf16[2,2,64,256]{3,2,1,0:T(8,128)(2,1)}, u32[]{:S(2)}) copy-start(bf16[2,2,64,256]{3,2,1,0:T(8,128)(2,1)} %get-tuple-element.214) | copy-start | bytes 393220 | tf_op jit(solution)/shard_map/cond
  104.7 31.6 %collective-permute-start.3 = (bf16[2,2,64,2048]{3,2,1,0:T(8,128)(2,1)}, bf16[2,2,64,2048]{3,2,1,0:T(8,128)(2,1)}, u32[]{:S(2)}, u32[]{:S(2)}) collective-permute-start(bf16[2,2,64,2048]{3,2,1,0:T(8,128)(2,1)} %collective-permute-done.1.refs_0_), channel_id=1, source_target_pairs={{0,1},{1,0},{2,3},{3,2},{4,5},{5,4},{6,7},{7,6},{8,9},{9,8},{10,11... | collective-permute-start | bytes 3145736 | tf_op jit(solution)/shard_map/cond/branch_0_fun/ppermute | solution.py:474
  107.7 56.1 %collective-permute-start.4 = (bf16[2,2,64,2048]{3,2,1,0:T(8,128)(2,1)}, bf16[2,2,64,2048]{3,2,1,0:T(8,128)(2,1)}, u32[]{:S(2)}, u32[]{:S(2)}) collective-permute-start(bf16[2,2,64,2048]{3,2,1,0:T(8,128)(2,1)} %get-tuple-element.222), channel_id=1, source_target_pairs={{0,2},{1,3},{2,0},{3,1},{4,6},{5,7},{6,4},{7,5},{8,10},{9,11},{10,... | collective-permute-start | bytes 3145736 | tf_op jit(solution)/shard_map/cond/branch_0_fun/ppermute | solution.py:474
  108.8 27.5 %collective-permute-start.2 = (bf16[2,2,64,256]{3,2,1,0:T(8,128)(2,1)S(1)}, bf16[2,2,64,256]{3,2,1,0:T(8,128)(2,1)S(1)}, u32[]{:S(2)}, u32[]{:S(2)}) collective-permute-start(bf16[2,2,64,256]{3,2,1,0:T(8,128)(2,1)S(1)} %copy-done.14), channel_id=1, source_target_pairs={{0,2},{1,3},{2,0},{3,1},{4,6},{5,7},{6,4},{7,5},{8,10},{9,11},{10,... | collective-permute-start | bytes 393224 | tf_op jit(solution)/shard_map/cond/branch_0_fun/ppermute | solution.py:474
  136.3 0.7 copy-start.13
  150.3 13.5 %copy-start.15 = (bf16[2,2,64,256]{3,2,1,0:T(8,128)(2,1)S(1)}, bf16[2,2,64,256]{3,2,1,0:T(8,128)(2,1)}, u32[]{:S(2)}) copy-start(bf16[2,2,64,256]{3,2,1,0:T(8,128)(2,1)} %get-tuple-element.223) | copy-start | bytes 393220 | tf_op jit(solution)/shard_map/cond
  163.8 6.6 %collective-permute-start.6 = (bf16[2,2,64,2048]{3,2,1,0:T(8,128)(2,1)}, bf16[2,2,64,2048]{3,2,1,0:T(8,128)(2,1)S(1)}, u32[]{:S(2)}, u32[]{:S(2)}) collective-permute-start(bf16[2,2,64,2048]{3,2,1,0:T(8,128)(2,1)} %collective-permute-done.4.refs_0_), channel_id=1, source_target_pairs={{0,1},{1,0},{2,3},{3,2},{4,5},{5,4},{6,7},{7,6},{8,9},{9,8},{10,11... | collective-permute-start | bytes 3145736 | tf_op jit(solution)/shard_map/cond/branch_0_fun/ppermute | solution.py:474
  163.8 5.9 %collective-permute-start.5 = (bf16[2,2,64,256]{3,2,1,0:T(8,128)(2,1)S(1)}, bf16[2,2,64,256]{3,2,1,0:T(8,128)(2,1)S(1)}, u32[]{:S(2)}, u32[]{:S(2)}) collective-permute-start(bf16[2,2,64,256]{3,2,1,0:T(8,128)(2,1)S(1)} %copy-done.15), channel_id=1, source_target_pairs={{0,2},{1,3},{2,0},{3,1},{4,6},{5,7},{6,4},{7,5},{8,10},{9,11},{10,... | collective-permute-start | bytes 393224 | tf_op jit(solution)/shard_map/cond/branch_0_fun/ppermute | solution.py:474
  166.9 31.1 %collective-permute-start.7 = (bf16[2,64,2048]{2,1,0:T(8,128)(2,1)}, bf16[2,64,2048]{2,1,0:T(8,128)(2,1)}, u32[]{:S(2)}, u32[]{:S(2)}) collective-permute-start(bf16[2,64,2048]{2,1,0:T(8,128)(2,1)} %get-tuple-element.230), channel_id=1, source_target_pairs={{0,2},{1,3},{2,0},{3,1},{4,6},{5,7},{6,4},{7,5},{8,10},{9,11},{10,... | collective-permute-start | bytes 1572872 | tf_op jit(solution)/shard_map/cond/branch_0_fun/ppermute | solution.py:474
  168.2 29.7 %collective-permute-start.8 = (bf16[2,64,2048]{2,1,0:T(8,128)(2,1)}, bf16[2,64,2048]{2,1,0:T(8,128)(2,1)}, u32[]{:S(2)}, u32[]{:S(2)}) collective-permute-start(bf16[2,64,2048]{2,1,0:T(8,128)(2,1)} %get-tuple-element.231), channel_id=1, source_target_pairs={{0,3},{1,2},{2,1},{3,0},{4,7},{5,6},{6,5},{7,4},{8,11},{9,10},{10,... | collective-permute-start | bytes 1572872 | tf_op jit(solution)/shard_map/cond/branch_0_fun/ppermute | solution.py:474
  168.3 36.1 %collective-permute-start.9 = (bf16[2,64,2048]{2,1,0:T(8,128)(2,1)}, bf16[2,64,2048]{2,1,0:T(8,128)(2,1)}, u32[]{:S(2)}, u32[]{:S(2)}) collective-permute-start(bf16[2,64,2048]{2,1,0:T(8,128)(2,1)} %get-tuple-element.234), channel_id=1, source_target_pairs={{0,2},{1,3},{2,0},{3,1},{4,6},{5,7},{6,4},{7,5},{8,10},{9,11},{10,... | collective-permute-start | bytes 1572872 | tf_op jit(solution)/shard_map/cond/branch_0_fun/ppermute | solution.py:474
  169.7 1.6 copy-start.12
  169.7 44.3 %collective-permute-start.10 = (bf16[2,64,2048]{2,1,0:T(8,128)(2,1)}, bf16[2,64,2048]{2,1,0:T(8,128)(2,1)}, u32[]{:S(2)}, u32[]{:S(2)}) collective-permute-start(bf16[2,64,2048]{2,1,0:T(8,128)(2,1)} %get-tuple-element.235), channel_id=1, source_target_pairs={{0,3},{1,2},{2,1},{3,0},{4,7},{5,6},{6,5},{7,4},{8,11},{9,10},{10,... | collective-permute-start | bytes 1572872 | tf_op jit(solution)/shard_map/cond/branch_0_fun/ppermute | solution.py:474
  170.4 1.0 copy-start.5
  177.6 20.4 %copy-start = (bf16[3,2,64,4096]{3,2,1,0:T(8,128)(2,1)}, bf16[3,2,64,4096]{3,2,1,0:T(8,128)(2,1)S(1)}, u32[]{:S(2)}) copy-start(bf16[3,2,64,4096]{3,2,1,0:T(8,128)(2,1)S(1)} %get-tuple-element.456) | copy-start | bytes 9437188 | tf_op jit(solution)/shard_map/cond

commit v2 on v1

--- a/solution.py
+++ b/solution.py
@@ -14,6 +14,7 @@
 UNIT = 128
 SIZES = (18, 23, 28, 32)
 FFN_STEPS = 4
+PEERS = (1, 2, 3)
 CHUNK = 16
 HBM = pl.BlockSpec(memory_space=pltpu.HBM)
 VMEM = pl.BlockSpec(memory_space=pltpu.VMEM)
@@ -266,70 +267,173 @@
     )(ids, q, new_kv, mlp, w_out, k_t, v_t, *nears, *pipe, k_buf, v_buf)
 
 
-def fetch_row(layer, me, own, blocks, kv, sem):
-    shard = own.shape[-1]
-    for relation in range(4):
-        at = pl.ds(pl.multiple_of(jnp.bitwise_xor(me, relation) * shard, UNIT), shard)
-        src = (own, blocks[0])[relation].at[layer, me] if relation < 2 else blocks[relation - 1]
-        move([(src, kv.at[:, :, at], sem)])
-
-
-def scores_body(layer, ids, q_ref, new_ref, own, b1, b2, b3, w_ref, k_out, kv, sem, out_sem, scores):
+def place_body(layer, part, relations, ids, new_ref, own, near, *refs):
+    blocks = {1: near}
+    blocks.update(zip([r for r in relations if r > 1], refs))
+    out, kv, sems, out_sem = refs[-4:]
     me = ids[0]
     length = ids[1 + me]
-    fetch_row(layer, me, own, (b1, b2, b3), kv, sem)
-    pltpu.make_async_copy(kv, kv, sem).wait()
-    settle(kv, new_ref[0], length, jnp.zeros_like, (length // UNIT, kv.shape[-1] // UNIT))
-    w_ref[...] = softmax_weights(stacked(q_ref), kv, scores, length)
-    copy = pltpu.make_async_copy(kv, k_out, out_sem)
-    copy.start()
-    copy.wait()
-
-
-def values_body(layer, ids, w_ref, new_ref, mlp_ref, wo_hbm, own, b1, b2, b3, part_ref, v_out, kv, wo, sem, out_sem, wo_sem):
-    me = ids[0]
-    length = ids[1 + me]
-    fetch_row(layer, me, own, (b1, b2, b3), kv, sem)
-    wo_copy = pltpu.make_async_copy(wo_hbm.at[layer], wo, wo_sem)
-    wo_copy.start()
-    pltpu.make_async_copy(kv, kv, sem).wait()
-    settle(kv, new_ref[1], length, jnp.zeros_like, (length // UNIT, kv.shape[-1] // UNIT))
-    wo_copy.wait()
-    copy = pltpu.make_async_copy(kv, v_out, out_sem)
-    mix_and_project(w_ref, kv, copy, wo, mlp_ref, part_ref)
-    copy.wait()
-
-
-def attend_global(layer, ids, q, new_kv, mlp, w_out, k_t, v_t, k_blocks, v_blocks):
-    heads, dim, shard = k_t.shape[2:]
-    row = jax.ShapeDtypeStruct((heads, dim, 4 * shard), BF16)
-    scratch = [pltpu.VMEM(row.shape, BF16), pltpu.SemaphoreType.DMA, pltpu.SemaphoreType.DMA]
+    shard = own.shape[-1]
+    units = shard // UNIT
+    spans = {r: pl.ds(pl.multiple_of(jnp.bitwise_xor(me, r) * shard, UNIT), shard) for r in relations}
+    for i, r in enumerate(relations):
+        src = (own, near)[r].at[layer, me] if r < 2 else blocks[r]
+        move([(src, kv.at[:, :, spans[r]], sems.at[i])])
+    stores = []
+    for i, r in enumerate(relations):
+        view = kv.at[:, :, spans[r]]
+        pltpu.make_async_copy(view, view, sems.at[i]).wait()
+        first = jnp.bitwise_xor(me, r) * units
+        settle(kv, new_ref[part], length, jnp.zeros_like, (jnp.maximum(first, length // UNIT), first + units))
+        stores.append(pltpu.make_async_copy(view, out.at[:, :, spans[r]], out_sem))
+        stores[-1].start()
+    for store in stores:
+        store.wait()
+
+
+def place(layer, part, relations, ids, new_kv, own, near, blocks, buf):
+    heads, dim, shard = own.shape[2:]
+    n_in = 4 + len(blocks)
+    return pl.pallas_call(
+        functools.partial(place_body, layer, part, relations),
+        in_specs=[SMEM, VMEM] + [HBM] * (3 + len(blocks)),
+        out_specs=HBM,
+        out_shape=jax.ShapeDtypeStruct(buf.shape, BF16),
+        scratch_shapes=[pltpu.VMEM(buf.shape, BF16), pltpu.SemaphoreType.DMA((len(relations),)), pltpu.SemaphoreType.DMA],
+        input_output_aliases={n_in: 0},
+        cost_estimate=cost(4 * heads * dim * shard * len(relations)),
+        name="place",
+    )(ids, new_kv, own, near, *blocks, buf)
+
+
+def spread_body(layer, ids, q_ref, new_ref, mlp_ref, h_ref, wo_hbm, k_own, v_own, out_ref, k_all, v_all, wo, q_all, stats, mixes, part_ref, slots, expd, sems, send_sems, recv_sems):
+    me = lax.axis_index("sp")
+    tp = lax.axis_index("tp")
+    barrier = pltpu.get_barrier_semaphore()
+    sp_peers = [{"sp": jnp.bitwise_xor(me, r)} for r in PEERS]
+    tp_peers = [{"tp": jnp.bitwise_xor(tp, r)} for r in PEERS]
+    for peer in sp_peers + tp_peers:
+        pl.semaphore_signal(barrier, inc=1, device_id=peer, device_id_type=pl.DeviceIdType.MESH)
+    loads = [pltpu.make_async_copy(k_own.at[layer], k_all, sems.at[0]), pltpu.make_async_copy(v_own.at[layer], v_all, sems.at[1]), pltpu.make_async_copy(wo_hbm.at[layer], wo, sems.at[2])]
+    for load in loads:
+        load.start()
+
+    def exchange(stage, peers, pairs):
+        copies = [
+            pltpu.make_async_remote_copy(src, dst, send_sems.at[stage, i], recv_sems.at[stage, i], device_id=peer, device_id_type=pl.DeviceIdType.MESH)
+            for i, (peer, (src, dst)) in enumerate(zip(peers, pairs))
+        ]
+        for copy in copies:
+            copy.start()
+        return copies
+
+    def done(copies):
+        for copy in copies:
+            copy.wait()
+
+    pl.semaphore_wait(barrier, 6)
+    queries = exchange(0, sp_peers, [(q_ref, q_all.at[i]) for i in range(3)])
+    n_q = q_ref.shape[0] * q_ref.shape[1]
+    dim = q_ref.shape[2]
+    shard = k_all.shape[-1]
+    upper = lax.broadcasted_iota(jnp.int32, (n_q, 1), 0) < n_q // 2
+    lane = lax.broadcasted_iota(jnp.int32, (1, UNIT), 1)
+    position = lax.broadcasted_iota(jnp.int32, (1, shard), 1) + me * shard
+    q_own = jnp.concatenate([q_ref[j] for j in range(q_ref.shape[0])], axis=0)
+    new_k = jnp.where(upper, new_ref[0, 0:1], new_ref[0, 1:2])
+    new_v = jnp.where(upper, new_ref[1, 0:1], new_ref[1, 1:2])
+    new_score = (q_own * new_k).sum(axis=-1, keepdims=True) * (dim ** -0.5)
+
+    def score(r):
+        row = jnp.bitwise_xor(me, r)
+        q = q_own if r == 0 else jnp.concatenate([q_all[r - 1, j] for j in range(q_ref.shape[0])], axis=0)
+        q = q.astype(BF16)
+        s0 = jnp.dot(q, k_all[row, 0], preferred_element_type=F32)
+        s1 = jnp.dot(q, k_all[row, 1], preferred_element_type=F32)
+        scores = jnp.where(position < ids[1 + row], jnp.where(upper, s0, s1) * (dim ** -0.5), -1e30)
+        top = scores.max(axis=-1, keepdims=True)
+        e = jnp.exp(scores - top)
+        expd[r] = e
+        stats[0, r] = jnp.where(lane == 0, top, jnp.where(lane == 1, e.sum(axis=-1, keepdims=True), new_score))
+
+    loads[0].wait()
+    score(0)
+    done(queries)
+    for r in PEERS:
+        score(r)
+    done(exchange(1, sp_peers, [(stats.at[0], stats.at[r]) for r in PEERS]))
+    loads[1].wait()
+    dims = (((1,), (1,)), ((), ()))
+    for r in (1, 2, 3, 0):
+        row = jnp.bitwise_xor(me, r)
+        seen = [stats[other, other ^ r] for other in range(4)]
+        fresh = stats[r, 0][:, 2:3]
+        top = fresh
+        for one in seen:
+            top = jnp.maximum(top, one[:, 0:1])
+        total = jnp.exp(fresh - top)
+        for one in seen:
+            total = total + one[:, 1:2] * jnp.exp(one[:, 0:1] - top)
+        weights = (expd[r] * (jnp.exp(stats[0, r][:, 0:1] - top) / total)).astype(BF16)
+        m0 = lax.dot_general(weights, v_all[row, 0], dims, preferred_element_type=F32)
+        m1 = lax.dot_general(weights, v_all[row, 1], dims, preferred_element_type=F32)
+        mixed = jnp.where(upper, m0, m1)
+        if r == 0:
+            mixed = mixed + (jnp.exp(fresh - top) / total).astype(BF16).astype(F32) * new_v
+        mixes[0, r] = mixed
+    done(exchange(2, sp_peers, [(mixes.at[0, r], mixes.at[1, r]) for r in PEERS]))
+    mixed = mixes[0, 0] + mixes[1, 1] + mixes[1, 2] + mixes[1, 3]
+    mixed = mixed.astype(BF16).astype(F32)
+    flat = jnp.concatenate([mixed[j:j + 1] for j in range(n_q)], axis=1)
+    flat = jnp.broadcast_to(flat, (8, flat.shape[1])).astype(BF16)
+    loads[2].wait()
+    part_ref[...] = jnp.dot(flat, wo[...], preferred_element_type=F32)[0:1] + mlp_ref[...]
+    done(exchange(3, tp_peers, [(part_ref, slots.at[i]) for i in range(3)]))
+    out_ref[...] = in_tp_order(tp, [part_ref[...]] + [slots[i] for i in range(3)], h_ref[...])
+
+
+def spread(layer, ids, q, new_kv, mlp, residual, w_out, k_t, v_t):
+    rows, heads, dim, shard = k_t.shape[1:]
     n_q = q.shape[0] * q.shape[1]
-    weights, k_glob = pl.pallas_call(
-        functools.partial(scores_body, layer),
-        in_specs=[SMEM, VMEM, VMEM] + [HBM] * 4,
-        out_specs=[VMEM, HBM],
-        out_shape=[jax.ShapeDtypeStruct((n_q, 4 * shard), BF16), row],
-        scratch_shapes=scratch + [pltpu.VMEM((n_q, 4 * shard), F32)],
+    return pl.pallas_call(
+        functools.partial(spread_body, layer),
+        in_specs=[SMEM, VMEM, VMEM, VMEM, VMEM, HBM, HBM, HBM],
+        out_specs=VMEM,
+        out_shape=jax.ShapeDtypeStruct(residual.shape, BF16),
+        scratch_shapes=[
+            pltpu.VMEM((rows, heads, dim, shard), BF16),
+            pltpu.VMEM((rows, heads, dim, shard), BF16),
+            pltpu.VMEM(w_out.shape[1:], BF16),
+            pltpu.VMEM((3,) + q.shape, F32),
+            pltpu.VMEM((4, 4, n_q, UNIT), F32),
+            pltpu.VMEM((2, 4, n_q, dim), F32),
+            pltpu.VMEM(mlp.shape, F32),
+            pltpu.VMEM((3,) + mlp.shape, F32),
+            pltpu.VMEM((4, n_q, shard), F32),
+            pltpu.SemaphoreType.DMA((3,)),
+            pltpu.SemaphoreType.DMA((4, 3)),
+            pltpu.SemaphoreType.DMA((4, 3)),
+        ],
+        compiler_params=pltpu.CompilerParams(collective_id=layer, has_side_effects=True),
         cost_estimate=cost(16 * heads * dim * shard),
-        name="scores",
-    )(ids, q, new_kv, k_t, *k_blocks)
-    part, v_glob = pl.pallas_call(
-        functools.partial(values_body, layer),
-        in_specs=[SMEM, VMEM, VMEM, VMEM] + [HBM] * 5,
-        out_specs=[VMEM, HBM],
-        out_shape=[jax.ShapeDtypeStruct(mlp.shape, F32), row],
-        scratch_shapes=scratch[:1] + [pltpu.VMEM(w_out.shape[1:], BF16)] + [pltpu.SemaphoreType.DMA] * 3,
-        cost_estimate=cost(16 * heads * dim * shard),
-        name="values",
-    )(ids, weights, new_kv, mlp, w_out, v_t, *v_blocks)
-    return part, k_glob, v_glob
+        name="spread",
+    )(ids, q, new_kv, mlp, residual, w_out, k_t, v_t)
+
+
+def in_tp_order(tp, parts, residual):
+    for t in range(4):
+        at = jnp.bitwise_xor(tp, t)
+        pick = parts[3]
+        for r in range(3):
+            pick = jnp.where(at == r, parts[r], pick)
+        total = pick if t == 0 else total + pick
+    return (residual.astype(F32) + total).astype(BF16)
 
 
 def tp_sum_body(part_ref, h_ref, out_ref, slots, send_sems, recv_sems):
     tp = lax.axis_index("tp")
     barrier = pltpu.get_barrier_semaphore()
-    peers = [{"tp": jnp.bitwise_xor(tp, r)} for r in (1, 2, 3)]
+    peers = [{"tp": jnp.bitwise_xor(tp, r)} for r in PEERS]
     for peer in peers:
         pl.semaphore_signal(barrier, inc=1, device_id=peer, device_id_type=pl.DeviceIdType.MESH)
     pl.semaphore_wait(barrier, 3)
@@ -341,14 +445,7 @@
         copy.start()
     for copy in copies:
         copy.wait()
-    parts = [part_ref[...]] + [slots[i] for i in range(3)]
-    for t in range(4):
-        at = jnp.bitwise_xor(tp, t)
-        pick = parts[3]
-        for r in range(3):
-            pick = jnp.where(at == r, parts[r], pick)
-        total = pick if t == 0 else total + pick
-    out_ref[...] = (h_ref[...].astype(F32) + total).astype(BF16)
+    out_ref[...] = in_tp_order(tp, [part_ref[...]] + [slots[i] for i in range(3)], h_ref[...])
 
 
 def tp_sum(layer, part, residual):
@@ -498,15 +595,16 @@
         weights = (w_query, w_key, w_value, w_gate, w_up, w_down)
         k_first = [swap(block(k_t, 0, r), "sp", r) for r in (2, 3)]
         v_far = swap(block(v_t, 0, 2), "sp", 2)
+        v_cut = block(v_t, 0, 3)
         nears = [swap(k_t, "sp", 1), swap(v_t, "sp", 1)]
         begun = front(0, dim, hidden, ln_gain, turns, *weights)
 
         def run(size):
             return run_scoped(size)
 
-        def run_scoped(size):
+        def run_scoped(size, ids=ids):
             k_win, v_win = fresh_buffers([(final, heads, dim, WINDOW)] * 2)
-            pipes = [k_first + [v_far, swap(block(v_t, 0, 3), "sp", 3)]]
+            pipes = [k_first + [v_far, swap(v_cut, "sp", 3)]]
             for layer in range(1, final):
                 packed = pack(layer, size, ids, k_t, v_t, nears)
                 pipes.append([swap(p, "sp", 2) for p in packed])
@@ -522,9 +620,14 @@
                     if layer and size < 2 * half:
                         pipes[layer].append(swap(after(pipes[layer][0], q), "sp", 1))
                     part, k_win, v_win = attend_window(layer, size if layer else None, ids, q, new_kv, mlp, w_out, k_t, v_t, nears, pipes[layer], k_win, v_win)
+                    residual = tp_sum(layer, part, residual)
                 else:
-                    part, k_glob, v_glob = attend_global(layer, ids, q, new_kv, mlp, w_out, k_t, v_t, [nears[0]] + late[:2], [nears[1]] + late[2:])
-                residual = tp_sum(layer, part, residual)
+                    k_glob, v_glob = fresh_buffers([(heads, dim, n_sp * shard)] * 2)
+                    residual = spread(layer, ids, q, new_kv, mlp, residual, w_out, k_t, v_t)
+                    k_glob = place(final, 0, (0,) + PEERS, ids, new_kv, k_t, nears[0], late[:2], k_glob)
+                    ids = after(ids, k_glob)
+                    v_glob = place(final, 1, (0, 1, 2), ids, new_kv, v_t, nears[1], late[2:3], v_glob)
+                    v_glob = place(final, 1, (3,), ids, new_kv, v_t, nears[1], late[3:], v_glob)
             return residual, k_win, v_win, k_glob, v_glob
 
         if len(SIZES) == 1:

time: 229 us -> 234 us (1.022)
  Pallas kernels: 116 us -> 128 us
  waiting for transfers between devices: 78.3 us -> 73.3 us
    pallas_call x2 -> x4, Pallas kernels: 11.1 us -> 29.4 us  [the longest x1 20.3 us: spread(): pl.pallas_call(functools.partial(spread_body, layer), in_specs=[SMEM, VME...]
    pallas_call x4 -> x3, Pallas kernels: 28.4 us -> 21.7 us  [tp_sum(): pl.pallas_call(tp_sum_body, in_specs=[VMEM, VMEM], out_specs=VMEM, out_sh...]
    ppermute x16, waiting for transfers between devices: 78.3 us -> 73.3 us  [swap(): return lax.ppermute(t, axis, [(i, i ^ relation) for i in range(n_sp)])]
    squeeze x4 -> x3, local copies, waits for them, and re-layouts: 7.16 us -> 6.27 us  [block(): lax.dynamic_slice(t, (layer, jnp.bitwise_xor(me, relation), 0, 0, 0), (1,...]
  transfers between devices with their start and end apart: 16 -> 16, of which waited for: 5 -> 4; matrix products, arithmetic and copies ran while one was open for 4% -> 3% of each run, Pallas kernels for 44% -> 52%
where the time goes in v2:
time: 234 us; the launch traced here: 233 us
  Pallas kernels  128 us (55%)
  waiting for transfers between devices  73.3 us (31%)
  starting transfers between devices  13.3 us (6%)
  local copies, waits for them, and re-layouts  8.4 us (4%)
  blocking collectives  4.89 us (2%)
  between operations  3.32 us (1%)
    ppermute x16, waiting for transfers between devices, swap(): return lax.ppermute(t, axis, [(i, i ^ relation) for i in range(n_sp)])  73.3 us
    pallas_call x4, Pallas kernels, front(): pl.pallas_call(functools.partial(body, layer, dim), grid=(FFN_STEPS,), in...  52.8 us
    pallas_call x3, Pallas kernels, tp_sum(): pl.pallas_call(tp_sum_body, in_specs=[VMEM, VMEM], out_specs=VMEM, out_sh...  21.7 us
    pallas_call x1, Pallas kernels, spread(): pl.pallas_call(functools.partial(spread_body, layer), in_specs=[SMEM, VME...  20.3 us
    pallas_call x3, Pallas kernels, attend_window(): pl.pallas_call(functools.partial(window_body, layer, size, half, n_pipe),...  18.1 us
    ppermute x16, starting transfers between devices, swap(): return lax.ppermute(t, axis, [(i, i ^ relation) for i in range(n_sp)])  13.3 us
    pallas_call x3, Pallas kernels, place(): pl.pallas_call(functools.partial(place_body, layer, part, relations), in_...  9.09 us
    squeeze x3, local copies, waits for them, and re-layouts, block(): lax.dynamic_slice(t, (layer, jnp.bitwise_xor(me, relation), 0, 0, 0), (1,...  6.27 us
  transfers between devices with their start and end apart: 16, of which 4 were waited for; matrix products, arithmetic and copies ran while one was open for 3% of the time, Pallas kernels for 52%

profile of v2, /device:TPU:0, one launch (start us, length us, event | category | flops | bytes accessed | tf_op | source)
XLA Modules:
  0.0 232.5 jit_solution(10827716290019854195)
XLA Ops:
  0.7 0.6 collective-permute-start.42
  1.2 0.1 collective-permute-start.43
  1.3 1.3 dynamic-slice_bitcast_fusion.17
  2.6 3.0 %collective-permute-start.44 = (bf16[2,64,2048]{2,1,0:T(8,128)(2,1)S(1)}, bf16[2,64,2048]{2,1,0:T(8,128)(2,1)}, u32[]{:S(2)}, u32[]{:S(2)}) collective-permute-start(bf16[2,64,2048]{2,1,0:T(8,128)(2,1)S(1)} %get-tuple-element.466), channel_id=1, source_target_pairs={{0,2},{1,3},{2,0},{3,1},{4,6},{5,7},{6,4},{7,5},{8,10},{9,11},{10,... | collective-permute-start | bytes 1572872 | tf_op jit(solution)/shard_map/ppermute | solution.py:571
  5.6 2.1 dynamic-slice_bitcast_fusion.16
  7.7 1.4 collective-permute-start.46
  9.1 0.1 reshape.42
  9.2 0.1 reduce_sum.9
  9.3 0.6 fusion
  10.0 4.9 %pmax.7 = s32[]{:T(128)} all-reduce(s32[]{:T(128)} %fusion), channel_id=1, replica_groups=mesh['dp'=2,'tp'=4,'sp'=4] {'dp'}, use_global_device_ids=true, to_apply=%region_2.3 | all-reduce | flops 1 | bytes 8 | tf_op jit(solution)/shard_map/pmax | solution.py:589
  14.9 0.6 dynamic_slice.64
  16.2 0.1 tile.21.sine
  16.2 0.1 tile.9.cosine
  18.3 12.7 %front.25 = (f32[4,2,64]{2,1,0:T(2,128)S(1)}, f32[2,2,64]{2,1,0:T(2,128)S(1)}, f32[1,2048]{1,0:T(1,128)S(1)}) custom-call(bf16[1,2048]{1,0:T(2,128)(2,1)S(1)} %copy-done.7, bf16[4,2048]{1,0:T(4,128)(2,1)S(1)} %copy-done.4, f32[1,128]{1,0:T(1,128)S(1)} %tile.9.cosine, f32[1,128]{1,0:T(1,128)S(1)} %tile.21.sine, bf16[4,2048,512]{2,1,0:T(8,128)(2,1)} %wq.1, ...), custom_call_target="tpu_custom_call" | custom-call | flops 28311552 | bytes 28311552 | tf_op jit(solution)/shard_map/front/pallas_call | solution.py:533
  31.1 0.1 pad_add_fusion
  31.1 9.2 %collective-permute-done.46 = bf16[2,64,2048]{2,1,0:T(8,128)(2,1)} collective-permute-done((bf16[2,64,2048]{2,1,0:T(8,128)(2,1)S(1)}, bf16[2,64,2048]{2,1,0:T(8,128)(2,1)}, u32[]{:S(2)}, u32[]{:S(2)}) %collective-permute-start.46) | collective-permute-done | bytes 524320 | tf_op jit(solution)/shard_map/ppermute | solution.py:571
  40.3 191.6 %conditional.1 = (bf16[1,2048]{1,0:T(2,128)(2,1)S(1)}, bf16[3,2,64,4096]{3,2,1,0:T(8,128)(2,1)}, bf16[3,2,64,4096]{3,2,1,0:T(8,128)(2,1)}, bf16[2,64,8192]{2,1,0:T(8,128)(2,1)}, bf16[2,64,8192]{2,1,0:T(8,128)(2,1)}) conditional(s32[]{:T(128)} %clamp.3, (bf16[2,64,2048]{2,1,0:T(8,128)(2,1)}, s32[5]{0:T(128)S(1)}, ...), branch_computations={%region_3.4_spmd, %region_4.5_spmd, %region_5.6_spmd, %region_6.7_... | conditional | flops 118562816 | bytes 170992256 | solution.py:636
  40.3 2.9 %pack.8 = (bf16[2,2,64,2048]{3,2,1,0:T(8,128)(2,1)}, bf16[2,2,64,256]{3,2,1,0:T(8,128)(2,1)}) custom-call(s32[5]{0:T(128)S(1)} %get-tuple-element.245.ids, bf16[4,4,2,64,2048]{4,3,2,1,0:T(8,128)(2,1)} %get-tuple-element.197.k_own.own, bf16[4,4,2,64,2048]{4,3,2,1,0:T(8,128)(2,1)} %get-tuple-element.198.v_own.own, ...), custom_call_target="tpu_custom_call" | custom-call | flops 2359296 | bytes 2359296 | tf_op jit(solution)/shard_map/cond/branch_0_fun/pack/pallas_call | solution.py:90
  43.2 1.8 collective-permute-start.1
  45.0 33.4 %collective-permute-done.refs_3_ = bf16[2,64,2048]{2,1,0:T(8,128)(2,1)} collective-permute-done((bf16[2,64,2048]{2,1,0:T(8,128)(2,1)}, bf16[2,64,2048]{2,1,0:T(8,128)(2,1)}, u32[]{:S(2)}, u32[]{:S(2)}) %collective-permute-start) | collective-permute-done | bytes 524320 | tf_op jit(solution)/shard_map/cond/branch_0_fun/ppermute | solution.py:571
  78.4 5.6 %attend_window.12 = (f32[1,2048]{1,0:T(1,128)}, bf16[3,2,64,4096]{3,2,1,0:T(8,128)(2,1)S(1)}, bf16[3,2,64,4096]{3,2,1,0:T(8,128)(2,1)}) custom-call(s32[5]{0:T(128)S(1)} %get-tuple-element.245.ids, f32[4,2,64]{2,1,0:T(2,128)S(1)} %get-tuple-element.193.q_ref, ...), custom_call_target="tpu_custom_call", output_to_operand_aliasing={{1}: (13, {}), {2}: (14, {})} | custom-call | flops 4194304 | bytes 4194304 | tf_op jit(solution)/shard_map/cond/branch_0_fun/attend_window/pallas_call | solution.py:249
  84.0 7.5 %tp_sum.12.h_ref = bf16[1,2048]{1,0:T(2,128)(2,1)} custom-call(f32[1,2048]{1,0:T(1,128)} %get-tuple-element.207.part_ref, bf16[1,2048]{1,0:T(2,128)(2,1)S(1)} %get-tuple-element.208.h_ref), custom_call_target="tpu_custom_call" | custom-call | flops 24576 | bytes 24576 | tf_op jit(solution)/shard_map/cond/branch_0_fun/tp_sum/pallas_call | solution.py:452
  91.5 13.4 %front.13 = (f32[4,2,64]{2,1,0:T(2,128)}, f32[2,2,64]{2,1,0:T(2,128)}, f32[1,2048]{1,0:T(1,128)}) custom-call(bf16[1,2048]{1,0:T(2,128)(2,1)} %tp_sum.12.h_ref, bf16[4,2048]{1,0:T(4,128)(2,1)S(1)} %get-tuple-element.209.gain, f32[1,128]{1,0:T(1,128)S(1)} %get-tuple-element.210.cosine, f32[1,128]{1,0:T(1,128)S(1)} %get-tuple-element.211.sine, ...), custom_call_target="tpu_custom_call" | custom-call | flops 28311552 | bytes 28311552 | tf_op jit(solution)/shard_map/cond/branch_0_fun/front/pallas_call | solution.py:533
  104.9 0.1 collective-permute-start.3
  105.0 2.9 %pack.9 = (bf16[2,2,64,2048]{3,2,1,0:T(8,128)(2,1)}, bf16[2,2,64,256]{3,2,1,0:T(8,128)(2,1)}) custom-call(s32[5]{0:T(128)S(1)} %get-tuple-element.245.ids, bf16[4,4,2,64,2048]{4,3,2,1,0:T(8,128)(2,1)} %get-tuple-element.197.k_own.own, bf16[4,4,2,64,2048]{4,3,2,1,0:T(8,128)(2,1)} %get-tuple-element.198.v_own.own, ...), custom_call_target="tpu_custom_call" | custom-call | flops 2359296 | bytes 2359296 | tf_op jit(solution)/shard_map/cond/branch_0_fun/pack/pallas_call | solution.py:90
  107.9 1.1 collective-permute-start.4
  109.0 1.0 collective-permute-start.2
  110.0 26.5 %collective-permute-done.2.refs_1_ = bf16[2,2,64,256]{3,2,1,0:T(8,128)(2,1)S(1)} collective-permute-done((bf16[2,2,64,256]{3,2,1,0:T(8,128)(2,1)S(1)}, bf16[2,2,64,256]{3,2,1,0:T(8,128)(2,1)S(1)}, u32[]{:S(2)}, u32[]{:S(2)}) %collective-permute-start.2) | collective-permute-done | bytes 131104 | tf_op jit(solution)/shard_map/cond/branch_0_fun/ppermute | solution.py:571
  136.5 0.7 copy-done.9
  137.2 6.2 %attend_window.13 = (f32[1,2048]{1,0:T(1,128)}, bf16[3,2,64,4096]{3,2,1,0:T(8,128)(2,1)S(1)}, bf16[3,2,64,4096]{3,2,1,0:T(8,128)(2,1)}) custom-call(s32[5]{0:T(128)S(1)} %get-tuple-element.245.ids, f32[4,2,64]{2,1,0:T(2,128)} %get-tuple-element.218.q_ref, f32[2,2,64]{2,1,0:T(2,128)} %get-tuple-element.219.new_ref, ...), custom_call_target="tpu_custom_call", output_to_operand_aliasing={{1}: (12, {}), {2}: (13, {})} | custom-call | flops 4194304 | bytes 4194304 | tf_op jit(solution)/shard_map/cond/branch_0_fun/attend_window/pallas_call | solution.py:249
  143.4 7.1 %tp_sum.13.h_ref = bf16[1,2048]{1,0:T(2,128)(2,1)} custom-call(f32[1,2048]{1,0:T(1,128)} %get-tuple-element.226.part_ref, bf16[1,2048]{1,0:T(2,128)(2,1)} %tp_sum.12.h_ref), custom_call_target="tpu_custom_call" | custom-call | flops 24576 | bytes 24576 | tf_op jit(solution)/shard_map/cond/branch_0_fun/tp_sum/pallas_call | solution.py:452
  150.5 13.4 %front.14 = (f32[4,2,64]{2,1,0:T(2,128)}, f32[2,2,64]{2,1,0:T(2,128)}, f32[1,2048]{1,0:T(1,128)}) custom-call(bf16[1,2048]{1,0:T(2,128)(2,1)} %tp_sum.13.h_ref, bf16[4,2048]{1,0:T(4,128)(2,1)S(1)} %get-tuple-element.209.gain, f32[1,128]{1,0:T(1,128)S(1)} %get-tuple-element.210.cosine, f32[1,128]{1,0:T(1,128)S(1)} %get-tuple-element.211.sine, ...), custom_call_target="tpu_custom_call" | custom-call | flops 28311552 | bytes 28311552 | tf_op jit(solution)/shard_map/cond/branch_0_fun/front/pallas_call | solution.py:533
  163.9 0.1 collective-permute-start.6
  164.0 0.7 collective-permute-start.5
  164.8 2.9 %dynamic-slice_bitcast_fusion = (bf16[2,64,2048]{2,1,0:T(8,128)(2,1)}, bf16[2,64,2048]{2,1,0:T(8,128)(2,1)}, bf16[2,64,2048]{2,1,0:T(8,128)(2,1)}, bf16[2,64,2048]{2,1,0:T(8,128)(2,1)}) fusion(bf16[4,4,2,64,2048]{4,3,2,1,0:T(8,128)(2,1)} %get-tuple-element.198.v_own.own, s32[]{:T(128)S(6)} %select_n.36, s32[]{:T(128)S(6)} %select_n.35, ...), kind=kLoop, calls=%fused_computation | loop fusion | bytes 4194312 | tf_op jit(solution)/shard_map/cond/branch_0_fun/squeeze | solution.py:593
  167.7 1.4 collective-permute-start.7
  169.0 0.1 collective-permute-start.8
  169.2 1.4 collective-permute-start.10
  170.5 0.6 collective-permute-start.9
  171.2 6.2 %attend_window.14 = (f32[1,2048]{1,0:T(1,128)}, bf16[3,2,64,4096]{3,2,1,0:T(8,128)(2,1)S(1)}, bf16[3,2,64,4096]{3,2,1,0:T(8,128)(2,1)}) custom-call(s32[5]{0:T(128)S(1)} %get-tuple-element.245.ids, f32[4,2,64]{2,1,0:T(2,128)} %get-tuple-element.227.q_ref, f32[2,2,64]{2,1,0:T(2,128)} %get-tuple-element.228.new_ref, ...), custom_call_target="tpu_custom_call", output_to_operand_aliasing={{1}: (12, {}), {2}: (13, {})} | custom-call | flops 4194304 | bytes 4194304 | tf_op jit(solution)/shard_map/cond/branch_0_fun/attend_window/pallas_call | solution.py:249
  177.4 7.1 %tp_sum.14.h_ref = bf16[1,2048]{1,0:T(2,128)(2,1)} custom-call(f32[1,2048]{1,0:T(1,128)} %get-tuple-element.235.part_ref, bf16[1,2048]{1,0:T(2,128)(2,1)} %tp_sum.13.h_ref), custom_call_target="tpu_custom_call" | custom-call | flops 24576 | bytes 24576 | tf_op jit(solution)/shard_map/cond/branch_0_fun/tp_sum/pallas_call | solution.py:452
  184.5 13.2 %front.15 = (f32[4,2,64]{2,1,0:T(2,128)}, f32[2,2,64]{2,1,0:T(2,128)}, f32[1,2048]{1,0:T(1,128)}) custom-call(bf16[1,2048]{1,0:T(2,128)(2,1)} %tp_sum.14.h_ref, bf16[4,2048]{1,0:T(4,128)(2,1)S(1)} %get-tuple-element.209.gain, bf16[4,2048,512]{2,1,0:T(8,128)(2,1)} %get-tuple-element.212.wq.refs_0_, bf16[4,2048,128]{2,1,0:T(8,128)(2,1)} %get-tuple-element.213.wk.refs_1_, ...), custom_call_target="tpu_custom_call" | custom-call | flops 28311552 | bytes 28311552 | tf_op jit(solution)/shard_map/cond/branch_0_fun/front/pallas_call | solution.py:533
  197.8 3.3 %place.12 = bf16[2,64,8192]{2,1,0:T(8,128)(2,1)} custom-call(s32[5]{0:T(128)S(1)} %get-tuple-element.245.ids, f32[2,2,64]{2,1,0:T(2,128)} %get-tuple-element.237.new_ref, bf16[4,4,2,64,2048]{4,3,2,1,0:T(8,128)(2,1)} %get-tuple-element.197.k_own.own, bf16[4,4,2,64,2048]{4,3,2,1,0:T(8,128)(2,1)} %get-tuple-element.199.k_near.near, ...), custom_call_target="tpu_custom_call", output_to_operand_aliasing={{}: (6, {})} | custom-call | flops 4194304 | bytes 4194304 | tf_op jit(solution)/shard_map/cond/branch_0_fun/place/pallas_call | solution.py:297
  201.1 4.1 %collective-permute-done.10.refs_0_ = bf16[2,64,2048]{2,1,0:T(8,128)(2,1)} collective-permute-done((bf16[2,64,2048]{2,1,0:T(8,128)(2,1)}, bf16[2,64,2048]{2,1,0:T(8,128)(2,1)}, u32[]{:S(2)}, u32[]{:S(2)}) %collective-permute-start.10) | collective-permute-done | bytes 524320 | tf_op jit(solution)/shard_map/cond/branch_0_fun/ppermute | solution.py:571
  205.3 3.0 %place.13.refs_1_ = bf16[2,64,8192]{2,1,0:T(8,128)(2,1)} custom-call(s32[5]{0:T(128)S(1)} %get-tuple-element.245.ids, f32[2,2,64]{2,1,0:T(2,128)} %get-tuple-element.237.new_ref, bf16[4,4,2,64,2048]{4,3,2,1,0:T(8,128)(2,1)} %get-tuple-element.198.v_own.own, ...), custom_call_target="tpu_custom_call", output_to_operand_aliasing={{}: (5, {})} | custom-call | flops 3145728 | bytes 3145728 | tf_op jit(solution)/shard_map/cond/branch_0_fun/place/pallas_call | solution.py:297
  208.2 20.3 %spread.4 = bf16[1,2048]{1,0:T(2,128)(2,1)S(1)} custom-call(s32[5]{0:T(128)S(1)} %get-tuple-element.245.ids, f32[4,2,64]{2,1,0:T(2,128)} %get-tuple-element.236.q_ref, f32[2,2,64]{2,1,0:T(2,128)} %get-tuple-element.237.new_ref, f32[1,2048]{1,0:T(1,128)} %get-tuple-element.238.mlp_ref, bf16[1,2048]{1,0:T(2,128)(2,1)} %tp_sum.14.h_ref, ...), custom_call_target="tpu_custom_call" | custom-call | flops 4194304 | bytes 4194304 | tf_op jit(solution)/shard_map/cond/branch_0_fun/spread/pallas_call | solution.py:398
  228.6 2.8 %place.14 = bf16[2,64,8192]{2,1,0:T(8,128)(2,1)} custom-call(s32[5]{0:T(128)S(1)} %get-tuple-element.245.ids, f32[2,2,64]{2,1,0:T(2,128)} %get-tuple-element.237.new_ref, bf16[4,4,2,64,2048]{4,3,2,1,0:T(8,128)(2,1)} %get-tuple-element.198.v_own.own, bf16[4,4,2,64,2048]{4,3,2,1,0:T(8,128)(2,1)} %get-tuple-element.200.v_near.near, ...), custom_call_target="tpu_custom_call", output_to_operand_aliasing={{}: (5, {})} | custom-call | flops 1048576 | bytes 1048576 | tf_op jit(solution)/shard_map/cond/branch_0_fun/place/pallas_call | solution.py:297
  231.9 0.6 copy.110
  (35 shorter events, 0.1 us)
Async XLA Ops:
  0.6 8.5 %copy-start.12 = (s32[4]{0:T(128)S(1)}, s32[4]{0:T(128)}, u32[]{:S(2)}) copy-start(s32[4]{0:T(128)} %param.18) | copy-start | bytes 52
  0.6 17.6 %copy-start.7 = (bf16[1,2048]{1,0:T(2,128)(2,1)S(1)}, bf16[1,2048]{1,0:T(2,128)(2,1)}, u32[]{:S(2)}) copy-start(bf16[1,2048]{1,0:T(2,128)(2,1)} %h_ref.1) | copy-start | bytes 12292
  0.7 17.6 %copy-start.4 = (bf16[4,2048]{1,0:T(4,128)(2,1)S(1)}, bf16[4,2048]{1,0:T(4,128)(2,1)}, u32[]{:S(2)}) copy-start(bf16[4,2048]{1,0:T(4,128)(2,1)} %gain.1) | copy-start | bytes 49156
  0.7 39.7 %collective-permute-start.42 = (bf16[4,4,2,64,2048]{4,3,2,1,0:T(8,128)(2,1)}, bf16[4,4,2,64,2048]{4,3,2,1,0:T(8,128)(2,1)}, u32[]{:S(2)}, u32[]{:S(2)}) collective-permute-start(bf16[4,4,2,64,2048]{4,3,2,1,0:T(8,128)(2,1)} %bitcast.69), channel_id=1, source_target_pairs={{0,1},{1,0},{2,3},{3,2},{4,5},{5,4},{6,7},{7,6},{8,9},{9,8},{10,11... | collective-permute-start | bytes 25165832 | tf_op jit(solution)/shard_map/ppermute | solution.py:571
  1.2 39.1 %collective-permute-start.43 = (bf16[4,4,2,64,2048]{4,3,2,1,0:T(8,128)(2,1)}, bf16[4,4,2,64,2048]{4,3,2,1,0:T(8,128)(2,1)}, u32[]{:S(2)}, u32[]{:S(2)}) collective-permute-start(bf16[4,4,2,64,2048]{4,3,2,1,0:T(8,128)(2,1)} %bitcast.64), channel_id=1, source_target_pairs={{0,1},{1,0},{2,3},{3,2},{4,5},{5,4},{6,7},{7,6},{8,9},{9,8},{10,11... | collective-permute-start | bytes 25165832 | tf_op jit(solution)/shard_map/ppermute | solution.py:571
  2.6 28.6 %collective-permute-start.44 = (bf16[2,64,2048]{2,1,0:T(8,128)(2,1)S(1)}, bf16[2,64,2048]{2,1,0:T(8,128)(2,1)}, u32[]{:S(2)}, u32[]{:S(2)}) collective-permute-start(bf16[2,64,2048]{2,1,0:T(8,128)(2,1)S(1)} %get-tuple-element.466), channel_id=1, source_target_pairs={{0,2},{1,3},{2,0},{3,1},{4,6},{5,7},{6,4},{7,5},{8,10},{9,11},{10,... | collective-permute-start | bytes 1572872 | tf_op jit(solution)/shard_map/ppermute | solution.py:571
  5.6 25.6 %collective-permute-start.45 = (bf16[2,64,2048]{2,1,0:T(8,128)(2,1)S(1)}, bf16[2,64,2048]{2,1,0:T(8,128)(2,1)}, u32[]{:S(2)}, u32[]{:S(2)}) collective-permute-start(bf16[2,64,2048]{2,1,0:T(8,128)(2,1)S(1)} %get-tuple-element.465), channel_id=1, source_target_pairs={{0,3},{1,2},{2,1},{3,0},{4,7},{5,6},{6,5},{7,4},{8,11},{9,10},{10,... | collective-permute-start | bytes 1572872 | tf_op jit(solution)/shard_map/ppermute | solution.py:571
  7.7 32.6 %collective-permute-start.46 = (bf16[2,64,2048]{2,1,0:T(8,128)(2,1)S(1)}, bf16[2,64,2048]{2,1,0:T(8,128)(2,1)}, u32[]{:S(2)}, u32[]{:S(2)}) collective-permute-start(bf16[2,64,2048]{2,1,0:T(8,128)(2,1)S(1)} %get-tuple-element.463), channel_id=1, source_target_pairs={{0,2},{1,3},{2,0},{3,1},{4,6},{5,7},{6,4},{7,5},{8,10},{9,11},{10,... | collective-permute-start | bytes 1572872 | tf_op jit(solution)/shard_map/ppermute | solution.py:571
  43.2 61.6 %collective-permute-start.1 = (bf16[2,2,64,2048]{3,2,1,0:T(8,128)(2,1)}, bf16[2,2,64,2048]{3,2,1,0:T(8,128)(2,1)}, u32[]{:S(2)}, u32[]{:S(2)}) collective-permute-start(bf16[2,2,64,2048]{3,2,1,0:T(8,128)(2,1)} %get-tuple-element.221), channel_id=1, source_target_pairs={{0,2},{1,3},{2,0},{3,1},{4,6},{5,7},{6,4},{7,5},{8,10},{9,11},{10,... | collective-permute-start | bytes 3145736 | tf_op jit(solution)/shard_map/cond/branch_0_fun/ppermute | solution.py:571
  45.0 33.4 %collective-permute-start = (bf16[2,64,2048]{2,1,0:T(8,128)(2,1)}, bf16[2,64,2048]{2,1,0:T(8,128)(2,1)}, u32[]{:S(2)}, u32[]{:S(2)}) collective-permute-start(bf16[2,64,2048]{2,1,0:T(8,128)(2,1)} %get-tuple-element.204), channel_id=1, source_target_pairs={{0,3},{1,2},{2,1},{3,0},{4,7},{5,6},{6,5},{7,4},{8,11},{9,10},{10,... | collective-permute-start | bytes 1572872 | tf_op jit(solution)/shard_map/cond/branch_0_fun/ppermute | solution.py:571
  104.9 4.1 %copy-start.11 = (bf16[2,2,64,256]{3,2,1,0:T(8,128)(2,1)S(1)}, bf16[2,2,64,256]{3,2,1,0:T(8,128)(2,1)}, u32[]{:S(2)}) copy-start(bf16[2,2,64,256]{3,2,1,0:T(8,128)(2,1)} %get-tuple-element.222) | copy-start | bytes 393220 | tf_op jit(solution)/shard_map/cond
  104.9 31.6 %collective-permute-start.3 = (bf16[2,2,64,2048]{3,2,1,0:T(8,128)(2,1)}, bf16[2,2,64,2048]{3,2,1,0:T(8,128)(2,1)}, u32[]{:S(2)}, u32[]{:S(2)}) collective-permute-start(bf16[2,2,64,2048]{3,2,1,0:T(8,128)(2,1)} %collective-permute-done.1.refs_0_), channel_id=1, source_target_pairs={{0,1},{1,0},{2,3},{3,2},{4,5},{5,4},{6,7},{7,6},{8,9},{9,8},{10,11... | collective-permute-start | bytes 3145736 | tf_op jit(solution)/shard_map/cond/branch_0_fun/ppermute | solution.py:571
  107.9 56.1 %collective-permute-start.4 = (bf16[2,2,64,2048]{3,2,1,0:T(8,128)(2,1)}, bf16[2,2,64,2048]{3,2,1,0:T(8,128)(2,1)}, u32[]{:S(2)}, u32[]{:S(2)}) collective-permute-start(bf16[2,2,64,2048]{3,2,1,0:T(8,128)(2,1)} %get-tuple-element.230), channel_id=1, source_target_pairs={{0,2},{1,3},{2,0},{3,1},{4,6},{5,7},{6,4},{7,5},{8,10},{9,11},{10,... | collective-permute-start | bytes 3145736 | tf_op jit(solution)/shard_map/cond/branch_0_fun/ppermute | solution.py:571
  109.0 27.5 %collective-permute-start.2 = (bf16[2,2,64,256]{3,2,1,0:T(8,128)(2,1)S(1)}, bf16[2,2,64,256]{3,2,1,0:T(8,128)(2,1)S(1)}, u32[]{:S(2)}, u32[]{:S(2)}) collective-permute-start(bf16[2,2,64,256]{3,2,1,0:T(8,128)(2,1)S(1)} %copy-done.11), channel_id=1, source_target_pairs={{0,2},{1,3},{2,0},{3,1},{4,6},{5,7},{6,4},{7,5},{8,10},{9,11},{10,... | collective-permute-start | bytes 393224 | tf_op jit(solution)/shard_map/cond/branch_0_fun/ppermute | solution.py:571
  136.5 0.7 copy-start.9
  150.5 13.5 %copy-start.10 = (bf16[2,2,64,256]{3,2,1,0:T(8,128)(2,1)S(1)}, bf16[2,2,64,256]{3,2,1,0:T(8,128)(2,1)}, u32[]{:S(2)}) copy-start(bf16[2,2,64,256]{3,2,1,0:T(8,128)(2,1)} %get-tuple-element.231) | copy-start | bytes 393220 | tf_op jit(solution)/shard_map/cond
  163.9 7.2 %collective-permute-start.6 = (bf16[2,2,64,2048]{3,2,1,0:T(8,128)(2,1)}, bf16[2,2,64,2048]{3,2,1,0:T(8,128)(2,1)}, u32[]{:S(2)}, u32[]{:S(2)}) collective-permute-start(bf16[2,2,64,2048]{3,2,1,0:T(8,128)(2,1)} %collective-permute-done.4.refs_0_), channel_id=1, source_target_pairs={{0,1},{1,0},{2,3},{3,2},{4,5},{5,4},{6,7},{7,6},{8,9},{9,8},{10,11... | collective-permute-start | bytes 3145736 | tf_op jit(solution)/shard_map/cond/branch_0_fun/ppermute | solution.py:571
  164.0 6.5 %collective-permute-start.5 = (bf16[2,2,64,256]{3,2,1,0:T(8,128)(2,1)S(1)}, bf16[2,2,64,256]{3,2,1,0:T(8,128)(2,1)S(1)}, u32[]{:S(2)}, u32[]{:S(2)}) collective-permute-start(bf16[2,2,64,256]{3,2,1,0:T(8,128)(2,1)S(1)} %copy-done.10), channel_id=1, source_target_pairs={{0,2},{1,3},{2,0},{3,1},{4,6},{5,7},{6,4},{7,5},{8,10},{9,11},{10,... | collective-permute-start | bytes 393224 | tf_op jit(solution)/shard_map/cond/branch_0_fun/ppermute | solution.py:571
  167.7 30.1 %collective-permute-start.7 = (bf16[2,64,2048]{2,1,0:T(8,128)(2,1)}, bf16[2,64,2048]{2,1,0:T(8,128)(2,1)}, u32[]{:S(2)}, u32[]{:S(2)}) collective-permute-start(bf16[2,64,2048]{2,1,0:T(8,128)(2,1)} %get-tuple-element.242), channel_id=1, source_target_pairs={{0,2},{1,3},{2,0},{3,1},{4,6},{5,7},{6,4},{7,5},{8,10},{9,11},{10,... | collective-permute-start | bytes 1572872 | tf_op jit(solution)/shard_map/cond/branch_0_fun/ppermute | solution.py:571
  169.0 28.8 %collective-permute-start.8 = (bf16[2,64,2048]{2,1,0:T(8,128)(2,1)}, bf16[2,64,2048]{2,1,0:T(8,128)(2,1)}, u32[]{:S(2)}, u32[]{:S(2)}) collective-permute-start(bf16[2,64,2048]{2,1,0:T(8,128)(2,1)} %get-tuple-element.243), channel_id=1, source_target_pairs={{0,3},{1,2},{2,1},{3,0},{4,7},{5,6},{6,5},{7,4},{8,11},{9,10},{10,... | collective-permute-start | bytes 1572872 | tf_op jit(solution)/shard_map/cond/branch_0_fun/ppermute | solution.py:571
  169.2 36.1 %collective-permute-start.10 = (bf16[2,64,2048]{2,1,0:T(8,128)(2,1)}, bf16[2,64,2048]{2,1,0:T(8,128)(2,1)}, u32[]{:S(2)}, u32[]{:S(2)}) collective-permute-start(bf16[2,64,2048]{2,1,0:T(8,128)(2,1)} %get-tuple-element.247), channel_id=1, source_target_pairs={{0,2},{1,3},{2,0},{3,1},{4,6},{5,7},{6,4},{7,5},{8,10},{9,11},{10,... | collective-permute-start | bytes 1572872 | tf_op jit(solution)/shard_map/cond/branch_0_fun/ppermute | solution.py:571
  170.5 0.7 copy-start.8
  170.5 58.1 %collective-permute-start.9 = (bf16[2,64,2048]{2,1,0:T(8,128)(2,1)}, bf16[2,64,2048]{2,1,0:T(8,128)(2,1)}, u32[]{:S(2)}, u32[]{:S(2)}) collective-permute-start(bf16[2,64,2048]{2,1,0:T(8,128)(2,1)} %get-tuple-element.246), channel_id=1, source_target_pairs={{0,3},{1,2},{2,1},{3,0},{4,7},{5,6},{6,5},{7,4},{8,11},{9,10},{10,... | collective-permute-start | bytes 1572872 | tf_op jit(solution)/shard_map/cond/branch_0_fun/ppermute | solution.py:571
  177.4 20.4 %copy-start = (bf16[3,2,64,4096]{3,2,1,0:T(8,128)(2,1)}, bf16[3,2,64,4096]{3,2,1,0:T(8,128)(2,1)S(1)}, u32[]{:S(2)}) copy-start(bf16[3,2,64,4096]{3,2,1,0:T(8,128)(2,1)S(1)} %get-tuple-element.470) | copy-start | bytes 9437188 | tf_op jit(solution)/shard_map/cond

commit v3 on v2

--- a/solution.py
+++ b/solution.py
@@ -306,120 +306,6 @@
     )(ids, new_kv, own, near, *blocks, buf)
 
 
-def spread_body(layer, ids, q_ref, new_ref, mlp_ref, h_ref, wo_hbm, k_own, v_own, out_ref, k_all, v_all, wo, q_all, stats, mixes, part_ref, slots, expd, sems, send_sems, recv_sems):
-    me = lax.axis_index("sp")
-    tp = lax.axis_index("tp")
-    barrier = pltpu.get_barrier_semaphore()
-    sp_peers = [{"sp": jnp.bitwise_xor(me, r)} for r in PEERS]
-    tp_peers = [{"tp": jnp.bitwise_xor(tp, r)} for r in PEERS]
-    for peer in sp_peers + tp_peers:
-        pl.semaphore_signal(barrier, inc=1, device_id=peer, device_id_type=pl.DeviceIdType.MESH)
-    loads = [pltpu.make_async_copy(k_own.at[layer], k_all, sems.at[0]), pltpu.make_async_copy(v_own.at[layer], v_all, sems.at[1]), pltpu.make_async_copy(wo_hbm.at[layer], wo, sems.at[2])]
-    for load in loads:
-        load.start()
-
-    def exchange(stage, peers, pairs):
-        copies = [
-            pltpu.make_async_remote_copy(src, dst, send_sems.at[stage, i], recv_sems.at[stage, i], device_id=peer, device_id_type=pl.DeviceIdType.MESH)
-            for i, (peer, (src, dst)) in enumerate(zip(peers, pairs))
-        ]
-        for copy in copies:
-            copy.start()
-        return copies
-
-    def done(copies):
-        for copy in copies:
-            copy.wait()
-
-    pl.semaphore_wait(barrier, 6)
-    queries = exchange(0, sp_peers, [(q_ref, q_all.at[i]) for i in range(3)])
-    n_q = q_ref.shape[0] * q_ref.shape[1]
-    dim = q_ref.shape[2]
-    shard = k_all.shape[-1]
-    upper = lax.broadcasted_iota(jnp.int32, (n_q, 1), 0) < n_q // 2
-    lane = lax.broadcasted_iota(jnp.int32, (1, UNIT), 1)
-    position = lax.broadcasted_iota(jnp.int32, (1, shard), 1) + me * shard
-    q_own = jnp.concatenate([q_ref[j] for j in range(q_ref.shape[0])], axis=0)
-    new_k = jnp.where(upper, new_ref[0, 0:1], new_ref[0, 1:2])
-    new_v = jnp.where(upper, new_ref[1, 0:1], new_ref[1, 1:2])
-    new_score = (q_own * new_k).sum(axis=-1, keepdims=True) * (dim ** -0.5)
-
-    def score(r):
-        row = jnp.bitwise_xor(me, r)
-        q = q_own if r == 0 else jnp.concatenate([q_all[r - 1, j] for j in range(q_ref.shape[0])], axis=0)
-        q = q.astype(BF16)
-        s0 = jnp.dot(q, k_all[row, 0], preferred_element_type=F32)
-        s1 = jnp.dot(q, k_all[row, 1], preferred_element_type=F32)
-        scores = jnp.where(position < ids[1 + row], jnp.where(upper, s0, s1) * (dim ** -0.5), -1e30)
-        top = scores.max(axis=-1, keepdims=True)
-        e = jnp.exp(scores - top)
-        expd[r] = e
-        stats[0, r] = jnp.where(lane == 0, top, jnp.where(lane == 1, e.sum(axis=-1, keepdims=True), new_score))
-
-    loads[0].wait()
-    score(0)
-    done(queries)
-    for r in PEERS:
-        score(r)
-    done(exchange(1, sp_peers, [(stats.at[0], stats.at[r]) for r in PEERS]))
-    loads[1].wait()
-    dims = (((1,), (1,)), ((), ()))
-    for r in (1, 2, 3, 0):
-        row = jnp.bitwise_xor(me, r)
-        seen = [stats[other, other ^ r] for other in range(4)]
-        fresh = stats[r, 0][:, 2:3]
-        top = fresh
-        for one in seen:
-            top = jnp.maximum(top, one[:, 0:1])
-        total = jnp.exp(fresh - top)
-        for one in seen:
-            total = total + one[:, 1:2] * jnp.exp(one[:, 0:1] - top)
-        weights = (expd[r] * (jnp.exp(stats[0, r][:, 0:1] - top) / total)).astype(BF16)
-        m0 = lax.dot_general(weights, v_all[row, 0], dims, preferred_element_type=F32)
-        m1 = lax.dot_general(weights, v_all[row, 1], dims, preferred_element_type=F32)
-        mixed = jnp.where(upper, m0, m1)
-        if r == 0:
-            mixed = mixed + (jnp.exp(fresh - top) / total).astype(BF16).astype(F32) * new_v
-        mixes[0, r] = mixed
-    done(exchange(2, sp_peers, [(mixes.at[0, r], mixes.at[1, r]) for r in PEERS]))
-    mixed = mixes[0, 0] + mixes[1, 1] + mixes[1, 2] + mixes[1, 3]
-    mixed = mixed.astype(BF16).astype(F32)
-    flat = jnp.concatenate([mixed[j:j + 1] for j in range(n_q)], axis=1)
-    flat = jnp.broadcast_to(flat, (8, flat.shape[1])).astype(BF16)
-    loads[2].wait()
-    part_ref[...] = jnp.dot(flat, wo[...], preferred_element_type=F32)[0:1] + mlp_ref[...]
-    done(exchange(3, tp_peers, [(part_ref, slots.at[i]) for i in range(3)]))
-    out_ref[...] = in_tp_order(tp, [part_ref[...]] + [slots[i] for i in range(3)], h_ref[...])
-
-
-def spread(layer, ids, q, new_kv, mlp, residual, w_out, k_t, v_t):
-    rows, heads, dim, shard = k_t.shape[1:]
-    n_q = q.shape[0] * q.shape[1]
-    return pl.pallas_call(
-        functools.partial(spread_body, layer),
-        in_specs=[SMEM, VMEM, VMEM, VMEM, VMEM, HBM, HBM, HBM],
-        out_specs=VMEM,
-        out_shape=jax.ShapeDtypeStruct(residual.shape, BF16),
-        scratch_shapes=[
-            pltpu.VMEM((rows, heads, dim, shard), BF16),
-            pltpu.VMEM((rows, heads, dim, shard), BF16),
-            pltpu.VMEM(w_out.shape[1:], BF16),
-            pltpu.VMEM((3,) + q.shape, F32),
-            pltpu.VMEM((4, 4, n_q, UNIT), F32),
-            pltpu.VMEM((2, 4, n_q, dim), F32),
-            pltpu.VMEM(mlp.shape, F32),
-            pltpu.VMEM((3,) + mlp.shape, F32),
-            pltpu.VMEM((4, n_q, shard), F32),
-            pltpu.SemaphoreType.DMA((3,)),
-            pltpu.SemaphoreType.DMA((4, 3)),
-            pltpu.SemaphoreType.DMA((4, 3)),
-        ],
-        compiler_params=pltpu.CompilerParams(collective_id=layer, has_side_effects=True),
-        cost_estimate=cost(16 * heads * dim * shard),
-        name="spread",
-    )(ids, q, new_kv, mlp, residual, w_out, k_t, v_t)
-
-
 def in_tp_order(tp, parts, residual):
     for t in range(4):
         at = jnp.bitwise_xor(tp, t)
@@ -430,80 +316,257 @@
     return (residual.astype(F32) + total).astype(BF16)
 
 
-def tp_sum_body(part_ref, h_ref, out_ref, slots, send_sems, recv_sems):
-    tp = lax.axis_index("tp")
-    barrier = pltpu.get_barrier_semaphore()
-    peers = [{"tp": jnp.bitwise_xor(tp, r)} for r in PEERS]
+def scores_body(layer, ids, q_ref, new_ref, own, near, far, cross, k_in, w_ref, last_ref, k_out, kv, sem, out_sem, scores):
+    me = ids[0]
+    length = ids[1 + me]
+    shard = own.shape[-1]
+    sources = [own.at[layer, me], near.at[layer, me], far, cross]
+    move([(src, kv.at[:, :, pl.ds(pl.multiple_of(jnp.bitwise_xor(me, r) * shard, UNIT), shard)], sem) for r, src in enumerate(sources)])
+    pltpu.make_async_copy(kv, kv, sem).wait()
+    settle(kv, new_ref[0], length, jnp.zeros_like, (length // UNIT, kv.shape[-1] // UNIT))
+    weights = softmax_weights(stacked(q_ref), kv, scores, length)
+    copy = pltpu.make_async_copy(kv, k_out, out_sem)
+    copy.start()
+    newest = lax.broadcasted_iota(jnp.int32, (1, weights.shape[1]), 1) == length
+    weights = weights.astype(F32)
+    last_ref[...] = jnp.broadcast_to(jnp.where(newest, weights, 0.0).sum(axis=-1, keepdims=True), last_ref.shape)
+    w_ref[...] = jnp.where(newest, 0.0, weights).astype(BF16)
+    copy.wait()
+
+
+def score_global(layer, ids, q, new_kv, k_t, near, blocks, k_buf):
+    n_q = q.shape[0] * q.shape[1]
+    seq = k_buf.shape[-1]
+    return pl.pallas_call(
+        functools.partial(scores_body, layer),
+        in_specs=[SMEM, VMEM, VMEM] + [HBM] * 5,
+        out_specs=[VMEM, VMEM, HBM],
+        out_shape=[jax.ShapeDtypeStruct((n_q, seq), BF16), jax.ShapeDtypeStruct((n_q, UNIT), F32), jax.ShapeDtypeStruct(k_buf.shape, BF16)],
+        scratch_shapes=[pltpu.VMEM(k_buf.shape, BF16), pltpu.SemaphoreType.DMA, pltpu.SemaphoreType.DMA, pltpu.VMEM((n_q, seq), F32)],
+        input_output_aliases={7: 2},
+        cost_estimate=cost(4 * k_buf.size),
+        name="scores",
+    )(ids, q, new_kv, k_t, near, *blocks, k_buf)
+
+
+def greet(axis):
+    me = lax.axis_index(axis)
+    peers = [{axis: jnp.bitwise_xor(me, r)} for r in PEERS]
     for peer in peers:
-        pl.semaphore_signal(barrier, inc=1, device_id=peer, device_id_type=pl.DeviceIdType.MESH)
-    pl.semaphore_wait(barrier, 3)
+        pl.semaphore_signal(pltpu.get_barrier_semaphore(), inc=1, device_id=peer, device_id_type=pl.DeviceIdType.MESH)
+    return peers
+
+
+def share(peers, src, slots, send_sems, recv_sems):
+    pl.semaphore_wait(pltpu.get_barrier_semaphore(), len(PEERS))
     copies = [
-        pltpu.make_async_remote_copy(part_ref, slots.at[i], send_sems.at[i], recv_sems.at[i], device_id=peer, device_id_type=pl.DeviceIdType.MESH)
+        pltpu.make_async_remote_copy(src, slots.at[i], send_sems.at[i], recv_sems.at[i], device_id=peer, device_id_type=pl.DeviceIdType.MESH)
         for i, peer in enumerate(peers)
     ]
     for copy in copies:
         copy.start()
+    return copies
+
+
+def settled_sum(copies, mine, slots, residual):
     for copy in copies:
         copy.wait()
-    out_ref[...] = in_tp_order(tp, [part_ref[...]] + [slots[i] for i in range(3)], h_ref[...])
-
-
-def tp_sum(layer, part, residual):
+    return in_tp_order(lax.axis_index("tp"), [mine[...]] + [slots[i] for i in range(len(PEERS))], residual)
+
+
+def finish_body(layer, ids, w_ref, last_ref, new_ref, mlp_ref, h_ref, wo_hbm, own, near, far, cross, v_in, out_ref, v_out, shards, placed, wo, part_ref, slots, sems, send_sems, recv_sems):
+    me = lax.axis_index("sp")
+    peers = greet("tp")
+    length = ids[1 + me]
+    shard = own.shape[-1]
+    sources = [own.at[layer, me], near.at[layer, me], far, cross]
+    loads = [pltpu.make_async_copy(src, shards.at[r], sems.at[r]) for r, src in enumerate(sources)]
+    loads.append(pltpu.make_async_copy(wo_hbm.at[layer], wo, sems.at[4]))
+    for load in loads:
+        load.start()
+    n_q = w_ref.shape[0]
+    upper = lax.broadcasted_iota(jnp.int32, (n_q, 1), 0) < n_q // 2
+    dims = (((1,), (1,)), ((), ()))
+    mixed = last_ref[:, 0:1] * jnp.where(upper, new_ref[1, 0:1], new_ref[1, 1:2])
+    for r in range(4):
+        loads[r].wait()
+        at = pl.ds(pl.multiple_of(jnp.bitwise_xor(me, r) * shard, UNIT), shard)
+        weights = w_ref[:, at]
+        m0 = lax.dot_general(weights, shards[r, 0], dims, preferred_element_type=F32)
+        m1 = lax.dot_general(weights, shards[r, 1], dims, preferred_element_type=F32)
+        mixed = mixed + jnp.where(upper, m0, m1)
+    mixed = mixed.astype(BF16).astype(F32)
+    flat = jnp.concatenate([mixed[j:j + 1] for j in range(n_q)], axis=1)
+    flat = jnp.broadcast_to(flat, (8, flat.shape[1])).astype(BF16)
+    loads[4].wait()
+    part_ref[...] = jnp.dot(flat, wo[...], preferred_element_type=F32)[0:1] + mlp_ref[...]
+    copies = share(peers, part_ref, slots, send_sems, recv_sems)
+    position = lax.broadcasted_iota(jnp.int32, (1, shard), 1) + jnp.bitwise_xor(me, 3) * shard
+    for head in range(placed.shape[0]):
+        fresh = new_ref[1][head:head + 1].T
+        old = shards[3, head].astype(F32)
+        placed[head] = jnp.where(position < length, old, jnp.where(position == length, fresh, 0.0)).astype(BF16)
+    out_ref[...] = settled_sum(copies, part_ref, slots, h_ref[...])
+    store = pltpu.make_async_copy(placed, v_out.at[:, :, at], sems.at[3])
+    store.start()
+    store.wait()
+
+
+def finish(layer, ids, weights, last, new_kv, mlp, residual, w_out, v_t, near, blocks, v_buf):
+    heads, dim, shard = v_t.shape[2:]
     return pl.pallas_call(
-        tp_sum_body,
-        in_specs=[VMEM, VMEM],
-        out_specs=VMEM,
-        out_shape=jax.ShapeDtypeStruct(residual.shape, BF16),
-        scratch_shapes=[pltpu.VMEM((3,) + part.shape, F32), pltpu.SemaphoreType.DMA((3,)), pltpu.SemaphoreType.DMA((3,))],
+        functools.partial(finish_body, layer),
+        in_specs=[SMEM] + [VMEM] * 5 + [HBM] * 6,
+        out_specs=[VMEM, HBM],
+        out_shape=[jax.ShapeDtypeStruct(residual.shape, BF16), jax.ShapeDtypeStruct(v_buf.shape, BF16)],
+        scratch_shapes=[
+            pltpu.VMEM((4, heads, dim, shard), BF16),
+            pltpu.VMEM((heads, dim, shard), BF16),
+            pltpu.VMEM(w_out.shape[1:], BF16),
+            pltpu.VMEM(mlp.shape, F32),
+            pltpu.VMEM((3,) + mlp.shape, F32),
+            pltpu.SemaphoreType.DMA((5,)),
+            pltpu.SemaphoreType.DMA((3,)),
+            pltpu.SemaphoreType.DMA((3,)),
+        ],
+        input_output_aliases={11: 1},
+        compiler_params=pltpu.CompilerParams(collective_id=layer + 1, has_side_effects=True),
+        cost_estimate=cost(16 * heads * dim * shard),
+        name="finish",
+    )(ids, weights, last, new_kv, mlp, residual, w_out, v_t, near, *blocks, v_buf)
+
+
+def turned(proj, dim, cosine, sine):
+    if cosine is None:
+        return proj
+    lane = lax.broadcasted_iota(jnp.int32, proj.shape, 1)
+    ahead = pltpu.roll(proj, proj.shape[1] - dim // 2, 1)
+    behind = pltpu.roll(proj, dim // 2, 1)
+    return proj * cosine[...] + jnp.where(lax.rem(lane, dim) < dim // 2, -ahead, behind) * sine[...]
+
+
+def normed(h, gain, layer):
+    rows32 = h.astype(F32)
+    centered = rows32 - rows32.mean(axis=-1, keepdims=True)
+    variance = (centered * centered).mean(axis=-1, keepdims=True)
+    return centered * lax.rsqrt(variance + NORM_EPS) * gain[...].astype(F32)[layer:layer + 1]
+
+
+def over_rows(u, mats, at_once=8):
+    def block(i, sums):
+        rows = lanes(i * at_once, at_once)
+        return tuple(t + jnp.dot(u[:, rows], m[rows, :], preferred_element_type=F32) for t, m in zip(sums, mats))
+
+    return lax.fori_loop(0, u.shape[1] // (at_once * UNIT), block, tuple(jnp.zeros((u.shape[0], m.shape[1]), F32) for m in mats))
+
+
+def rounded(proj):
+    return proj.astype(BF16).astype(F32)
+
+
+def heads_out(ref, row, dim):
+    for head in range(ref.shape[0]):
+        ref[head:head + 1, :] = row[0:1, head * dim:(head + 1) * dim]
+
+
+def sum_front_body(layer, dim, n_turns, part_ref, h_ref, gain, *refs):
+    cosine, sine = refs[:n_turns] or (None, None)
+    sources, (h_out, q_out, new_out, mlp_out), refs = refs[n_turns:n_turns + 6], refs[n_turns + 6:n_turns + 10], refs[n_turns + 10:]
+    wq, wk, wv, wg, wu, wd, slots, u, gate, up, sems, send_sems, recv_sems = refs
+    peers = greet("tp")
+    small = [pltpu.make_async_copy(src.at[layer], dst, sems.at[i, 0]) for i, (src, dst) in enumerate(zip(sources[:3], (wq, wk, wv)))]
+    for copy in small:
+        copy.start()
+    steps = sems.shape[1]
+    depth = wg.shape[0] // steps
+
+    def piece(which, i):
+        rows = pl.ds(pl.multiple_of(i * depth, depth), depth)
+        return pltpu.make_async_copy(sources[which].at[layer, rows], (wg, wu, wd)[which - 3].at[rows], sems.at[which, i])
+
+    def begin(i, carry):
+        piece(3, i).start()
+        piece(4, i).start()
+        return carry
+
+    def begin_down(i, carry):
+        piece(5, i).start()
+        return carry
+
+    lax.fori_loop(0, steps, begin, 0)
+    lax.fori_loop(0, steps, begin_down, 0)
+    h = settled_sum(share(peers, part_ref, slots, send_sems, recv_sems), part_ref, slots, h_ref[...])
+    h_out[...] = h
+    u[...] = jnp.broadcast_to(normed(h, gain, layer), u.shape).astype(BF16)
+    gate[...] = jnp.zeros_like(gate)
+    up[...] = jnp.zeros_like(up)
+    for copy in small:
+        copy.wait()
+    query, key_new, value_new = over_rows(u, (wq, wk, wv), 4)
+    key_new = turned(key_new, dim, cosine, sine)
+    heads_out(new_out.at[0], rounded(key_new), dim)
+    heads_out(new_out.at[1], rounded(value_new), dim)
+    width = key_new.shape[1]
+    for j in range(q_out.shape[0]):
+        heads_out(q_out.at[j], rounded(turned(query[:, j * width:(j + 1) * width], dim, cosine, sine)), dim)
+
+    def widen(i, carry):
+        piece(3, i).wait()
+        piece(4, i).wait()
+        rows = pl.ds(pl.multiple_of(i * depth, depth), depth)
+        gate[...] += jnp.dot(u[:, rows], wg[rows, :], preferred_element_type=F32)
+        up[...] += jnp.dot(u[:, rows], wu[rows, :], preferred_element_type=F32)
+        return carry
+
+    lax.fori_loop(0, steps, widen, 0)
+    u[...] = (jax.nn.silu(gate[...]) * up[...]).astype(BF16)
+    gate[...] = jnp.zeros_like(gate)
+
+    def narrow(i, carry):
+        piece(5, i).wait()
+        rows = pl.ds(pl.multiple_of(i * depth, depth), depth)
+        gate[...] += jnp.dot(u[:, rows], wd[rows, :], preferred_element_type=F32)
+        return carry
+
+    lax.fori_loop(0, steps, narrow, 0)
+    mlp_out[...] = gate[0:1, :]
+
+
+def sum_front(layer, dim, part, residual, ln_gain, turns, *weights):
+    width = residual.shape[1]
+    q_width, kv_width = weights[0].shape[2], weights[1].shape[2]
+    wide = pltpu.VMEM((8, width), F32)
+    return pl.pallas_call(
+        functools.partial(sum_front_body, layer, dim, len(turns)),
+        in_specs=[VMEM] * (3 + len(turns)) + [HBM] * 6,
+        out_specs=[VMEM] * 4,
+        out_shape=[
+            jax.ShapeDtypeStruct((1, width), BF16),
+            jax.ShapeDtypeStruct((FFN_STEPS, q_width // FFN_STEPS // dim, dim), F32),
+            jax.ShapeDtypeStruct((2, kv_width // dim, dim), F32),
+            jax.ShapeDtypeStruct((1, width), F32),
+        ],
+        scratch_shapes=[pltpu.VMEM(w.shape[1:], BF16) for w in weights]
+        + [pltpu.VMEM((3,) + part.shape, F32), pltpu.VMEM((8, width), BF16), wide, wide, pltpu.SemaphoreType.DMA((6, 8)), pltpu.SemaphoreType.DMA((3,)), pltpu.SemaphoreType.DMA((3,))],
         compiler_params=pltpu.CompilerParams(collective_id=layer, has_side_effects=True),
-        cost_estimate=cost(12 * part.size),
-        name="tp_sum",
-    )(part, residual)
+        cost_estimate=cost(2 * sum(w[0].size for w in weights)),
+        name="sum_front",
+    )(part, residual, ln_gain, *turns, *weights)
 
 
 def front_body(layer, dim, h_ref, gain, cosine, sine, wq, wk, wv, wg, wu, wd, q_out, new_out, mlp_out, u, acc):
     step = pl.program_id(0)
 
-    def turn(proj):
-        if cosine is None:
-            return proj
-        width = proj.shape[1]
-        lane = lax.broadcasted_iota(jnp.int32, proj.shape, 1)
-        ahead = pltpu.roll(proj, width - dim // 2, 1)
-        behind = pltpu.roll(proj, dim // 2, 1)
-        swapped = jnp.where(lax.rem(lane, dim) < dim // 2, -ahead, behind)
-        return proj * cosine[...] + swapped * sine[...]
-
-    def over_rows(mats):
-        depth = 8 * UNIT
-
-        def block(i, sums):
-            rows = lanes(i * 8, 8)
-            return tuple(t + jnp.dot(u[:, rows], m[0, rows, :], preferred_element_type=F32) for t, m in zip(sums, mats))
-
-        return lax.fori_loop(0, u.shape[1] // depth, block, tuple(jnp.zeros((u.shape[0], m.shape[2]), F32) for m in mats))
-
-    def rounded(proj):
-        return proj.astype(BF16).astype(F32)
-
     @pl.when(step == 0)
     def _():
-        rows32 = h_ref[...].astype(F32)
-        centered = rows32 - rows32.mean(axis=-1, keepdims=True)
-        variance = (centered * centered).mean(axis=-1, keepdims=True)
-        scaled = centered * lax.rsqrt(variance + NORM_EPS) * gain[...].astype(F32)[layer:layer + 1]
-        u[...] = jnp.broadcast_to(scaled, u.shape).astype(BF16)
+        u[...] = jnp.broadcast_to(normed(h_ref[...], gain, layer), u.shape).astype(BF16)
         acc[...] = jnp.zeros_like(acc)
-        both = over_rows((wk, wv))
-        key_new, value_new = rounded(turn(both[0])), rounded(both[1])
-        for part, new in ((0, key_new), (1, value_new)):
-            for head in range(new_out.shape[1]):
-                new_out[part, head:head + 1, :] = new[0:1, head * dim:(head + 1) * dim]
-
-    query, gate, up = over_rows((wq, wg, wu))
-    query = rounded(turn(query))
-    for head in range(q_out.shape[1]):
-        q_out[0, head:head + 1, :] = query[0:1, head * dim:(head + 1) * dim]
+        key_new, value_new = over_rows(u, (wk.at[0], wv.at[0]))
+        heads_out(new_out.at[0], rounded(turned(key_new, dim, cosine, sine)), dim)
+        heads_out(new_out.at[1], rounded(value_new), dim)
+
+    query, gate, up = over_rows(u, (wq.at[0], wg.at[0], wu.at[0]))
+    heads_out(q_out.at[0], rounded(turned(query, dim, cosine, sine)), dim)
     active = (jax.nn.silu(gate) * up).astype(BF16)
 
     def down(i, carry):
@@ -516,10 +579,6 @@
     @pl.when(step == FFN_STEPS - 1)
     def _():
         mlp_out[...] = acc[0:1, :]
-
-
-def plain_front_body(layer, dim, h_ref, gain, *refs):
-    front_body(layer, dim, h_ref, gain, None, None, *refs)
 
 
 def front(layer, dim, residual, ln_gain, turns, w_query, w_key, w_value, w_gate, w_up, w_down):
@@ -529,9 +588,8 @@
     whole = lambda *shape: pl.BlockSpec(shape, lambda j: (0,) * len(shape))
     col = lambda rows, cols: pl.BlockSpec((1, rows, cols), lambda j: (layer, 0, j))
     fixed = lambda rows, cols: pl.BlockSpec((1, rows, cols), lambda j: (layer, 0, 0))
-    body = front_body if turns else plain_front_body
     return pl.pallas_call(
-        functools.partial(body, layer, dim),
+        functools.partial(front_body, layer, dim),
         grid=(FFN_STEPS,),
         in_specs=[whole(1, width), whole(*ln_gain.shape)] + [whole(1, kv_width)] * len(turns)
         + [col(width, q_step), fixed(width, kv_width), fixed(width, kv_width), col(width, ffn_step), col(width, ffn_step), pl.BlockSpec((1, ffn_step, width), lambda j: (layer, j, 0))],
@@ -612,7 +670,7 @@
             for layer in range(n_layers):
                 sliding = layer < final
                 if layer:
-                    q, new_kv, mlp = front(layer, dim, residual, ln_gain, turns if sliding else (), *weights)
+                    residual, q, new_kv, mlp = sum_front(layer, dim, part, residual, ln_gain, turns if sliding else (), *weights)
                 if layer == 1:
                     cuts = after([block(t, final, r) for t in (k_t, v_t) for r in (2, 3)], q)
                     late = [swap(c, "sp", 2 + i % 2) for i, c in enumerate(cuts)]
@@ -620,14 +678,12 @@
                     if layer and size < 2 * half:
                         pipes[layer].append(swap(after(pipes[layer][0], q), "sp", 1))
                     part, k_win, v_win = attend_window(layer, size if layer else None, ids, q, new_kv, mlp, w_out, k_t, v_t, nears, pipes[layer], k_win, v_win)
-                    residual = tp_sum(layer, part, residual)
                 else:
                     k_glob, v_glob = fresh_buffers([(heads, dim, n_sp * shard)] * 2)
-                    residual = spread(layer, ids, q, new_kv, mlp, residual, w_out, k_t, v_t)
-                    k_glob = place(final, 0, (0,) + PEERS, ids, new_kv, k_t, nears[0], late[:2], k_glob)
-                    ids = after(ids, k_glob)
+                    attn, last, k_glob = score_global(layer, ids, q, new_kv, k_t, nears[0], late[:2], k_glob)
+                    ids = after(ids, attn)
                     v_glob = place(final, 1, (0, 1, 2), ids, new_kv, v_t, nears[1], late[2:3], v_glob)
-                    v_glob = place(final, 1, (3,), ids, new_kv, v_t, nears[1], late[3:], v_glob)
+                    residual, v_glob = finish(layer, ids, attn, last, new_kv, mlp, residual, w_out, v_t, nears[1], late[2:], v_glob)
             return residual, k_win, v_win, k_glob, v_glob
 
         if len(SIZES) == 1:

time: 234 us -> 217 us (0.927)
  Pallas kernels: 128 us -> 96.6 us
  waiting for transfers between devices: 73.3 us -> 84.4 us
  local copies, waits for them, and re-layouts: 8.4 us -> 11.5 us
    pallas_call x8 -> x6, Pallas kernels: 94.8 us -> 69.7 us  [the longest x3 42.1 us: sum_front(): pl.pallas_call(functools.partial(sum_front_body, layer, dim, len(turns)),...]
    ppermute x16, waiting for transfers between devices: 73.3 us -> 84.4 us  [swap(): return lax.ppermute(t, axis, [(i, i ^ relation) for i in range(n_sp)])]
    pallas_call x3 -> x1, Pallas kernels: 9.09 us -> 3.04 us  [place(): pl.pallas_call(functools.partial(place_body, layer, part, relations), in_...]
    unnamed x7 -> x8, local copies, waits for them, and re-layouts: 0.61 us -> 3.71 us
  transfers between devices with their start and end apart: 16 -> 16, of which waited for: 4 -> 6; matrix products, arithmetic and copies ran while one was open for 3% -> 4% of each run, Pallas kernels for 52% -> 39%
where the time goes in v3:
time: 217 us; the launch traced here: 216 us
  Pallas kernels  96.6 us (45%)
  waiting for transfers between devices  84.4 us (39%)
  starting transfers between devices  13.3 us (6%)
  local copies, waits for them, and re-layouts  11.5 us (5%)
  blocking collectives  4.89 us (2%)
  between operations  3.32 us (2%)
    ppermute x16, waiting for transfers between devices, swap(): return lax.ppermute(t, axis, [(i, i ^ relation) for i in range(n_sp)])  84.4 us
    pallas_call x3, Pallas kernels, sum_front(): pl.pallas_call(functools.partial(sum_front_body, layer, dim, len(turns)),...  42.1 us
    pallas_call x3, Pallas kernels, attend_window(): pl.pallas_call(functools.partial(window_body, layer, size, half, n_pipe),...  18.1 us
    ppermute x16, starting transfers between devices, swap(): return lax.ppermute(t, axis, [(i, i ^ relation) for i in range(n_sp)])  13.3 us
    pallas_call x1, Pallas kernels, front(): pl.pallas_call(functools.partial(front_body, layer, dim), grid=(FFN_STEPS...  12.7 us
    pallas_call x1, Pallas kernels, finish(): pl.pallas_call(functools.partial(finish_body, layer), in_specs=[SMEM] + [...  9.75 us
    squeeze x3, local copies, waits for them, and re-layouts, block(): lax.dynamic_slice(t, (layer, jnp.bitwise_xor(me, relation), 0, 0, 0), (1,...  6.32 us
    pallas_call x2, Pallas kernels, pack(): pl.pallas_call(functools.partial(pack_body, layer, size, half), in_specs=...  5.8 us
  transfers between devices with their start and end apart: 16, of which 6 were waited for; matrix products, arithmetic and copies ran while one was open for 4% of the time, Pallas kernels for 39%

profile of v3, /device:TPU:0, one launch (start us, length us, event | category | flops | bytes accessed | tf_op | source)
XLA Modules:
  0.0 215.7 jit_solution(1686310065490640181)
XLA Ops:
  0.7 0.6 collective-permute-start.42
  1.2 0.1 collective-permute-start.43
  1.3 1.3 dynamic-slice_bitcast_fusion.17
  2.6 3.0 %collective-permute-start.44 = (bf16[2,64,2048]{2,1,0:T(8,128)(2,1)S(1)}, bf16[2,64,2048]{2,1,0:T(8,128)(2,1)}, u32[]{:S(2)}, u32[]{:S(2)}) collective-permute-start(bf16[2,64,2048]{2,1,0:T(8,128)(2,1)S(1)} %get-tuple-element.498), channel_id=1, source_target_pairs={{0,2},{1,3},{2,0},{3,1},{4,6},{5,7},{6,4},{7,5},{8,10},{9,11},{10,... | collective-permute-start | bytes 1572872 | tf_op jit(solution)/shard_map/ppermute | solution.py:629
  5.6 2.1 dynamic-slice_bitcast_fusion.16
  7.7 1.4 collective-permute-start.46
  9.1 0.1 reshape.42
  9.2 0.1 reduce_sum.9
  9.3 0.6 fusion
  10.0 4.9 %pmax.7 = s32[]{:T(128)} all-reduce(s32[]{:T(128)} %fusion), channel_id=1, replica_groups=mesh['dp'=2,'tp'=4,'sp'=4] {'dp'}, use_global_device_ids=true, to_apply=%region_2.3 | all-reduce | flops 1 | bytes 8 | tf_op jit(solution)/shard_map/pmax | solution.py:647
  14.9 0.6 dynamic_slice.64
  16.1 0.1 fusion.1
  16.2 0.1 tile.21.sine
  16.3 0.1 tile.9.cosine
  18.3 12.7 %front.1 = (f32[4,2,64]{2,1,0:T(2,128)S(1)}, f32[2,2,64]{2,1,0:T(2,128)S(1)}, f32[1,2048]{1,0:T(1,128)S(1)}) custom-call(bf16[1,2048]{1,0:T(2,128)(2,1)S(1)} %copy-done.7, bf16[4,2048]{1,0:T(4,128)(2,1)S(1)} %copy-done.4, f32[1,128]{1,0:T(1,128)S(1)} %tile.9.cosine, f32[1,128]{1,0:T(1,128)S(1)} %tile.21.sine, bf16[4,2048,512]{2,1,0:T(8,128)(2,1)} %wq.1, ...), custom_call_target="tpu_custom_call" | custom-call | flops 28311552 | bytes 28311552 | tf_op jit(solution)/shard_map/front/pallas_call | solution.py:591
  31.1 0.1 pad_add_fusion
  31.2 9.2 %collective-permute-done.46 = bf16[2,64,2048]{2,1,0:T(8,128)(2,1)} collective-permute-done((bf16[2,64,2048]{2,1,0:T(8,128)(2,1)S(1)}, bf16[2,64,2048]{2,1,0:T(8,128)(2,1)}, u32[]{:S(2)}, u32[]{:S(2)}) %collective-permute-start.46) | collective-permute-done | bytes 524320 | tf_op jit(solution)/shard_map/ppermute | solution.py:629
  40.3 171.7 %conditional.1 = (bf16[1,2048]{1,0:T(2,128)(2,1)S(1)}, bf16[3,2,64,4096]{3,2,1,0:T(8,128)(2,1)}, bf16[3,2,64,4096]{3,2,1,0:T(8,128)(2,1)}, bf16[2,64,8192]{2,1,0:T(8,128)(2,1)}, bf16[2,64,8192]{2,1,0:T(8,128)(2,1)}) conditional(s32[]{:T(128)} %clamp.3, (bf16[2,64,2048]{2,1,0:T(8,128)(2,1)}, s32[5]{0:T(128)S(1)}, ...), branch_computations={%region_3.4_spmd, %region_4.5_spmd, %region_5.6_spmd, %region_6.7_... | conditional | flops 117440512 | bytes 169869920 | solution.py:692
  40.3 2.9 %pack.8 = (bf16[2,2,64,2048]{3,2,1,0:T(8,128)(2,1)}, bf16[2,2,64,256]{3,2,1,0:T(8,128)(2,1)}) custom-call(s32[5]{0:T(128)S(1)} %get-tuple-element.245.ids, bf16[4,4,2,64,2048]{4,3,2,1,0:T(8,128)(2,1)} %get-tuple-element.197.k_own.own, bf16[4,4,2,64,2048]{4,3,2,1,0:T(8,128)(2,1)} %get-tuple-element.198.v_own.own, ...), custom_call_target="tpu_custom_call" | custom-call | flops 2359296 | bytes 2359296 | tf_op jit(solution)/shard_map/cond/branch_0_fun/pack/pallas_call | solution.py:90
  43.2 1.8 collective-permute-start.1
  45.0 33.4 %collective-permute-done.refs_3_ = bf16[2,64,2048]{2,1,0:T(8,128)(2,1)} collective-permute-done((bf16[2,64,2048]{2,1,0:T(8,128)(2,1)}, bf16[2,64,2048]{2,1,0:T(8,128)(2,1)}, u32[]{:S(2)}, u32[]{:S(2)}) %collective-permute-start) | collective-permute-done | bytes 524320 | tf_op jit(solution)/shard_map/cond/branch_0_fun/ppermute | solution.py:629
  78.4 5.6 %attend_window.12 = (f32[1,2048]{1,0:T(1,128)}, bf16[3,2,64,4096]{3,2,1,0:T(8,128)(2,1)S(1)}, bf16[3,2,64,4096]{3,2,1,0:T(8,128)(2,1)}) custom-call(s32[5]{0:T(128)S(1)} %get-tuple-element.245.ids, f32[4,2,64]{2,1,0:T(2,128)S(1)} %get-tuple-element.193.q_ref, ...), custom_call_target="tpu_custom_call", output_to_operand_aliasing={{1}: (13, {}), {2}: (14, {})} | custom-call | flops 4194304 | bytes 4194304 | tf_op jit(solution)/shard_map/cond/branch_0_fun/attend_window/pallas_call | solution.py:249
  84.0 14.3 %sum_front.12 = (bf16[1,2048]{1,0:T(2,128)(2,1)}, f32[4,2,64]{2,1,0:T(2,128)}, f32[2,2,64]{2,1,0:T(2,128)}, f32[1,2048]{1,0:T(1,128)}) custom-call(f32[1,2048]{1,0:T(1,128)} %get-tuple-element.207.part_ref, bf16[1,2048]{1,0:T(2,128)(2,1)S(1)} %get-tuple-element.208.h_ref, bf16[4,2048]{1,0:T(4,128)(2,1)S(1)} %get-tuple-element.209.gain, ...), custom_call_target="tpu_custom_call" | custom-call | flops 28311552 | bytes 28311552 | tf_op jit(solution)/shard_map/cond/branch_0_fun/sum_front/pallas_call | solution.py:539
  98.3 0.1 collective-permute-start.3
  98.4 2.9 %pack.9 = (bf16[2,2,64,2048]{3,2,1,0:T(8,128)(2,1)}, bf16[2,2,64,256]{3,2,1,0:T(8,128)(2,1)}) custom-call(s32[5]{0:T(128)S(1)} %get-tuple-element.245.ids, bf16[4,4,2,64,2048]{4,3,2,1,0:T(8,128)(2,1)} %get-tuple-element.197.k_own.own, bf16[4,4,2,64,2048]{4,3,2,1,0:T(8,128)(2,1)} %get-tuple-element.198.v_own.own, ...), custom_call_target="tpu_custom_call" | custom-call | flops 2359296 | bytes 2359296 | tf_op jit(solution)/shard_map/cond/branch_0_fun/pack/pallas_call | solution.py:90
  101.3 1.1 collective-permute-start.4
  102.4 1.0 collective-permute-start.2
  103.4 26.5 %collective-permute-done.2.refs_1_ = bf16[2,2,64,256]{3,2,1,0:T(8,128)(2,1)S(1)} collective-permute-done((bf16[2,2,64,256]{3,2,1,0:T(8,128)(2,1)S(1)}, bf16[2,2,64,256]{3,2,1,0:T(8,128)(2,1)S(1)}, u32[]{:S(2)}, u32[]{:S(2)}) %collective-permute-start.2) | collective-permute-done | bytes 131104 | tf_op jit(solution)/shard_map/cond/branch_0_fun/ppermute | solution.py:629
  130.0 0.7 copy-done.9
  130.6 6.2 %attend_window.13 = (f32[1,2048]{1,0:T(1,128)}, bf16[3,2,64,4096]{3,2,1,0:T(8,128)(2,1)S(1)}, bf16[3,2,64,4096]{3,2,1,0:T(8,128)(2,1)}) custom-call(s32[5]{0:T(128)S(1)} %get-tuple-element.245.ids, f32[4,2,64]{2,1,0:T(2,128)} %get-tuple-element.218.q_ref, f32[2,2,64]{2,1,0:T(2,128)} %get-tuple-element.219.new_ref, ...), custom_call_target="tpu_custom_call", output_to_operand_aliasing={{1}: (12, {}), {2}: (13, {})} | custom-call | flops 4194304 | bytes 4194304 | tf_op jit(solution)/shard_map/cond/branch_0_fun/attend_window/pallas_call | solution.py:249
  136.9 13.9 %sum_front.13 = (bf16[1,2048]{1,0:T(2,128)(2,1)}, f32[4,2,64]{2,1,0:T(2,128)}, f32[2,2,64]{2,1,0:T(2,128)}, f32[1,2048]{1,0:T(1,128)}) custom-call(f32[1,2048]{1,0:T(1,128)} %get-tuple-element.226.part_ref, bf16[1,2048]{1,0:T(2,128)(2,1)} %get-tuple-element.227.h_ref, bf16[4,2048]{1,0:T(4,128)(2,1)S(1)} %get-tuple-element.209.gain, ...), custom_call_target="tpu_custom_call" | custom-call | flops 28311552 | bytes 28311552 | tf_op jit(solution)/shard_map/cond/branch_0_fun/sum_front/pallas_call | solution.py:539
  150.8 0.1 collective-permute-start.6
  150.9 0.7 collective-permute-start.5
  151.6 2.9 %dynamic-slice_bitcast_fusion = (bf16[2,64,2048]{2,1,0:T(8,128)(2,1)}, bf16[2,64,2048]{2,1,0:T(8,128)(2,1)}, bf16[2,64,2048]{2,1,0:T(8,128)(2,1)}, bf16[2,64,2048]{2,1,0:T(8,128)(2,1)}) fusion(bf16[4,4,2,64,2048]{4,3,2,1,0:T(8,128)(2,1)} %get-tuple-element.198.v_own.own, s32[]{:T(128)S(6)} %select_n.36, s32[]{:T(128)S(6)} %select_n.35, ...), kind=kLoop, calls=%fused_computation | loop fusion | bytes 4194312 | tf_op jit(solution)/shard_map/cond/branch_0_fun/squeeze | solution.py:651
  154.6 1.4 collective-permute-start.7
  155.9 0.1 collective-permute-start.8
  156.1 1.4 collective-permute-start.9
  157.4 0.6 collective-permute-start.10
  158.1 6.2 %attend_window.14 = (f32[1,2048]{1,0:T(1,128)}, bf16[3,2,64,4096]{3,2,1,0:T(8,128)(2,1)S(1)}, bf16[3,2,64,4096]{3,2,1,0:T(8,128)(2,1)}) custom-call(s32[5]{0:T(128)S(1)} %get-tuple-element.245.ids, f32[4,2,64]{2,1,0:T(2,128)} %get-tuple-element.228.q_ref, f32[2,2,64]{2,1,0:T(2,128)} %get-tuple-element.229.new_ref, ...), custom_call_target="tpu_custom_call", output_to_operand_aliasing={{1}: (12, {}), {2}: (13, {})} | custom-call | flops 4194304 | bytes 4194304 | tf_op jit(solution)/shard_map/cond/branch_0_fun/attend_window/pallas_call | solution.py:249
  164.3 13.9 %sum_front.14 = (bf16[1,2048]{1,0:T(2,128)(2,1)}, f32[4,2,64]{2,1,0:T(2,128)}, f32[2,2,64]{2,1,0:T(2,128)}, f32[1,2048]{1,0:T(1,128)}) custom-call(f32[1,2048]{1,0:T(1,128)} %get-tuple-element.236.part_ref, bf16[1,2048]{1,0:T(2,128)(2,1)} %get-tuple-element.237.h_ref, bf16[4,2048]{1,0:T(4,128)(2,1)S(1)} %get-tuple-element.209.gain, ...), custom_call_target="tpu_custom_call" | custom-call | flops 28311552 | bytes 28311552 | tf_op jit(solution)/shard_map/cond/branch_0_fun/sum_front/pallas_call | solution.py:539
  178.2 1.6 collective-permute-done.8.cross
  179.8 5.1 %scores.4 = (bf16[8,8192]{1,0:T(8,128)(2,1)}, f32[8,128]{1,0:T(8,128)}, bf16[2,64,8192]{2,1,0:T(8,128)(2,1)}) custom-call(s32[5]{0:T(128)S(1)} %get-tuple-element.245.ids, f32[4,2,64]{2,1,0:T(2,128)} %get-tuple-element.238.q_ref, f32[2,2,64]{2,1,0:T(2,128)} %get-tuple-element.239.new_ref, ...), custom_call_target="tpu_custom_call", output_to_operand_aliasing={{2}: (7, {})} | custom-call | flops 4194304 | bytes 4194304 | tf_op jit(solution)/shard_map/cond/branch_0_fun/scores/pallas_call | solution.py:340
  184.9 7.2 %collective-permute-done.9.refs_0_.far = bf16[2,64,2048]{2,1,0:T(8,128)(2,1)} collective-permute-done((bf16[2,64,2048]{2,1,0:T(8,128)(2,1)}, bf16[2,64,2048]{2,1,0:T(8,128)(2,1)}, u32[]{:S(2)}, u32[]{:S(2)}) %collective-permute-start.9) | collective-permute-done | bytes 524320 | tf_op jit(solution)/shard_map/cond/branch_0_fun/ppermute | solution.py:629
  192.2 3.0 %place.4.v_in = bf16[2,64,8192]{2,1,0:T(8,128)(2,1)} custom-call(s32[5]{0:T(128)S(1)} %get-tuple-element.245.ids, f32[2,2,64]{2,1,0:T(2,128)} %get-tuple-element.239.new_ref, bf16[4,4,2,64,2048]{4,3,2,1,0:T(8,128)(2,1)} %get-tuple-element.198.v_own.own, bf16[4,4,2,64,2048]{4,3,2,1,0:T(8,128)(2,1)} %get-tuple-element.200.v_near.near, ...), custom_call_target="tpu_custom_call", output_to_operand_aliasing={{}: (5, {})} | custom-call | flops 3145728 | bytes 3145728 | tf_op jit(solution)/shard_map/cond/branch_0_fun/place/pallas_call | solution.py:297
  195.2 6.5 %collective-permute-done.10.cross = bf16[2,64,2048]{2,1,0:T(8,128)(2,1)} collective-permute-done((bf16[2,64,2048]{2,1,0:T(8,128)(2,1)}, bf16[2,64,2048]{2,1,0:T(8,128)(2,1)}, u32[]{:S(2)}, u32[]{:S(2)}) %collective-permute-start.10) | collective-permute-done | bytes 524320 | tf_op jit(solution)/shard_map/cond/branch_0_fun/ppermute | solution.py:629
  201.8 9.7 %finish.4 = (bf16[1,2048]{1,0:T(2,128)(2,1)S(1)}, bf16[2,64,8192]{2,1,0:T(8,128)(2,1)}) custom-call(s32[5]{0:T(128)S(1)} %get-tuple-element.245.ids, bf16[8,8192]{1,0:T(8,128)(2,1)} %get-tuple-element.244.w_ref, f32[8,128]{1,0:T(8,128)} %get-tuple-element.246.last_ref, f32[2,2,64]{2,1,0:T(2,128)} %get-tuple-element.239.new_ref, ...), custom_call_target="tpu_custom_call", output_to_operand_aliasing={{1}: (11, {})} | custom-call | flops 4194304 | bytes 4194304 | tf_op jit(solution)/shard_map/cond/branch_0_fun/finish/pallas_call | solution.py:417
  212.0 0.6 copy.111
  212.6 3.1 %copy.112 = bf16[1,2,8192,64]{2,3,1,0:T(8,128)(2,1)} copy(bf16[1,2,8192,64]{2,3,1,0:T(8,128)(2,1)} %bitcast.35) | data formatting | bytes 4194304
  (32 shorter events, 0.1 us)
Async XLA Ops:
  0.6 8.5 %copy-start.12 = (s32[4]{0:T(128)S(1)}, s32[4]{0:T(128)}, u32[]{:S(2)}) copy-start(s32[4]{0:T(128)} %param.18) | copy-start | bytes 52
  0.6 17.7 %copy-start.7 = (bf16[1,2048]{1,0:T(2,128)(2,1)S(1)}, bf16[1,2048]{1,0:T(2,128)(2,1)}, u32[]{:S(2)}) copy-start(bf16[1,2048]{1,0:T(2,128)(2,1)} %h_ref.1) | copy-start | bytes 12292
  0.7 17.7 %copy-start.4 = (bf16[4,2048]{1,0:T(4,128)(2,1)S(1)}, bf16[4,2048]{1,0:T(4,128)(2,1)}, u32[]{:S(2)}) copy-start(bf16[4,2048]{1,0:T(4,128)(2,1)} %gain.1) | copy-start | bytes 49156
  0.7 39.7 %collective-permute-start.42 = (bf16[4,4,2,64,2048]{4,3,2,1,0:T(8,128)(2,1)}, bf16[4,4,2,64,2048]{4,3,2,1,0:T(8,128)(2,1)}, u32[]{:S(2)}, u32[]{:S(2)}) collective-permute-start(bf16[4,4,2,64,2048]{4,3,2,1,0:T(8,128)(2,1)} %bitcast.69), channel_id=1, source_target_pairs={{0,1},{1,0},{2,3},{3,2},{4,5},{5,4},{6,7},{7,6},{8,9},{9,8},{10,11... | collective-permute-start | bytes 25165832 | tf_op jit(solution)/shard_map/ppermute | solution.py:629
  1.2 39.1 %collective-permute-start.43 = (bf16[4,4,2,64,2048]{4,3,2,1,0:T(8,128)(2,1)}, bf16[4,4,2,64,2048]{4,3,2,1,0:T(8,128)(2,1)}, u32[]{:S(2)}, u32[]{:S(2)}) collective-permute-start(bf16[4,4,2,64,2048]{4,3,2,1,0:T(8,128)(2,1)} %bitcast.64), channel_id=1, source_target_pairs={{0,1},{1,0},{2,3},{3,2},{4,5},{5,4},{6,7},{7,6},{8,9},{9,8},{10,11... | collective-permute-start | bytes 25165832 | tf_op jit(solution)/shard_map/ppermute | solution.py:629
  2.6 28.6 %collective-permute-start.44 = (bf16[2,64,2048]{2,1,0:T(8,128)(2,1)S(1)}, bf16[2,64,2048]{2,1,0:T(8,128)(2,1)}, u32[]{:S(2)}, u32[]{:S(2)}) collective-permute-start(bf16[2,64,2048]{2,1,0:T(8,128)(2,1)S(1)} %get-tuple-element.498), channel_id=1, source_target_pairs={{0,2},{1,3},{2,0},{3,1},{4,6},{5,7},{6,4},{7,5},{8,10},{9,11},{10,... | collective-permute-start | bytes 1572872 | tf_op jit(solution)/shard_map/ppermute | solution.py:629
  5.6 25.6 %collective-permute-start.45 = (bf16[2,64,2048]{2,1,0:T(8,128)(2,1)S(1)}, bf16[2,64,2048]{2,1,0:T(8,128)(2,1)}, u32[]{:S(2)}, u32[]{:S(2)}) collective-permute-start(bf16[2,64,2048]{2,1,0:T(8,128)(2,1)S(1)} %get-tuple-element.497), channel_id=1, source_target_pairs={{0,3},{1,2},{2,1},{3,0},{4,7},{5,6},{6,5},{7,4},{8,11},{9,10},{10,... | collective-permute-start | bytes 1572872 | tf_op jit(solution)/shard_map/ppermute | solution.py:629
  7.7 32.6 %collective-permute-start.46 = (bf16[2,64,2048]{2,1,0:T(8,128)(2,1)S(1)}, bf16[2,64,2048]{2,1,0:T(8,128)(2,1)}, u32[]{:S(2)}, u32[]{:S(2)}) collective-permute-start(bf16[2,64,2048]{2,1,0:T(8,128)(2,1)S(1)} %get-tuple-element.495), channel_id=1, source_target_pairs={{0,2},{1,3},{2,0},{3,1},{4,6},{5,7},{6,4},{7,5},{8,10},{9,11},{10,... | collective-permute-start | bytes 1572872 | tf_op jit(solution)/shard_map/ppermute | solution.py:629
  43.2 55.1 %collective-permute-start.1 = (bf16[2,2,64,2048]{3,2,1,0:T(8,128)(2,1)}, bf16[2,2,64,2048]{3,2,1,0:T(8,128)(2,1)}, u32[]{:S(2)}, u32[]{:S(2)}) collective-permute-start(bf16[2,2,64,2048]{3,2,1,0:T(8,128)(2,1)} %get-tuple-element.221), channel_id=1, source_target_pairs={{0,2},{1,3},{2,0},{3,1},{4,6},{5,7},{6,4},{7,5},{8,10},{9,11},{10,... | collective-permute-start | bytes 3145736 | tf_op jit(solution)/shard_map/cond/branch_0_fun/ppermute | solution.py:629
  45.0 33.4 %collective-permute-start = (bf16[2,64,2048]{2,1,0:T(8,128)(2,1)}, bf16[2,64,2048]{2,1,0:T(8,128)(2,1)}, u32[]{:S(2)}, u32[]{:S(2)}) collective-permute-start(bf16[2,64,2048]{2,1,0:T(8,128)(2,1)} %get-tuple-element.204), channel_id=1, source_target_pairs={{0,3},{1,2},{2,1},{3,0},{4,7},{5,6},{6,5},{7,4},{8,11},{9,10},{10,... | collective-permute-start | bytes 1572872 | tf_op jit(solution)/shard_map/cond/branch_0_fun/ppermute | solution.py:629
  98.3 4.1 %copy-start.11 = (bf16[2,2,64,256]{3,2,1,0:T(8,128)(2,1)S(1)}, bf16[2,2,64,256]{3,2,1,0:T(8,128)(2,1)}, u32[]{:S(2)}) copy-start(bf16[2,2,64,256]{3,2,1,0:T(8,128)(2,1)} %get-tuple-element.222) | copy-start | bytes 393220 | tf_op jit(solution)/shard_map/cond
  98.3 31.6 %collective-permute-start.3 = (bf16[2,2,64,2048]{3,2,1,0:T(8,128)(2,1)}, bf16[2,2,64,2048]{3,2,1,0:T(8,128)(2,1)}, u32[]{:S(2)}, u32[]{:S(2)}) collective-permute-start(bf16[2,2,64,2048]{3,2,1,0:T(8,128)(2,1)} %collective-permute-done.1.refs_0_), channel_id=1, source_target_pairs={{0,1},{1,0},{2,3},{3,2},{4,5},{5,4},{6,7},{7,6},{8,9},{9,8},{10,11... | collective-permute-start | bytes 3145736 | tf_op jit(solution)/shard_map/cond/branch_0_fun/ppermute | solution.py:629
  101.3 49.5 %collective-permute-start.4 = (bf16[2,2,64,2048]{3,2,1,0:T(8,128)(2,1)}, bf16[2,2,64,2048]{3,2,1,0:T(8,128)(2,1)}, u32[]{:S(2)}, u32[]{:S(2)}) collective-permute-start(bf16[2,2,64,2048]{3,2,1,0:T(8,128)(2,1)} %get-tuple-element.231), channel_id=1, source_target_pairs={{0,2},{1,3},{2,0},{3,1},{4,6},{5,7},{6,4},{7,5},{8,10},{9,11},{10,... | collective-permute-start | bytes 3145736 | tf_op jit(solution)/shard_map/cond/branch_0_fun/ppermute | solution.py:629
  102.4 27.5 %collective-permute-start.2 = (bf16[2,2,64,256]{3,2,1,0:T(8,128)(2,1)S(1)}, bf16[2,2,64,256]{3,2,1,0:T(8,128)(2,1)S(1)}, u32[]{:S(2)}, u32[]{:S(2)}) collective-permute-start(bf16[2,2,64,256]{3,2,1,0:T(8,128)(2,1)S(1)} %copy-done.11), channel_id=1, source_target_pairs={{0,2},{1,3},{2,0},{3,1},{4,6},{5,7},{6,4},{7,5},{8,10},{9,11},{10,... | collective-permute-start | bytes 393224 | tf_op jit(solution)/shard_map/cond/branch_0_fun/ppermute | solution.py:629
  130.0 0.7 copy-start.9
  136.8 14.1 %copy-start.10 = (bf16[2,2,64,256]{3,2,1,0:T(8,128)(2,1)S(1)}, bf16[2,2,64,256]{3,2,1,0:T(8,128)(2,1)}, u32[]{:S(2)}) copy-start(bf16[2,2,64,256]{3,2,1,0:T(8,128)(2,1)} %get-tuple-element.232) | copy-start | bytes 393220 | tf_op jit(solution)/shard_map/cond
  150.8 7.3 %collective-permute-start.6 = (bf16[2,2,64,2048]{3,2,1,0:T(8,128)(2,1)}, bf16[2,2,64,2048]{3,2,1,0:T(8,128)(2,1)}, u32[]{:S(2)}, u32[]{:S(2)}) collective-permute-start(bf16[2,2,64,2048]{3,2,1,0:T(8,128)(2,1)} %collective-permute-done.4.refs_0_), channel_id=1, source_target_pairs={{0,1},{1,0},{2,3},{3,2},{4,5},{5,4},{6,7},{7,6},{8,9},{9,8},{10,11... | collective-permute-start | bytes 3145736 | tf_op jit(solution)/shard_map/cond/branch_0_fun/ppermute | solution.py:629
  150.9 6.5 %collective-permute-start.5 = (bf16[2,2,64,256]{3,2,1,0:T(8,128)(2,1)S(1)}, bf16[2,2,64,256]{3,2,1,0:T(8,128)(2,1)S(1)}, u32[]{:S(2)}, u32[]{:S(2)}) collective-permute-start(bf16[2,2,64,256]{3,2,1,0:T(8,128)(2,1)S(1)} %copy-done.10), channel_id=1, source_target_pairs={{0,2},{1,3},{2,0},{3,1},{4,6},{5,7},{6,4},{7,5},{8,10},{9,11},{10,... | collective-permute-start | bytes 393224 | tf_op jit(solution)/shard_map/cond/branch_0_fun/ppermute | solution.py:629
  154.6 23.6 %collective-permute-start.7 = (bf16[2,64,2048]{2,1,0:T(8,128)(2,1)}, bf16[2,64,2048]{2,1,0:T(8,128)(2,1)}, u32[]{:S(2)}, u32[]{:S(2)}) collective-permute-start(bf16[2,64,2048]{2,1,0:T(8,128)(2,1)} %get-tuple-element.241), channel_id=1, source_target_pairs={{0,2},{1,3},{2,0},{3,1},{4,6},{5,7},{6,4},{7,5},{8,10},{9,11},{10,... | collective-permute-start | bytes 1572872 | tf_op jit(solution)/shard_map/cond/branch_0_fun/ppermute | solution.py:629
  155.9 23.9 %collective-permute-start.8 = (bf16[2,64,2048]{2,1,0:T(8,128)(2,1)}, bf16[2,64,2048]{2,1,0:T(8,128)(2,1)}, u32[]{:S(2)}, u32[]{:S(2)}) collective-permute-start(bf16[2,64,2048]{2,1,0:T(8,128)(2,1)} %get-tuple-element.242), channel_id=1, source_target_pairs={{0,3},{1,2},{2,1},{3,0},{4,7},{5,6},{6,5},{7,4},{8,11},{9,10},{10,... | collective-permute-start | bytes 1572872 | tf_op jit(solution)/shard_map/cond/branch_0_fun/ppermute | solution.py:629
  156.1 36.1 %collective-permute-start.9 = (bf16[2,64,2048]{2,1,0:T(8,128)(2,1)}, bf16[2,64,2048]{2,1,0:T(8,128)(2,1)}, u32[]{:S(2)}, u32[]{:S(2)}) collective-permute-start(bf16[2,64,2048]{2,1,0:T(8,128)(2,1)} %get-tuple-element.249), channel_id=1, source_target_pairs={{0,2},{1,3},{2,0},{3,1},{4,6},{5,7},{6,4},{7,5},{8,10},{9,11},{10,... | collective-permute-start | bytes 1572872 | tf_op jit(solution)/shard_map/cond/branch_0_fun/ppermute | solution.py:629
  157.4 0.7 copy-start.8
  157.4 44.3 %collective-permute-start.10 = (bf16[2,64,2048]{2,1,0:T(8,128)(2,1)}, bf16[2,64,2048]{2,1,0:T(8,128)(2,1)}, u32[]{:S(2)}, u32[]{:S(2)}) collective-permute-start(bf16[2,64,2048]{2,1,0:T(8,128)(2,1)} %get-tuple-element.250), channel_id=1, source_target_pairs={{0,3},{1,2},{2,1},{3,0},{4,7},{5,6},{6,5},{7,4},{8,11},{9,10},{10,... | collective-permute-start | bytes 1572872 | tf_op jit(solution)/shard_map/cond/branch_0_fun/ppermute | solution.py:629
  164.3 13.9 %copy-start = (bf16[3,2,64,4096]{3,2,1,0:T(8,128)(2,1)}, bf16[3,2,64,4096]{3,2,1,0:T(8,128)(2,1)S(1)}, u32[]{:S(2)}) copy-start(bf16[3,2,64,4096]{3,2,1,0:T(8,128)(2,1)S(1)} %get-tuple-element.502) | copy-start | bytes 9437188 | tf_op jit(solution)/shard_map/cond
